TPU v7x, 128 devices: a whole 4x4x4 slice. The times are simulated.
128 devices in a mesh: gx: 8 (over z, x_lo), gy: 16 (over y, x_hi, core).
Axes of the slice: x: 4 (x_hi: 2, x_lo: 2; x = x_hi * 2 + x_lo), y: 4, z: 4, core: 2. Of those that a mesh axis runs over, the one named last changes fastest.
Arguments:
- forcing: float32 [4, 2048, 4096], P(None, ('gx', 'gy')), may hold values from -6 to 6
- ice_state: float32 [2, 2048, 4096], P(None, ('gx', 'gy')), may hold values from 0.3 to 3, as said below
- velocity: float32 [2, 2048, 4096], P(None, ('gx', 'gy')), may hold values from -4 to 4
- stress: float32 [3, 2048, 4096], P(None, ('gx', 'gy')), may hold values from -4 to 4
- ice_mask: int32 [2048, 4096], P(('gx', 'gy')), may hold values from 0 to 2, as said below
Outputs:
- ice_velocity: float32 [2, 2048, 4096], P(None, ('gx', 'gy'))
- ice_stress: float32 [3, 2048, 4096], P(None, ('gx', 'gy'))
- ocean_stress: float32 [2, 2048, 4096], P(None, ('gx', 'gy'))
Inputs may be any that keep to these rules, and one draw needn't show every extreme that they name: `ice_state`: row 0 lies in 0.7 to 1, row 1 in 0.3 to 3. `ice_mask`: 0 marks land, 1 open water, 2 ice-covered cells.
All inputs are finite; a program needn't handle non-finite values.
Results may differ from a plain program's by a relative error of at most 0.00002.
Values sent between devices are 32-bit elements; how exact they have to be, the bound alone decides.
No kernel may reach another device: no remote copies, remote signals or barrier semaphores. Data moves between devices by JAX's collectives and lax.ppermute only.
A program may use at most 128 MiB of HBM per device.

v0:
```python
import math

import jax
import jax.numpy as jnp
import numpy as np
from jax import lax
from jax.experimental import pallas as pl
from jax.experimental.pallas import tpu as pltpu
from jax.sharding import PartitionSpec as P

F32 = jnp.float32
AXES = ("gx", "gy")
C = 16
R = 32
H = 3
NC = C + 2 * H
FIELDS = ("uo", "vo", "tx", "ty", "a", "h", "u", "v", "s1", "s2", "s12", "mask")
WHERE = {n: k for k, n in enumerate(FIELDS)}
STATE = ("u", "v", "s1", "s2", "s12")
FIRST = [(n, m) for m in range(2) for n in FIELDS] + [("u", 2), ("v", 2)]
SECOND = [(n, m) for m in range(2) for n in STATE] + [("u", 2), ("v", 2)]
U, V, S1, S2, S12 = range(5)
PR, MI, UO, CU, VO, CV, MK, OU, OV = range(9)
T, D2, W, DV2, E1, UP = range(6)
K29 = 29.0 / 30.0
STAGE = (2, 8 * 40, 128)
TOP = len(FIELDS)


def view(x):
    c = x.shape[0]
    return x.reshape(c, 2, 8, 8, 4, 128).transpose(0, 1, 3, 4, 2, 5).reshape(c, 2, 8, 32, 128)


def unview(y):
    c = y.shape[0]
    return y.reshape(c, 2, 8, 4, 8, 128).transpose(0, 1, 4, 2, 3, 5).reshape(c, C, 4096)


def iotas(shape):
    return lax.broadcasted_iota(jnp.int32, shape, 0), lax.broadcasted_iota(jnp.int32, shape, 1)


def root(x):
    return x * lax.rsqrt(jnp.maximum(x, 1e-30))


def below(x, masks):
    lane0, _, sub0, _ = masks
    r = pltpu.roll(x, 1, 1)
    q = jnp.where(sub0, 0.0, pltpu.roll(r[24:32], 1, 0))
    return jnp.where(lane0, jnp.concatenate([q, r[0:24]], 0), r)


def above(x, masks):
    _, lane127, _, _ = masks
    r = pltpu.roll(x, 127, 1)
    q = pltpu.roll(r[0:8], 7, 0)
    return jnp.where(lane127, jnp.concatenate([r[8:32], q], 0), r)


def make_masks():
    _, lane = iotas((R, 128))
    sub, _ = iotas((8, 128))
    return lane == 0, lane == 127, sub == 0, sub == 7


def rows(c):
    return pl.ds(pl.multiple_of((c + H) * R, R), R)


def each_column(lo, hi, chunk, body):
    def step(t, carry):
        for q in range(chunk):
            body(lo + t * chunk + q)
        return carry

    lax.fori_loop(0, (hi - lo) // chunk, step, 0)


def stress_terms(x1, e1, sc4, x, y, s, p):
    d = x1 + e1
    e = x1 - e1
    delta = root(d * d + 0.25 * (e * e) + (1.0 / 64.0) * (sc4 * sc4))
    r = p / (delta + 0.05)
    dk = x + y
    ek = x - y
    dk2 = root((1.0 / 16.0) * (dk * dk) + (1.0 / 64.0) * (ek * ek) + 0.25 * (s * s))
    rk = p / (dk2 + 0.05)
    return r * (d - delta), r * (0.25 * e), rk * (0.125 * s)


def momentum(w, o, c, mi, force, cor, ice, open_o):
    g = 0.5 * root((o - w) * (o - w) + 0.0025) * mi
    new = (30.0 * w + c + force * mi + g * o + cor) / (31.0 + g)
    return jnp.where(ice, new, open_o)


def subcycle(st, sc, tmp, f4, masks, vel, stress, mom):
    def shift(c):
        u, v = st[U, rows(c), :], st[V, rows(c), :]
        up, um = above(u, masks), below(u, masks)
        vp, vm = above(v, masks), below(v, masks)
        tmp[T, rows(c), :] = u + up
        tmp[D2, rows(c), :] = up - um
        tmp[UP, rows(c), :] = up - u
        tmp[W, rows(c), :] = v + vm
        tmp[E1, rows(c), :] = v - vm
        tmp[DV2, rows(c), :] = vp - vm

    each_column(*vel, shift)

    def strain(c):
        ld = lambda k, d=0: tmp[k, rows(c + d), :]
        us = lambda d: st[U, rows(c + d), :]
        vs = lambda d: st[V, rows(c + d), :]
        a1, a2, a12 = stress_terms(
            us(0) - us(-1),
            ld(E1),
            (ld(D2) + ld(D2, -1)) + (ld(W, 1) - ld(W, -1)),
            ld(T, 1) - ld(T, -1),
            ld(DV2) + ld(DV2, 1),
            ld(UP) + (vs(1) - vs(0)),
            sc[PR, rows(c), :],
        )
        st[S1, rows(c), :] = K29 * st[S1, rows(c), :] + a1
        st[S2, rows(c), :] = K29 * st[S2, rows(c), :] + a2
        st[S12, rows(c), :] = K29 * st[S12, rows(c), :] + a12

    each_column(*stress, strain)

    def move(c):
        ss = lambda k, d=0: st[k, rows(c + d), :]
        q1 = ss(S1) + ss(S2)
        q1n = ss(S1, 1) + ss(S2, 1)
        q2 = ss(S1) - ss(S2)
        s12 = ss(S12)
        fu = 0.5 * (q1n - q1) + (s12 - below(s12, masks))
        fv = 0.5 * (above(q2, masks) - q2) + (s12 - ss(S12, -1))
        cu = f4 * (tmp[W, rows(c), :] + tmp[W, rows(c + 1), :])
        cv = f4 * (tmp[T, rows(c), :] + tmp[T, rows(c - 1), :])
        k = lambda n: sc[n, rows(c), :]
        ice = k(MK) == 2.0
        mi = k(MI)
        st[U, rows(c), :] = momentum(ss(U), k(UO), k(CU), mi, fu, cu, ice, k(OU))
        st[V, rows(c), :] = momentum(ss(V), k(VO), k(CV), mi, fv, -cv, ice, k(OV))

    each_column(*mom, move)


def two_subcycles(st, sc, tmp, f4):
    masks = make_masks()
    subcycle(st, sc, tmp, f4, masks, (-3, 19, 11), (-2, 18, 5), (-2, 18, 5))
    subcycle(st, sc, tmp, f4, masks, (-2, 18, 5), (-1, 17, 6), (0, 16, 4))


def statics(raw):
    a, h, mask = raw["a"], raw["h"], raw["mask"]
    ice = mask == 2.0
    opened = mask == 1.0
    mi = 1.0 / (a * h)
    out = {
        PR: jnp.where(ice, h * jnp.exp(-20.0 * (1.0 - a)) * (1.0 / 30.0), 0.0),
        MI: mi,
        UO: raw["uo"],
        CU: raw["u"] + raw["tx"] * mi,
        VO: raw["vo"],
        CV: raw["v"] + raw["ty"] * mi,
        MK: mask,
        OU: jnp.where(opened, raw["uo"], 0.0),
        OV: jnp.where(opened, raw["vo"], 0.0),
    }
    return out, ice


def put_column(st, sc, at, raw):
    out, ice = statics(raw)
    for k, x in out.items():
        sc[k, at, :] = x
    st[U, at, :] = raw["u"]
    st[V, at, :] = raw["v"]
    st[S1, at, :] = jnp.where(ice, raw["s1"], 0.0)
    st[S2, at, :] = jnp.where(ice, raw["s2"], 0.0)
    st[S12, at, :] = jnp.where(ice, raw["s12"], 0.0)


def stage_in(srcs, stage, mstage, sems):
    copies = []
    at = 0
    for k, src in enumerate(srcs):
        n = src.shape[0]
        if k < 4:
            dst = stage.reshape(11, 2, 8, 40, 128).at[pl.ds(at, n), :, :, pl.ds(0, 32), :]
        else:
            dst = mstage.reshape(1, 2, 8, 40, 128).at[:, :, :, pl.ds(0, 32), :]
        copies.append(pltpu.make_async_copy(src, dst, sems.at[k]))
        at += n
    for c in copies:
        c.start()
    for c in copies:
        c.wait()


def staged_column(stage, mstage, name, c):
    ref, f = (mstage, 0) if name == "mask" else (stage, WHERE[name])
    parts = [ref[f, c // 8, pl.ds(8 * k + c % 8, 8, stride=40), :] for k in range(4)]
    return jnp.concatenate(parts, 0).astype(F32)


def parity():
    return lax.rem(lax.axis_index("gy"), 2)


def pack_kernel(f_ref, i_ref, v_ref, s_ref, m_ref, b_out, a_out, m_out, stage, mstage, sems):
    stage_in((f_ref, i_ref, v_ref, s_ref, m_ref), stage, mstage, sems)
    even = parity() == 0
    for n, (name, m) in enumerate(FIRST):
        left = staged_column(stage, mstage, name, m)
        right = staged_column(stage, mstage, name, C - 1 - m)
        b_out[pl.ds(n * R, R), :] = jnp.where(even, left, right)
        a_out[pl.ds(n * R, R), :] = jnp.where(even, right, left)
    for k in range(TOP):
        for ih in range(2):
            ref, f = (mstage, 0) if k == TOP - 1 else (stage, k)
            m_out[pl.ds(k * C + 8 * ih, 8), :] = ref[f, ih, pl.ds(7 * 40 + 24, 8), :].astype(F32)


def halo_rows(even, m):
    left, right = (H - 1 - m) * R, (H + C + m) * R
    via_b = pl.ds(pl.multiple_of(jnp.where(even, left, right), R), R)
    via_a = pl.ds(pl.multiple_of(jnp.where(even, right, left), R), R)
    return via_b, via_a


def first_kernel(
    f_ref, i_ref, v_ref, s_ref, m_ref, rb, ra, rm, cor, st, sc, strip, b_out, a_out,
    tmp, stage, mstage, sems,
):
    stage_in((f_ref, i_ref, v_ref, s_ref, m_ref), stage, mstage, sems)
    even = parity() == 0
    zero = jnp.zeros((R, 128), F32)
    for k in (S1, S2, S12):
        st[k, rows(-3), :] = zero
        st[k, rows(18), :] = zero
    for m in range(H):
        via = halo_rows(even, m)
        for at, src in zip(via, (rb, ra)):
            raw = {
                name: src[pl.ds(n * R, R), :] for n, (name, d) in enumerate(FIRST) if d == m
            }
            if m < 2:
                put_column(st, sc, at, raw)
            else:
                st[U, at, :] = raw["u"]
                st[V, at, :] = raw["v"]
    for c in range(C):
        put_column(
            st, sc, rows(c), {name: staged_column(stage, mstage, name, c) for name in FIELDS}
        )
    for k in range(TOP):
        for ih in range(2):
            ref, f = (mstage, 0) if k == TOP - 1 else (stage, k)
            strip[k, pl.ds(8 + 8 * ih, 8), :] = ref[f, ih, pl.ds(7 * 40 + 24, 8), :].astype(F32)
        for c in range(C):
            strip[TOP + k, pl.ds(8 + c, 1), :] = rm[pl.ds(k * C + (C - 1 - c), 1), :]
    two_subcycles(st, sc, tmp, 0.25 * cor[...])
    for n, (name, m) in enumerate(SECOND):
        left = st[STATE.index(name), rows(m), :]
        right = st[STATE.index(name), rows(C - 1 - m), :]
        b_out[pl.ds(n * R, R), :] = jnp.where(even, left, right)
        a_out[pl.ds(n * R, R), :] = jnp.where(even, right, left)
    base = len(SECOND) * R
    for k in range(2 * TOP):
        left = strip[k, pl.ds(8, 8), :]
        right = strip[k, pl.ds(16, 8), :]
        b_out[pl.ds(base + 8 * k, 8), :] = jnp.where(even, left, right)
        a_out[pl.ds(base + 8 * k, 8), :] = jnp.where(even, right, left)


def run_strips(strip, work, cor):
    _, lane = iotas((R, 128))
    last = lane == 127
    f4 = jnp.broadcast_to(0.25 * cor[pl.ds(31, 1), :], (R, 128))
    fixed = []
    for side in range(2):
        raw = {name: strip[side * TOP + k] for k, name in enumerate(FIELDS)}
        out, ice = statics(raw)
        fixed.append(out)
        work[5 * side + U] = raw["u"]
        work[5 * side + V] = raw["v"]
        for k, name in ((S1, "s1"), (S2, "s2"), (S12, "s12")):
            work[5 * side + k] = jnp.where(ice, raw[name], 0.0)
        for k in range(9):
            work[10 + 9 * side + k] = out[k]

    def step(t, carry):
        x = [[work[5 * side + k] for k in range(5)] for side in range(2)]
        east = [lambda y: pltpu.roll(y, R - 1, 0), lambda y: pltpu.roll(y, 1, 0)]
        west = [east[1], east[0]]
        down = lambda y: pltpu.roll(y, 1, 1)
        up = lambda y, other, sign: jnp.where(last, sign * other, pltpu.roll(y, 127, 1))
        terms = []
        for side in range(2):
            e, w = east[side], west[side]
            u, v = x[side][U], x[side][V]
            ou, ov = x[1 - side][U], x[1 - side][V]
            upu, um, vp, vm = up(u, ou, -1.0), down(u), up(v, ov, -1.0), down(v)
            tt, d2, ww, dv2 = u + upu, upu - um, v + vm, vp - vm
            terms.append((tt, ww))
            k = lambda n: work[10 + 9 * side + n]
            a1, a2, a12 = stress_terms(
                u - w(u),
                v - vm,
                (d2 + w(d2)) + (e(ww) - w(ww)),
                e(tt) - w(tt),
                dv2 + e(dv2),
                (upu - u) + (e(v) - v),
                k(PR),
            )
            x[side][S1] = K29 * x[side][S1] + a1
            x[side][S2] = K29 * x[side][S2] + a2
            x[side][S12] = K29 * x[side][S12] + a12
        new = []
        for side in range(2):
            e, w = east[side], west[side]
            u, v, s1, s2, s12 = x[side]
            q1, q2 = s1 + s2, s1 - s2
            other = x[1 - side][S1] - x[1 - side][S2]
            fu = 0.5 * (e(q1) - q1) + (s12 - down(s12))
            fv = 0.5 * (up(q2, other, 1.0) - q2) + (s12 - w(s12))
            tt, ww = terms[side]
            k = lambda n: work[10 + 9 * side + n]
            ice = k(MK) == 2.0
            nu = momentum(u, k(UO), k(CU), k(MI), fu, f4 * (ww + e(ww)), ice, k(OU))
            nv = momentum(v, k(VO), k(CV), k(MI), fv, -f4 * (tt + w(tt)), ice, k(OV))
            new.append((nu, nv, s1, s2, s12))
        for side in range(2):
            for k in range(5):
                work[5 * side + k] = new[side][k]
        return carry

    lax.fori_loop(0, 4, step, 0)


def second_kernel(
    st_in, sc, strip_in, rb, ra, cor, vel_o, str_o, oce_o, st, tmp, strip, work, stage, sems
):
    even = parity() == 0
    for k in range(5):
        st[k] = st_in[k]
    for m in range(H):
        via = halo_rows(even, m)
        for at, src in zip(via, (rb, ra)):
            for n, (name, d) in enumerate(SECOND):
                if d == m:
                    st[STATE.index(name), at, :] = src[pl.ds(n * R, R), :]
    base = len(SECOND) * R
    for k in range(2 * TOP):
        strip[k, pl.ds(8, 16), :] = strip_in[k, pl.ds(8, 16), :]
        xb = rb[pl.ds(base + 8 * k, 8), :]
        xa = ra[pl.ds(base + 8 * k, 8), :]
        strip[k, pl.ds(0, 8), :] = jnp.where(even, xb, xa)
        strip[k, pl.ds(24, 8), :] = jnp.where(even, xa, xb)
    run_strips(strip, work, cor)
    two_subcycles(st, sc, tmp, 0.25 * cor[...])
    row, lane = iotas((R, 128))
    top = (row == R - 1) & (lane >= 120)

    for c in range(C):
        x = [
            jnp.where(top, work[k, pl.ds(8 + c, 1), :], st[k, rows(c), :]) for k in range(5)
        ]
        for w, o in ((U, UO), (V, VO)):
            d = x[w] - sc[o, rows(c), :]
            x.append(0.5 * root(d * d + 0.0025) * d)
        for f, y in enumerate(x):
            for k in range(4):
                stage[f, c // 8, pl.ds(8 * k + c % 8, 8, stride=40), :] = y[8 * k : 8 * k + 8]
    whole = stage.reshape(7, 2, 8, 40, 128)
    copies = []
    for n, (dst, at) in enumerate(((vel_o, 0), (str_o, 2), (oce_o, 5))):
        src = whole.at[pl.ds(at, dst.shape[0]), :, :, pl.ds(0, 32), :]
        copies.append(pltpu.make_async_copy(src, dst, sems.at[n]))
    for c in copies:
        c.start()
    for c in copies:
        c.wait()


ANY = pl.BlockSpec(memory_space=pl.ANY)
VM = pl.BlockSpec(memory_space=pltpu.VMEM)


def shape(*dims):
    return jax.ShapeDtypeStruct(dims, F32)


def swap(b, a):
    n = 128
    cross = [(d, (d + 1) % n if d % 2 else (d - 1) % n) for d in range(n)]
    chip = [(d, d ^ 1) for d in range(n)]
    return lax.ppermute(b, AXES, cross), lax.ppermute(a, AXES, chip)


def coriolis():
    b = 4 * np.arange(8)[None, :] + np.arange(4)[:, None]
    j = b.reshape(32, 1) * 128 + np.arange(128)[None, :]
    return (0.5 * np.sin(math.pi * ((j + 0.5) / 4096 - 0.5))).astype(np.float32)


def staging():
    return [
        pltpu.VMEM((11, *STAGE), F32),
        pltpu.VMEM((1, *STAGE), jnp.int32),
        pltpu.SemaphoreType.DMA((5,)),
    ]


def on_device(forcing, ice_state, velocity, stress, ice_mask):
    raw = [view(x) for x in (forcing, ice_state, velocity, stress, ice_mask[None])]
    n1, n2 = len(FIRST) * R, len(SECOND) * R + 2 * TOP * 8
    b, a, m = pl.pallas_call(
        pack_kernel,
        out_shape=[shape(n1, 128), shape(n1, 128), shape(TOP * C, 128)],
        in_specs=[ANY] * 5,
        out_specs=[VM] * 3,
        scratch_shapes=staging(),
        compiler_params=pltpu.CompilerParams(vmem_limit_bytes=24 << 20),
        name="pack",
    )(*raw)
    rb, ra = swap(b, a)
    rm = lax.ppermute(m, AXES, [(d, 127 - d) for d in range(128)])
    cor = jnp.asarray(coriolis())
    st, sc, strip, b, a = pl.pallas_call(
        first_kernel,
        out_shape=[
            shape(5, NC * R, 128),
            shape(9, NC * R, 128),
            shape(2 * TOP, R, 128),
            shape(n2, 128),
            shape(n2, 128),
        ],
        in_specs=[ANY] * 5 + [VM] * 4,
        out_specs=[VM] * 5,
        scratch_shapes=[pltpu.VMEM((6, NC * R, 128), F32), *staging()],
        compiler_params=pltpu.CompilerParams(vmem_limit_bytes=32 << 20),
        name="first",
    )(*raw, rb, ra, rm, cor)
    rb, ra = swap(b, a)
    vel, strs, ocean = pl.pallas_call(
        second_kernel,
        out_shape=[shape(n, 2, 8, 32, 128) for n in (2, 3, 2)],
        in_specs=[VM] * 6,
        out_specs=[ANY] * 3,
        scratch_shapes=[
            pltpu.VMEM((5, NC * R, 128), F32),
            pltpu.VMEM((6, NC * R, 128), F32),
            pltpu.VMEM((2 * TOP, R, 128), F32),
            pltpu.VMEM((28, R, 128), F32),
            pltpu.VMEM((7, *STAGE), F32),
            pltpu.SemaphoreType.DMA((3,)),
        ],
        compiler_params=pltpu.CompilerParams(vmem_limit_bytes=32 << 20),
        name="second",
    )(st, sc, strip, rb, ra, cor)
    return unview(vel), unview(strs), unview(ocean)


def solution(mesh):
    slab = P(None, AXES, None)
    return jax.shard_map(
        on_device,
        mesh=mesh,
        in_specs=(slab, slab, slab, slab, P(AXES, None)),
        out_specs=(slab, slab, slab),
        check_vma=False,
    )
```

profile of v0, /device:TPU:0, one launch (start us, length us, event | category | flops | bytes accessed | tf_op | source)
XLA Modules:
  0.0 51.2 jit_solution(951488211161470342)
XLA Ops:
  0.6 0.0 copy-start
  0.6 1.2 %copy-done = f32[4,16,4096]{2,1,0:T(8,128)S(1)} copy-done((f32[4,16,4096]{2,1,0:T(8,128)S(1)}, f32[4,16,4096]{2,1,0:T(8,128)}, u32[]{:S(2)}) %copy-start) | copy-done | bytes 1048600
  1.9 1.1 %copy-done.2 = f32[3,16,4096]{2,1,0:T(8,128)S(1)} copy-done((f32[3,16,4096]{2,1,0:T(8,128)S(1)}, f32[3,16,4096]{2,1,0:T(8,128)}, u32[]{:S(2)}) %copy-start.2) | copy-done | bytes 786456
  3.0 1.0 %copy-done.4 = f32[2,16,4096]{2,1,0:T(8,128)S(1)} copy-done((f32[2,16,4096]{2,1,0:T(8,128)S(1)}, f32[2,16,4096]{2,1,0:T(8,128)}, u32[]{:S(2)}) %copy-start.4) | copy-done | bytes 524312
  4.0 1.0 %copy-done.6 = f32[2,16,4096]{2,1,0:T(8,128)S(1)} copy-done((f32[2,16,4096]{2,1,0:T(8,128)S(1)}, f32[2,16,4096]{2,1,0:T(8,128)}, u32[]{:S(2)}) %copy-start.6) | copy-done | bytes 524312
  5.1 0.9 %copy-done.8 = s32[16,4096]{1,0:T(8,128)S(1)} copy-done((s32[16,4096]{1,0:T(8,128)S(1)}, s32[16,4096]{1,0:T(8,128)}, u32[]{:S(2)}) %copy-start.8) | copy-done | bytes 262168
  6.0 0.0 copy-start.9
  6.0 0.5 pack.1
  6.5 8.3 %collective-permute-start = (f32[832,128]{1,0:T(8,128)S(1)}, f32[832,128]{1,0:T(8,128)S(1)}, u32[]{:S(2)}, u32[]{:S(2)}) collective-permute-start(f32[832,128]{1,0:T(8,128)S(1)} %get-tuple-element.14), channel_id=1, source_target_pairs={{0,127},{1,2},{2,1},{3,4},{4,3},{5,6},{6,5},{7,8},{8,7},{9,10},{10... | collective-permute-start | bytes 1277960 | tf_op jit(solution)/shard_map/ppermute | solution.py:402
  14.9 0.0 collective-permute-start.1
  14.9 1.5 %collective-permute-start.2 = (f32[192,128]{1,0:T(8,128)S(1)}, f32[192,128]{1,0:T(8,128)S(1)}, u32[]{:S(2)}, u32[]{:S(2)}) collective-permute-start(f32[192,128]{1,0:T(8,128)S(1)} %get-tuple-element.16), channel_id=1, source_target_pairs={{0,127},{1,126},{2,125},{3,124},{4,123},{5,122},{6,121},{7,120},{8... | collective-permute-start | bytes 294920 | tf_op jit(solution)/shard_map/ppermute | solution.py:432
  16.4 11.0 %collective-permute-done.2.rm = f32[192,128]{1,0:T(8,128)S(1)} collective-permute-done((f32[192,128]{1,0:T(8,128)S(1)}, f32[192,128]{1,0:T(8,128)S(1)}, u32[]{:S(2)}, u32[]{:S(2)}) %collective-permute-start.2) | collective-permute-done | bytes 98336 | tf_op jit(solution)/shard_map/ppermute | solution.py:432
  27.3 0.0 collective-permute-done.rb
  27.3 0.0 collective-permute-done.1.ra
  27.3 0.0 copy-done.1
  27.4 0.0 copy-done.3
  27.4 0.0 copy-start.10
  27.4 0.7 %copy-done.10 = f32[32,128]{1,0:T(8,128)S(1)} copy-done((f32[32,128]{1,0:T(8,128)S(1)}, f32[32,128]{1,0:T(8,128)}, u32[]{:S(2)}) %copy-start.10) | copy-done | bytes 16408
  28.1 4.9 %first.1 = (f32[5,704,128]{2,1,0:T(8,128)S(1)}, f32[9,704,128]{2,1,0:T(8,128)S(1)}, f32[24,32,128]{2,1,0:T(8,128)S(1)}, f32[576,128]{1,0:T(8,128)S(1)}, f32[576,128]{1,0:T(8,128)S(1)}) custom-call(f32[4,2,8,32,128]{4,3,2,1,0:T(8,128)S(1)} %bitcast.41, f32[2,2,8,32,128]{4,3,2,1,0:T(8,128)S(1)} %bitcast.45, f32[2,2,8,32,128]{4,3,2,1,0:T(8,128)S(1)} %bitcast.47, ...), custom_call_target="tpu_custom_call" | custom-call | tf_op jit(solution)/shard_map/first/pallas_call | solution.py:434
  33.1 2.7 %collective-permute-start.3 = (f32[576,128]{1,0:T(8,128)S(1)}, f32[576,128]{1,0:T(8,128)S(1)}, u32[]{:S(2)}, u32[]{:S(2)}) collective-permute-start(f32[576,128]{1,0:T(8,128)S(1)} %get-tuple-element.20), channel_id=1, source_target_pairs={{0,127},{1,2},{2,1},{3,4},{4,3},{5,6},{6,5},{7,8},{8,7},{9,10},{10... | collective-permute-start | bytes 884744 | tf_op jit(solution)/shard_map/ppermute | solution.py:402
  35.7 0.0 collective-permute-start.4
  35.8 8.9 %collective-permute-done.3.rb = f32[576,128]{1,0:T(8,128)S(1)} collective-permute-done((f32[576,128]{1,0:T(8,128)S(1)}, f32[576,128]{1,0:T(8,128)S(1)}, u32[]{:S(2)}, u32[]{:S(2)}) %collective-permute-start.3) | collective-permute-done | bytes 294944 | tf_op jit(solution)/shard_map/ppermute | solution.py:402
  44.7 0.0 collective-permute-done.4.ra
  44.7 6.5 %second.1 = (f32[2,2,8,32,128]{4,3,2,1,0:T(8,128)}, f32[3,2,8,32,128]{4,3,2,1,0:T(8,128)}, f32[2,2,8,32,128]{4,3,2,1,0:T(8,128)}) custom-call(f32[5,704,128]{2,1,0:T(8,128)S(1)} %get-tuple-element.17.st_in, f32[9,704,128]{2,1,0:T(8,128)S(1)} %get-tuple-element.18.sc, f32[24,32,128]{2,1,0:T(8,128)S(1)} %get-tuple-element.19.strip_in, ...), custom_call_target="tpu_custom_call" | custom-call | tf_op jit(solution)/shard_map/second/pallas_call | solution.py:450
  (11 shorter events, 0.0 us)
Async XLA Ops:
  0.6 1.2 %copy-start = (f32[4,16,4096]{2,1,0:T(8,128)S(1)}, f32[4,16,4096]{2,1,0:T(8,128)}, u32[]{:S(2)}) copy-start(f32[4,16,4096]{2,1,0:T(8,128)} %param.6) | copy-start | bytes 3145732
  1.9 1.1 %copy-start.2 = (f32[3,16,4096]{2,1,0:T(8,128)S(1)}, f32[3,16,4096]{2,1,0:T(8,128)}, u32[]{:S(2)}) copy-start(f32[3,16,4096]{2,1,0:T(8,128)} %param.9) | copy-start | bytes 2359300
  3.0 1.0 %copy-start.4 = (f32[2,16,4096]{2,1,0:T(8,128)S(1)}, f32[2,16,4096]{2,1,0:T(8,128)}, u32[]{:S(2)}) copy-start(f32[2,16,4096]{2,1,0:T(8,128)} %param.7) | copy-start | bytes 1572868
  4.0 1.0 %copy-start.6 = (f32[2,16,4096]{2,1,0:T(8,128)S(1)}, f32[2,16,4096]{2,1,0:T(8,128)}, u32[]{:S(2)}) copy-start(f32[2,16,4096]{2,1,0:T(8,128)} %param.8) | copy-start | bytes 1572868
  5.1 0.9 %copy-start.8 = (s32[16,4096]{1,0:T(8,128)S(1)}, s32[16,4096]{1,0:T(8,128)}, u32[]{:S(2)}) copy-start(s32[16,4096]{1,0:T(8,128)} %param.10) | copy-start | bytes 786436
  6.0 21.3 %copy-start.1 = (f32[4,16,4096]{2,1,0:T(8,128)S(1)}, f32[4,16,4096]{2,1,0:T(8,128)}, u32[]{:S(2)}) copy-start(f32[4,16,4096]{2,1,0:T(8,128)} %param.6) | copy-start | bytes 3145732
  6.0 21.3 %copy-start.3 = (f32[3,16,4096]{2,1,0:T(8,128)S(1)}, f32[3,16,4096]{2,1,0:T(8,128)}, u32[]{:S(2)}) copy-start(f32[3,16,4096]{2,1,0:T(8,128)} %param.9) | copy-start | bytes 2359300
  6.0 21.3 %copy-start.5 = (f32[2,16,4096]{2,1,0:T(8,128)S(1)}, f32[2,16,4096]{2,1,0:T(8,128)}, u32[]{:S(2)}) copy-start(f32[2,16,4096]{2,1,0:T(8,128)} %param.7) | copy-start | bytes 1572868
  6.0 21.3 %copy-start.7 = (f32[2,16,4096]{2,1,0:T(8,128)S(1)}, f32[2,16,4096]{2,1,0:T(8,128)}, u32[]{:S(2)}) copy-start(f32[2,16,4096]{2,1,0:T(8,128)} %param.8) | copy-start | bytes 1572868
  6.0 21.4 %copy-start.9 = (s32[16,4096]{1,0:T(8,128)S(1)}, s32[16,4096]{1,0:T(8,128)}, u32[]{:S(2)}) copy-start(s32[16,4096]{1,0:T(8,128)} %param.10) | copy-start | bytes 786436
  6.5 20.8 %collective-permute-start = (f32[832,128]{1,0:T(8,128)S(1)}, f32[832,128]{1,0:T(8,128)S(1)}, u32[]{:S(2)}, u32[]{:S(2)}) collective-permute-start(f32[832,128]{1,0:T(8,128)S(1)} %get-tuple-element.14), channel_id=1, source_target_pairs={{0,127},{1,2},{2,1},{3,4},{4,3},{5,6},{6,5},{7,8},{8,7},{9,10},{10... | collective-permute-start | bytes 1277960 | tf_op jit(solution)/shard_map/ppermute | solution.py:402
  14.9 12.5 %collective-permute-start.1 = (f32[832,128]{1,0:T(8,128)S(1)}, f32[832,128]{1,0:T(8,128)S(1)}, u32[]{:S(2)}, u32[]{:S(2)}) collective-permute-start(f32[832,128]{1,0:T(8,128)S(1)} %get-tuple-element.15), channel_id=1, source_target_pairs={{0,1},{1,0},{2,3},{3,2},{4,5},{5,4},{6,7},{7,6},{8,9},{9,8},{10,11... | collective-permute-start | bytes 1277960 | tf_op jit(solution)/shard_map/ppermute | solution.py:402
  14.9 12.5 %collective-permute-start.2 = (f32[192,128]{1,0:T(8,128)S(1)}, f32[192,128]{1,0:T(8,128)S(1)}, u32[]{:S(2)}, u32[]{:S(2)}) collective-permute-start(f32[192,128]{1,0:T(8,128)S(1)} %get-tuple-element.16), channel_id=1, source_target_pairs={{0,127},{1,126},{2,125},{3,124},{4,123},{5,122},{6,121},{7,120},{8... | collective-permute-start | bytes 294920 | tf_op jit(solution)/shard_map/ppermute | solution.py:432
  27.4 0.7 %copy-start.10 = (f32[32,128]{1,0:T(8,128)S(1)}, f32[32,128]{1,0:T(8,128)}, u32[]{:S(2)}) copy-start(f32[32,128]{1,0:T(8,128)} %constant.2.clone.cor) | copy-start | bytes 49156
  33.1 11.7 %collective-permute-start.3 = (f32[576,128]{1,0:T(8,128)S(1)}, f32[576,128]{1,0:T(8,128)S(1)}, u32[]{:S(2)}, u32[]{:S(2)}) collective-permute-start(f32[576,128]{1,0:T(8,128)S(1)} %get-tuple-element.20), channel_id=1, source_target_pairs={{0,127},{1,2},{2,1},{3,4},{4,3},{5,6},{6,5},{7,8},{8,7},{9,10},{10... | collective-permute-start | bytes 884744 | tf_op jit(solution)/shard_map/ppermute | solution.py:402
  35.7 9.0 %collective-permute-start.4 = (f32[576,128]{1,0:T(8,128)S(1)}, f32[576,128]{1,0:T(8,128)S(1)}, u32[]{:S(2)}, u32[]{:S(2)}) collective-permute-start(f32[576,128]{1,0:T(8,128)S(1)} %get-tuple-element.21), channel_id=1, source_target_pairs={{0,1},{1,0},{2,3},{3,2},{4,5},{5,4},{6,7},{7,6},{8,9},{9,8},{10,11... | collective-permute-start | bytes 884744 | tf_op jit(solution)/shard_map/ppermute | solution.py:402
where the time goes:
time: 51.6 us; the launch traced here: 51.2 us
  waiting for transfers between devices  19.9 us (39%)
  starting transfers between devices  12.6 us (24%)
  Pallas kernels  11.9 us (23%)
  local copies, waits for them, and re-layouts  6.11 us (12%)
  between operations  0.72 us (1%)
    ppermute x4, starting transfers between devices, swap(): return (lax.ppermute(b, AXES, cross), lax.ppermute(a, AXES, chip))  11 us
    ppermute x1, waiting for transfers between devices, on_device(): rm = lax.ppermute(m, AXES, [(d, 127 - d) for d in range(128)])  11 us
    ppermute x4, waiting for transfers between devices, swap(): return (lax.ppermute(b, AXES, cross), lax.ppermute(a, AXES, chip))  8.93 us
    pallas_call x1, Pallas kernels, on_device(): pl.pallas_call(second_kernel, out_shape=[shape(n, 2, 8, 32, 128) for n in...  6.47 us
    unnamed x22, local copies, waits for them, and re-layouts  6.11 us
    pallas_call x1, Pallas kernels, on_device(): pl.pallas_call(first_kernel, out_shape=[shape(5, NC * R, 128), shape(9, N...  4.94 us
    ppermute x1, starting transfers between devices, on_device(): rm = lax.ppermute(m, AXES, [(d, 127 - d) for d in range(128)])  1.52 us
  transfers between devices with their start and end apart: 5, of which 2 were waited for; matrix products, arithmetic and copies ran while one was open for 0% of the time, Pallas kernels for 0%

commit v1 on v0

--- a/solution.py
+++ b/solution.py
@@ -17,7 +17,8 @@
 FIELDS = ("uo", "vo", "tx", "ty", "a", "h", "u", "v", "s1", "s2", "s12", "mask")
 WHERE = {n: k for k, n in enumerate(FIELDS)}
 STATE = ("u", "v", "s1", "s2", "s12")
-FIRST = [(n, m) for m in range(2) for n in FIELDS] + [("u", 2), ("v", 2)]
+NEAR = [(n, 1) for n in ("a", "h", "u", "v", "s1", "s2", "s12", "mask", "o", "t")]
+FIRST = [(n, 0) for n in FIELDS] + NEAR + [("u", 2), ("v", 2)]
 SECOND = [(n, m) for m in range(2) for n in STATE] + [("u", 2), ("v", 2)]
 U, V, S1, S2, S12 = range(5)
 PR, MI, UO, CU, VO, CV, MK, OU, OV = range(9)
@@ -69,13 +70,19 @@
     return pl.ds(pl.multiple_of((c + H) * R, R), R)
 
 
-def each_column(lo, hi, chunk, body):
-    def step(t, carry):
-        for q in range(chunk):
-            body(lo + t * chunk + q)
-        return carry
-
-    lax.fori_loop(0, (hi - lo) // chunk, step, 0)
+def each_column(span, body):
+    if isinstance(span, tuple):
+        lo, hi, chunk = span
+
+        def step(t, carry):
+            for q in range(chunk):
+                body(lo + t * chunk + q)
+            return carry
+
+        lax.fori_loop(0, (hi - lo) // chunk, step, 0)
+    else:
+        for c in span:
+            body(c)
 
 
 def stress_terms(x1, e1, sc4, x, y, s, p):
@@ -108,7 +115,7 @@
         tmp[E1, rows(c), :] = v - vm
         tmp[DV2, rows(c), :] = vp - vm
 
-    each_column(*vel, shift)
+    each_column(vel, shift)
 
     def strain(c):
         ld = lambda k, d=0: tmp[k, rows(c + d), :]
@@ -127,7 +134,7 @@
         st[S2, rows(c), :] = K29 * st[S2, rows(c), :] + a2
         st[S12, rows(c), :] = K29 * st[S12, rows(c), :] + a12
 
-    each_column(*stress, strain)
+    each_column(stress, strain)
 
     def move(c):
         ss = lambda k, d=0: st[k, rows(c + d), :]
@@ -145,13 +152,27 @@
         st[U, rows(c), :] = momentum(ss(U), k(UO), k(CU), mi, fu, cu, ice, k(OU))
         st[V, rows(c), :] = momentum(ss(V), k(VO), k(CV), mi, fv, -cv, ice, k(OV))
 
-    each_column(*mom, move)
-
-
-def two_subcycles(st, sc, tmp, f4):
+    each_column(mom, move)
+
+
+def both(a, b, c, d):
+    return [*range(a, b), *range(c, d)]
+
+
+def interior(st, sc, tmp1, tmp2, f4):
     masks = make_masks()
-    subcycle(st, sc, tmp, f4, masks, (-3, 19, 11), (-2, 18, 5), (-2, 18, 5))
-    subcycle(st, sc, tmp, f4, masks, (-2, 18, 5), (-1, 17, 6), (0, 16, 4))
+    subcycle(st, sc, tmp1, f4, masks, (0, 16, 8), (1, 15, 7), (2, 14, 6))
+    subcycle(st, sc, tmp2, f4, masks, (2, 14, 6), (3, 13, 5), (4, 12, 4))
+
+
+def edges(st, sc, tmp1, tmp2, f4):
+    masks = make_masks()
+    subcycle(
+        st, sc, tmp1, f4, masks, both(-3, 0, 16, 19), both(-2, 1, 15, 18), both(-2, 2, 14, 18)
+    )
+    subcycle(
+        st, sc, tmp2, f4, masks, both(-2, 2, 14, 18), both(-1, 3, 13, 17), both(0, 4, 12, 16)
+    )
 
 
 def statics(raw):
@@ -211,18 +232,40 @@
     return lax.rem(lax.axis_index("gy"), 2)
 
 
+def squeeze(tiles):
+    _, lane = iotas((8, 128))
+    out = []
+    for t in range(0, len(tiles), 8):
+        x = tiles[t + 7]
+        for g in range(7):
+            x = jnp.where(lane // 16 == g, pltpu.roll(tiles[t + g], 16 * (g + 1), 1), x)
+        out.append(x)
+    return out
+
+
+def spread(packed, n):
+    x = packed[n // 8]
+    g = n % 8
+    return x if g == 7 else pltpu.roll(x, 128 - 16 * (g + 1), 1)
+
+
+def top_tile(stage, mstage, k, ih):
+    ref, f = (mstage, 0) if k == TOP - 1 else (stage, k)
+    return ref[f, ih, pl.ds(7 * 40 + 24, 8), :].astype(F32)
+
+
 def pack_kernel(f_ref, i_ref, v_ref, s_ref, m_ref, b_out, a_out, m_out, stage, mstage, sems):
     stage_in((f_ref, i_ref, v_ref, s_ref, m_ref), stage, mstage, sems)
     even = parity() == 0
     for n, (name, m) in enumerate(FIRST):
-        left = staged_column(stage, mstage, name, m)
-        right = staged_column(stage, mstage, name, C - 1 - m)
+        far = {"o": ("vo", "uo"), "t": ("ty", "tx")}.get(name, (name, name))
+        left = staged_column(stage, mstage, far[0], m)
+        right = staged_column(stage, mstage, far[1], C - 1 - m)
         b_out[pl.ds(n * R, R), :] = jnp.where(even, left, right)
         a_out[pl.ds(n * R, R), :] = jnp.where(even, right, left)
-    for k in range(TOP):
-        for ih in range(2):
-            ref, f = (mstage, 0) if k == TOP - 1 else (stage, k)
-            m_out[pl.ds(k * C + 8 * ih, 8), :] = ref[f, ih, pl.ds(7 * 40 + 24, 8), :].astype(F32)
+    tops = squeeze([top_tile(stage, mstage, k, ih) for k in range(TOP) for ih in range(2)])
+    for n, x in enumerate(tops):
+        m_out[pl.ds(8 * n, 8), :] = x
 
 
 def halo_rows(even, m):
@@ -232,60 +275,75 @@
     return via_b, via_a
 
 
-def first_kernel(
-    f_ref, i_ref, v_ref, s_ref, m_ref, rb, ra, rm, cor, st, sc, strip, b_out, a_out,
-    tmp, stage, mstage, sems,
+def first_interior(
+    f_ref, i_ref, v_ref, s_ref, m_ref, cor, st, sc, tmp1, tmp2, strip, f4, stage, mstage, sems
 ):
     stage_in((f_ref, i_ref, v_ref, s_ref, m_ref), stage, mstage, sems)
-    even = parity() == 0
     zero = jnp.zeros((R, 128), F32)
     for k in (S1, S2, S12):
         st[k, rows(-3), :] = zero
         st[k, rows(18), :] = zero
+    f4[...] = 0.25 * cor[...]
+    for c in range(C):
+        put_column(
+            st, sc, rows(c), {name: staged_column(stage, mstage, name, c) for name in FIELDS}
+        )
+    for k in range(TOP):
+        for ih in range(2):
+            strip[k, pl.ds(8 + 8 * ih, 8), :] = top_tile(stage, mstage, k, ih)
+    interior(st, sc, tmp1, tmp2, f4[...])
+
+
+def first_edges(*refs):
+    rb, ra, rm, f4 = refs[:4]
+    st, sc, tmp1, tmp2, strip, b_out, a_out = refs[9:]
+    even = parity() == 0
     for m in range(H):
         via = halo_rows(even, m)
         for at, src in zip(via, (rb, ra)):
             raw = {
                 name: src[pl.ds(n * R, R), :] for n, (name, d) in enumerate(FIRST) if d == m
             }
+            if m == 1:
+                raw["uo"] = raw["vo"] = raw["o"]
+                raw["tx"] = raw["ty"] = raw["t"]
             if m < 2:
                 put_column(st, sc, at, raw)
             else:
                 st[U, at, :] = raw["u"]
                 st[V, at, :] = raw["v"]
-    for c in range(C):
-        put_column(
-            st, sc, rows(c), {name: staged_column(stage, mstage, name, c) for name in FIELDS}
-        )
+    flip = 7 - iotas((8, 128))[0]
+    packed = [rm[pl.ds(8 * n, 8), :] for n in range(3)]
     for k in range(TOP):
         for ih in range(2):
-            ref, f = (mstage, 0) if k == TOP - 1 else (stage, k)
-            strip[k, pl.ds(8 + 8 * ih, 8), :] = ref[f, ih, pl.ds(7 * 40 + 24, 8), :].astype(F32)
-        for c in range(C):
-            strip[TOP + k, pl.ds(8 + c, 1), :] = rm[pl.ds(k * C + (C - 1 - c), 1), :]
-    two_subcycles(st, sc, tmp, 0.25 * cor[...])
+            x = spread(packed, 2 * k + ih)
+            strip[TOP + k, pl.ds(16 - 8 * ih, 8), :] = jnp.take_along_axis(x, flip, axis=0)
+    edges(st, sc, tmp1, tmp2, f4[...])
     for n, (name, m) in enumerate(SECOND):
         left = st[STATE.index(name), rows(m), :]
         right = st[STATE.index(name), rows(C - 1 - m), :]
         b_out[pl.ds(n * R, R), :] = jnp.where(even, left, right)
         a_out[pl.ds(n * R, R), :] = jnp.where(even, right, left)
     base = len(SECOND) * R
-    for k in range(2 * TOP):
-        left = strip[k, pl.ds(8, 8), :]
-        right = strip[k, pl.ds(16, 8), :]
-        b_out[pl.ds(base + 8 * k, 8), :] = jnp.where(even, left, right)
-        a_out[pl.ds(base + 8 * k, 8), :] = jnp.where(even, right, left)
-
-
-def run_strips(strip, work, cor):
+    left = squeeze([strip[k, pl.ds(8, 8), :] for k in range(2 * TOP)])
+    right = squeeze([strip[k, pl.ds(16, 8), :] for k in range(2 * TOP)])
+    for n in range(3):
+        b_out[pl.ds(base + 8 * n, 8), :] = jnp.where(even, left[n], right[n])
+        a_out[pl.ds(base + 8 * n, 8), :] = jnp.where(even, right[n], left[n])
+
+
+def second_interior(*refs):
+    f4, (st, sc, tmp1, tmp2) = refs[0], refs[5:]
+    interior(st, sc, tmp1, tmp2, f4[...])
+
+
+def run_strips(strip, work, cor4):
     _, lane = iotas((R, 128))
     last = lane == 127
-    f4 = jnp.broadcast_to(0.25 * cor[pl.ds(31, 1), :], (R, 128))
-    fixed = []
+    f4 = jnp.broadcast_to(cor4[pl.ds(31, 1), :], (R, 128))
     for side in range(2):
         raw = {name: strip[side * TOP + k] for k, name in enumerate(FIELDS)}
         out, ice = statics(raw)
-        fixed.append(out)
         work[5 * side + U] = raw["u"]
         work[5 * side + V] = raw["v"]
         for k, name in ((S1, "s1"), (S2, "s2"), (S12, "s12")):
@@ -293,7 +351,7 @@
         for k in range(9):
             work[10 + 9 * side + k] = out[k]
 
-    def step(t, carry):
+    def step():
         x = [[work[5 * side + k] for k in range(5)] for side in range(2)]
         east = [lambda y: pltpu.roll(y, R - 1, 0), lambda y: pltpu.roll(y, 1, 0)]
         west = [east[1], east[0]]
@@ -337,17 +395,14 @@
         for side in range(2):
             for k in range(5):
                 work[5 * side + k] = new[side][k]
-        return carry
-
-    lax.fori_loop(0, 4, step, 0)
-
-
-def second_kernel(
-    st_in, sc, strip_in, rb, ra, cor, vel_o, str_o, oce_o, st, tmp, strip, work, stage, sems
-):
+
+    return step
+
+
+def second_edges(*refs):
+    rb, ra, f4 = refs[:3]
+    vel_o, str_o, oce_o, st, sc, tmp1, tmp2, strip, work, stage, sems = refs[8:]
     even = parity() == 0
-    for k in range(5):
-        st[k] = st_in[k]
     for m in range(H):
         via = halo_rows(even, m)
         for at, src in zip(via, (rb, ra)):
@@ -355,14 +410,17 @@
                 if d == m:
                     st[STATE.index(name), at, :] = src[pl.ds(n * R, R), :]
     base = len(SECOND) * R
+    pb = [rb[pl.ds(base + 8 * n, 8), :] for n in range(3)]
+    pa = [ra[pl.ds(base + 8 * n, 8), :] for n in range(3)]
+    low = [jnp.where(even, b, a) for b, a in zip(pb, pa)]
+    high = [jnp.where(even, a, b) for b, a in zip(pb, pa)]
     for k in range(2 * TOP):
-        strip[k, pl.ds(8, 16), :] = strip_in[k, pl.ds(8, 16), :]
-        xb = rb[pl.ds(base + 8 * k, 8), :]
-        xa = ra[pl.ds(base + 8 * k, 8), :]
-        strip[k, pl.ds(0, 8), :] = jnp.where(even, xb, xa)
-        strip[k, pl.ds(24, 8), :] = jnp.where(even, xa, xb)
-    run_strips(strip, work, cor)
-    two_subcycles(st, sc, tmp, 0.25 * cor[...])
+        strip[k, pl.ds(0, 8), :] = spread(low, k)
+        strip[k, pl.ds(24, 8), :] = spread(high, k)
+    step = run_strips(strip, work, f4)
+    for _ in range(4):
+        step()
+    edges(st, sc, tmp1, tmp2, f4[...])
     row, lane = iotas((R, 128))
     top = (row == R - 1) & (lane >= 120)
 
@@ -387,7 +445,7 @@
         c.wait()
 
 
-ANY = pl.BlockSpec(memory_space=pl.ANY)
+HBM = pl.BlockSpec(memory_space=pltpu.HBM)
 VM = pl.BlockSpec(memory_space=pltpu.VMEM)
 
 
@@ -416,53 +474,83 @@
     ]
 
 
+def call(kernel, name, out, ins, specs, scratch, alias=None, outs=None, cost=None):
+    return pl.pallas_call(
+        kernel,
+        out_shape=out,
+        in_specs=specs,
+        out_specs=outs or [VM] * len(out),
+        scratch_shapes=scratch,
+        input_output_aliases=alias or {},
+        compiler_params=pltpu.CompilerParams(vmem_limit_bytes=20 << 20),
+        cost_estimate=cost,
+        name=name,
+    )(*ins)
+
+
 def on_device(forcing, ice_state, velocity, stress, ice_mask):
-    raw = [view(x) for x in (forcing, ice_state, velocity, stress, ice_mask[None])]
-    n1, n2 = len(FIRST) * R, len(SECOND) * R + 2 * TOP * 8
-    b, a, m = pl.pallas_call(
+    raw = [
+        pltpu.with_memory_space_constraint(view(x), pltpu.HBM)
+        for x in (forcing, ice_state, velocity, stress, ice_mask[None])
+    ]
+    n1, n2 = len(FIRST) * R, len(SECOND) * R + 24
+    b, a, m = call(
         pack_kernel,
-        out_shape=[shape(n1, 128), shape(n1, 128), shape(TOP * C, 128)],
-        in_specs=[ANY] * 5,
-        out_specs=[VM] * 3,
-        scratch_shapes=staging(),
-        compiler_params=pltpu.CompilerParams(vmem_limit_bytes=24 << 20),
-        name="pack",
-    )(*raw)
+        "pack",
+        [shape(n1, 128), shape(n1, 128), shape(24, 128)],
+        raw,
+        [HBM] * 5,
+        staging(),
+    )
     rb, ra = swap(b, a)
     rm = lax.ppermute(m, AXES, [(d, 127 - d) for d in range(128)])
     cor = jnp.asarray(coriolis())
-    st, sc, strip, b, a = pl.pallas_call(
-        first_kernel,
-        out_shape=[
-            shape(5, NC * R, 128),
-            shape(9, NC * R, 128),
-            shape(2 * TOP, R, 128),
-            shape(n2, 128),
-            shape(n2, 128),
-        ],
-        in_specs=[ANY] * 5 + [VM] * 4,
-        out_specs=[VM] * 5,
-        scratch_shapes=[pltpu.VMEM((6, NC * R, 128), F32), *staging()],
-        compiler_params=pltpu.CompilerParams(vmem_limit_bytes=32 << 20),
-        name="first",
-    )(*raw, rb, ra, rm, cor)
+    cost = pl.CostEstimate(flops=20_000_000, bytes_accessed=4_000_000, transcendentals=500_000)
+    main = [shape(5, NC * R, 128), shape(9, NC * R, 128), *[shape(6, NC * R, 128)] * 2]
+    strips = shape(2 * TOP, R, 128)
+    *state, strip, f4 = call(
+        first_interior,
+        "interior1",
+        [*main, strips, shape(R, 128)],
+        [*raw, cor],
+        [HBM] * 5 + [VM],
+        staging(),
+        cost=cost,
+    )
+    *state, strip, b, a = call(
+        first_edges,
+        "edges1",
+        [*main, strips, shape(n2, 128), shape(n2, 128)],
+        [rb, ra, rm, f4, *state, strip],
+        [VM] * 9,
+        [],
+        alias={4 + k: k for k in range(5)},
+    )
     rb, ra = swap(b, a)
-    vel, strs, ocean = pl.pallas_call(
-        second_kernel,
-        out_shape=[shape(n, 2, 8, 32, 128) for n in (2, 3, 2)],
-        in_specs=[VM] * 6,
-        out_specs=[ANY] * 3,
-        scratch_shapes=[
-            pltpu.VMEM((5, NC * R, 128), F32),
-            pltpu.VMEM((6, NC * R, 128), F32),
-            pltpu.VMEM((2 * TOP, R, 128), F32),
+    state = call(
+        second_interior,
+        "interior2",
+        main,
+        [f4, *state],
+        [VM] * 5,
+        [],
+        alias={1 + k: k for k in range(4)},
+        cost=cost,
+    )
+    vel, strs, ocean, *_ = call(
+        second_edges,
+        "edges2",
+        [*[shape(n, 2, 8, 32, 128) for n in (2, 3, 2)], *main, strips],
+        [rb, ra, f4, *state, strip],
+        [VM] * 8,
+        [
             pltpu.VMEM((28, R, 128), F32),
             pltpu.VMEM((7, *STAGE), F32),
             pltpu.SemaphoreType.DMA((3,)),
         ],
-        compiler_params=pltpu.CompilerParams(vmem_limit_bytes=32 << 20),
-        name="second",
-    )(st, sc, strip, rb, ra, cor)
+        alias={3 + k: 3 + k for k in range(5)},
+        outs=[HBM] * 3 + [VM] * 5,
+    )
     return unview(vel), unview(strs), unview(ocean)
 
 

time: 51.6 us -> 36.7 us (0.71)
  waiting for transfers between devices: 19.9 us -> 8.76 us
  local copies, waits for them, and re-layouts: 6.11 us -> 0.01 us
  Pallas kernels: 11.9 us -> 14.3 us
    ppermute x1, waiting for transfers between devices: 11 us -> 3.39 us  [on_device(): rm = lax.ppermute(m, AXES, [(d, 127 - d) for d in range(128)])]
    unnamed x22 -> x2, local copies, waits for them, and re-layouts: 6.11 us -> 0.01 us
    ppermute x4, waiting for transfers between devices: 8.93 us -> 5.38 us  [swap(): return (lax.ppermute(b, AXES, cross), lax.ppermute(a, AXES, chip))]
    pallas_call x3 -> x5, Pallas kernels: 11.9 us -> 14.3 us  [call(): pl.pallas_call(kernel, out_shape=out, in_specs=specs, out_specs=outs or [...]
  transfers between devices with their start and end apart: 5 -> 5, of which waited for: 2 -> 2; matrix products, arithmetic and copies ran while one was open for 0% -> 0% of each run, Pallas kernels for 0% -> 20%
where the time goes in v1:
time: 36.7 us; the launch traced here: 36.6 us
  Pallas kernels  14.3 us (39%)
  starting transfers between devices  12.9 us (35%)
  waiting for transfers between devices  8.76 us (24%)
  between operations  0.67 us (2%)
    pallas_call x5, Pallas kernels, call(): pl.pallas_call(kernel, out_shape=out, in_specs=specs, out_specs=outs or [...  14.3 us
    ppermute x4, starting transfers between devices, swap(): return (lax.ppermute(b, AXES, cross), lax.ppermute(a, AXES, chip))  11.4 us
    ppermute x4, waiting for transfers between devices, swap(): return (lax.ppermute(b, AXES, cross), lax.ppermute(a, AXES, chip))  5.38 us
    ppermute x1, waiting for transfers between devices, on_device(): rm = lax.ppermute(m, AXES, [(d, 127 - d) for d in range(128)])  3.39 us
    ppermute x1, starting transfers between devices, on_device(): rm = lax.ppermute(m, AXES, [(d, 127 - d) for d in range(128)])  1.52 us
  transfers between devices with their start and end apart: 5, of which 2 were waited for; matrix products, arithmetic and copies ran while one was open for 0% of the time, Pallas kernels for 20%

profile of v1, /device:TPU:0, one launch (start us, length us, event | category | flops | bytes accessed | tf_op | source)
XLA Modules:
  0.0 36.6 jit_solution(11103745355388034270)
XLA Ops:
  0.6 0.0 copy-start
  0.6 2.1 %pack.1 = (f32[768,128]{1,0:T(8,128)S(1)}, f32[768,128]{1,0:T(8,128)S(1)}, f32[24,128]{1,0:T(8,128)S(1)}) custom-call(f32[4,2,8,32,128]{4,3,2,1,0:T(8,128)} %bitcast.40, f32[2,2,8,32,128]{4,3,2,1,0:T(8,128)} %bitcast.44, f32[2,2,8,32,128]{4,3,2,1,0:T(8,128)} %bitcast.46, f32[3,2,8,32,128]{4,3,2,1,0:T(8,128)} %bitcast.42, s32[1,2,8,32,128]{4,3,2,1,0:T(8,128)} %bitcast.48), custom_call_target="tpu_custom_call" | custom-call | tf_op jit(solution)/shard_map/pack/pallas_call | solution.py:478
  2.7 8.3 %collective-permute-start = (f32[768,128]{1,0:T(8,128)S(1)}, f32[768,128]{1,0:T(8,128)S(1)}, u32[]{:S(2)}, u32[]{:S(2)}) collective-permute-start(f32[768,128]{1,0:T(8,128)S(1)} %get-tuple-element.26), channel_id=1, source_target_pairs={{0,127},{1,2},{2,1},{3,4},{4,3},{5,6},{6,5},{7,8},{8,7},{9,10},{10... | collective-permute-start | bytes 1179656 | tf_op jit(solution)/shard_map/ppermute | solution.py:460
  11.0 0.0 collective-permute-start.1
  11.0 1.5 %collective-permute-start.2 = (f32[24,128]{1,0:T(8,128)S(1)}, f32[24,128]{1,0:T(8,128)S(1)}, u32[]{:S(2)}, u32[]{:S(2)}) collective-permute-start(f32[24,128]{1,0:T(8,128)S(1)} %get-tuple-element.28), channel_id=1, source_target_pairs={{0,127},{1,126},{2,125},{3,124},{4,123},{5,122},{6,121},{7,120},{8... | collective-permute-start | bytes 36872 | tf_op jit(solution)/shard_map/ppermute | solution.py:506
  12.6 0.0 copy-done
  12.6 5.0 %interior1.1 = (f32[5,704,128]{2,1,0:T(8,128)S(1)}, f32[9,704,128]{2,1,0:T(8,128)S(1)}, f32[6,704,128]{2,1,0:T(8,128)S(1)}, f32[6,704,128]{2,1,0:T(8,128)S(1)}, ...) custom-call(f32[4,2,8,32,128]{4,3,2,1,0:T(8,128)} %bitcast.41, f32[2,2,8,32,128]{4,3,2,1,0:T(8,128)} %bitcast.45, ...), custom_call_target="tpu_custom_call" | custom-call | flops 20000000 | bytes 4000000 | tf_op jit(solution)/shard_map/interior1/pallas_call | solution.py:478
  17.6 3.4 %collective-permute-done.2.refs_2_ = f32[24,128]{1,0:T(8,128)S(1)} collective-permute-done((f32[24,128]{1,0:T(8,128)S(1)}, f32[24,128]{1,0:T(8,128)S(1)}, u32[]{:S(2)}, u32[]{:S(2)}) %collective-permute-start.2) | collective-permute-done | bytes 12320 | tf_op jit(solution)/shard_map/ppermute | solution.py:506
  21.0 0.0 collective-permute-done.refs_0_
  21.0 0.0 collective-permute-done.1.refs_1_
  21.0 1.3 %edges1.1 = (f32[5,704,128]{2,1,0:T(8,128)S(1)}, f32[9,704,128]{2,1,0:T(8,128)S(1)}, f32[6,704,128]{2,1,0:T(8,128)S(1)}, f32[6,704,128]{2,1,0:T(8,128)S(1)}, f32...) custom-call(f32[768,128]{1,0:T(8,128)S(1)} %collective-permute-done., ...), custom_call_target="tpu_custom_call", output_to_operand_aliasing={{0}: (4, {}), {1}: (5, {}), {2}: (6, {}), {3}: (7, {}), {4}... | custom-call | tf_op jit(solution)/shard_map/edges1/pallas_call | solution.py:478
  22.3 3.0 %collective-permute-start.3 = (f32[408,128]{1,0:T(8,128)S(1)}, f32[408,128]{1,0:T(8,128)S(1)}, u32[]{:S(2)}, u32[]{:S(2)}) collective-permute-start(f32[408,128]{1,0:T(8,128)S(1)} %get-tuple-element.35), channel_id=1, source_target_pairs={{0,127},{1,2},{2,1},{3,4},{4,3},{5,6},{6,5},{7,8},{8,7},{9,10},{10... | collective-permute-start | bytes 626696 | tf_op jit(solution)/shard_map/ppermute | solution.py:460
  25.4 0.0 collective-permute-start.4
  25.4 2.3 %interior2.1 = (f32[5,704,128]{2,1,0:T(8,128)S(1)}, f32[9,704,128]{2,1,0:T(8,128)S(1)}, f32[6,704,128]{2,1,0:T(8,128)S(1)}, f32[6,704,128]{2,1,0:T(8,128)S(1)}) custom-call(f32[32,128]{1,0:T(8,128)S(1)} %get-tuple-element.29.refs_3_.refs_0_.refs_2_, ...), custom_call_target="tpu_custom_call", output_to_operand_aliasing={{0}: (1, {}), {1}: (2, {}), {2}: (3, {}), {3}: (4, {})} | custom-call | flops 20000000 | bytes 4000000 | tf_op jit(solution)/shard_map/interior2/pallas_call | solution.py:478
  27.7 5.4 %collective-permute-done.3.refs_0_ = f32[408,128]{1,0:T(8,128)S(1)} collective-permute-done((f32[408,128]{1,0:T(8,128)S(1)}, f32[408,128]{1,0:T(8,128)S(1)}, u32[]{:S(2)}, u32[]{:S(2)}) %collective-permute-start.3) | collective-permute-done | bytes 208928 | tf_op jit(solution)/shard_map/ppermute | solution.py:460
  33.0 0.0 collective-permute-done.4.refs_1_
  33.0 3.5 %edges2.1 = (f32[2,2,8,32,128]{4,3,2,1,0:T(8,128)}, f32[3,2,8,32,128]{4,3,2,1,0:T(8,128)}, f32[2,2,8,32,128]{4,3,2,1,0:T(8,128)}, f32[5,704,128]{2,1,0:T(8,128)S...) custom-call(f32[408,128]{1,0:T(8,128)S(1)} %collective-permute-done., ...), custom_call_target="tpu_custom_call", output_to_operand_aliasing={{3}: (3, {}), {4}: (4, {}), {5}: (5, {}), {6}: (6, {}), {7}... | custom-call | tf_op jit(solution)/shard_map/edges2/pallas_call | solution.py:478
Async XLA Ops:
  0.6 11.9 %copy-start = (f32[32,128]{1,0:T(8,128)S(1)}, f32[32,128]{1,0:T(8,128)}, u32[]{:S(2)}) copy-start(f32[32,128]{1,0:T(8,128)} %constant.2.clone.cor) | copy-start | bytes 49156
  2.7 18.3 %collective-permute-start = (f32[768,128]{1,0:T(8,128)S(1)}, f32[768,128]{1,0:T(8,128)S(1)}, u32[]{:S(2)}, u32[]{:S(2)}) collective-permute-start(f32[768,128]{1,0:T(8,128)S(1)} %get-tuple-element.26), channel_id=1, source_target_pairs={{0,127},{1,2},{2,1},{3,4},{4,3},{5,6},{6,5},{7,8},{8,7},{9,10},{10... | collective-permute-start | bytes 1179656 | tf_op jit(solution)/shard_map/ppermute | solution.py:460
  11.0 9.9 %collective-permute-start.1 = (f32[768,128]{1,0:T(8,128)S(1)}, f32[768,128]{1,0:T(8,128)S(1)}, u32[]{:S(2)}, u32[]{:S(2)}) collective-permute-start(f32[768,128]{1,0:T(8,128)S(1)} %get-tuple-element.27), channel_id=1, source_target_pairs={{0,1},{1,0},{2,3},{3,2},{4,5},{5,4},{6,7},{7,6},{8,9},{9,8},{10,11... | collective-permute-start | bytes 1179656 | tf_op jit(solution)/shard_map/ppermute | solution.py:460
  11.0 9.9 %collective-permute-start.2 = (f32[24,128]{1,0:T(8,128)S(1)}, f32[24,128]{1,0:T(8,128)S(1)}, u32[]{:S(2)}, u32[]{:S(2)}) collective-permute-start(f32[24,128]{1,0:T(8,128)S(1)} %get-tuple-element.28), channel_id=1, source_target_pairs={{0,127},{1,126},{2,125},{3,124},{4,123},{5,122},{6,121},{7,120},{8... | collective-permute-start | bytes 36872 | tf_op jit(solution)/shard_map/ppermute | solution.py:506
  22.3 10.7 %collective-permute-start.3 = (f32[408,128]{1,0:T(8,128)S(1)}, f32[408,128]{1,0:T(8,128)S(1)}, u32[]{:S(2)}, u32[]{:S(2)}) collective-permute-start(f32[408,128]{1,0:T(8,128)S(1)} %get-tuple-element.35), channel_id=1, source_target_pairs={{0,127},{1,2},{2,1},{3,4},{4,3},{5,6},{6,5},{7,8},{8,7},{9,10},{10... | collective-permute-start | bytes 626696 | tf_op jit(solution)/shard_map/ppermute | solution.py:460
  25.4 7.7 %collective-permute-start.4 = (f32[408,128]{1,0:T(8,128)S(1)}, f32[408,128]{1,0:T(8,128)S(1)}, u32[]{:S(2)}, u32[]{:S(2)}) collective-permute-start(f32[408,128]{1,0:T(8,128)S(1)} %get-tuple-element.36), channel_id=1, source_target_pairs={{0,1},{1,0},{2,3},{3,2},{4,5},{5,4},{6,7},{7,6},{8,9},{9,8},{10,11... | collective-permute-start | bytes 626696 | tf_op jit(solution)/shard_map/ppermute | solution.py:460

commit v2 on v1

--- a/solution.py
+++ b/solution.py
@@ -17,9 +17,7 @@
 FIELDS = ("uo", "vo", "tx", "ty", "a", "h", "u", "v", "s1", "s2", "s12", "mask")
 WHERE = {n: k for k, n in enumerate(FIELDS)}
 STATE = ("u", "v", "s1", "s2", "s12")
-NEAR = [(n, 1) for n in ("a", "h", "u", "v", "s1", "s2", "s12", "mask", "o", "t")]
-FIRST = [(n, 0) for n in FIELDS] + NEAR + [("u", 2), ("v", 2)]
-SECOND = [(n, m) for m in range(2) for n in STATE] + [("u", 2), ("v", 2)]
+NEXT = ("u", "v", "z", "alpha", "beta")
 U, V, S1, S2, S12 = range(5)
 PR, MI, UO, CU, VO, CV, MK, OU, OV = range(9)
 T, D2, W, DV2, E1, UP = range(6)
@@ -165,14 +163,81 @@
     subcycle(st, sc, tmp2, f4, masks, (2, 14, 6), (3, 13, 5), (4, 12, 4))
 
 
-def edges(st, sc, tmp1, tmp2, f4):
+def edges(st, sc, tmp1, tmp2, f4, left, right):
     masks = make_masks()
+    st[U, rows(-2), :], st[V, rows(-2), :] = left["u"], left["v"]
+    st[U, rows(17), :], st[V, rows(17), :] = right["u"], right["v"]
+    st[S12, rows(-2), :] = left["z"]
+    st[S1, rows(17), :] = right["z"]
+    st[S2, rows(17), :] = jnp.zeros((R, 128), F32)
     subcycle(
-        st, sc, tmp1, f4, masks, both(-3, 0, 16, 19), both(-2, 1, 15, 18), both(-2, 2, 14, 18)
-    )
+        st, sc, tmp1, f4, masks, both(-2, 0, 16, 18), both(-1, 1, 15, 17), both(-1, 2, 14, 17)
+    )
+    n11 = 0.5 * (st[S1, rows(-1), :] + st[S2, rows(-1), :])
+    st[U, rows(-2), :] = left["alpha"] + left["beta"] * n11
+    st[V, rows(17), :] = right["alpha"] - right["beta"] * st[S12, rows(16), :]
     subcycle(
         st, sc, tmp2, f4, masks, both(-2, 2, 14, 18), both(-1, 3, 13, 17), both(0, 4, 12, 16)
     )
+
+
+def outgoing(st, sc, f4):
+    masks = make_masks()
+
+    def around(c):
+        s = lambda k, d=0: st[k, rows(c + d), :]
+        f = lambda k: sc[k, rows(c), :]
+        t, d2, w, dv2 = [], [], [], []
+        for d in (-1, 0, 1):
+            u, v = s(U, d), s(V, d)
+            up, um, vp, vm = above(u, masks), below(u, masks), above(v, masks), below(v, masks)
+            t.append(u + up)
+            d2.append(up - um)
+            w.append(v + vm)
+            dv2.append(vp - vm)
+            if d == 0:
+                e1, rise = v - vm, up - u
+        a1, a2, a12 = stress_terms(
+            s(U) - s(U, -1),
+            e1,
+            (d2[1] + d2[0]) + (w[2] - w[0]),
+            t[2] - t[0],
+            dv2[1] + dv2[2],
+            rise + (s(V, 1) - s(V)),
+            f(PR),
+        )
+        s1, s2, s12 = K29 * s(S1) + a1, K29 * s(S2) + a2, K29 * s(S12) + a12
+        return s, f, t, w, s1 + s2, s1 - s2, s12
+
+    def numbers(x, o, c, mi, force, cor, ice, open_o):
+        g = 0.5 * root((o - x) * (o - x) + 0.0025) * mi
+        b = 1.0 / (31.0 + g)
+        a = (30.0 * x + c + force * mi + g * o + cor) * b
+        return jnp.where(ice, a, open_o), jnp.where(ice, mi * b, 0.0)
+
+    s, f, t, w, q1, q2, s12 = around(1)
+    force = 0.5 * (above(q2, masks) - q2) + s12
+    ab = numbers(
+        s(V), f(VO), f(CV), f(MI), force, -f4 * (t[1] + t[0]), f(MK) == 2.0, f(OV)
+    )
+    left = (s(U), s(V), q1, *ab)
+    s, f, t, w, q1, q2, s12 = around(C - 2)
+    force = (s12 - below(s12, masks)) - 0.5 * q1
+    ab = numbers(s(U), f(UO), f(CU), f(MI), force, f4 * (w[1] + w[2]), f(MK) == 2.0, f(OU))
+    return left, (s(U), s(V), s12, *ab)
+
+
+def send(b_out, a_out, n, left, right, even):
+    b_out[pl.ds(n * R, R), :] = jnp.where(even, left, right)
+    a_out[pl.ds(n * R, R), :] = jnp.where(even, right, left)
+
+
+def receive(rb, ra, names, even):
+    left, right = {}, {}
+    for n, name in enumerate(names):
+        b, a = rb[pl.ds(n * R, R), :], ra[pl.ds(n * R, R), :]
+        left[name], right[name] = jnp.where(even, b, a), jnp.where(even, a, b)
+    return left, right
 
 
 def statics(raw):
@@ -254,36 +319,36 @@
     return ref[f, ih, pl.ds(7 * 40 + 24, 8), :].astype(F32)
 
 
-def pack_kernel(f_ref, i_ref, v_ref, s_ref, m_ref, b_out, a_out, m_out, stage, mstage, sems):
+def pack_kernel(
+    f_ref, i_ref, v_ref, s_ref, m_ref, cor, b_out, a_out, m_out, f4, st, sc, stage, mstage, sems
+):
+    cor_in = pltpu.make_async_copy(cor, f4, sems.at[5])
+    cor_in.start()
     stage_in((f_ref, i_ref, v_ref, s_ref, m_ref), stage, mstage, sems)
+    cor_in.wait()
     even = parity() == 0
-    for n, (name, m) in enumerate(FIRST):
-        far = {"o": ("vo", "uo"), "t": ("ty", "tx")}.get(name, (name, name))
-        left = staged_column(stage, mstage, far[0], m)
-        right = staged_column(stage, mstage, far[1], C - 1 - m)
-        b_out[pl.ds(n * R, R), :] = jnp.where(even, left, right)
-        a_out[pl.ds(n * R, R), :] = jnp.where(even, right, left)
+    for c in (1, C - 2):
+        put_column(
+            st, sc, rows(c), {name: staged_column(stage, mstage, name, c) for name in FIELDS}
+        )
+    for c in (0, 2, C - 3, C - 1):
+        for k, name in ((U, "u"), (V, "v")):
+            st[k, rows(c), :] = staged_column(stage, mstage, name, c)
+    for n, name in enumerate(FIELDS):
+        left = staged_column(stage, mstage, name, 0)
+        right = staged_column(stage, mstage, name, C - 1)
+        send(b_out, a_out, n, left, right, even)
+    for n, pair in enumerate(zip(*outgoing(st, sc, f4[...]))):
+        send(b_out, a_out, TOP + n, *pair, even)
     tops = squeeze([top_tile(stage, mstage, k, ih) for k in range(TOP) for ih in range(2)])
     for n, x in enumerate(tops):
         m_out[pl.ds(8 * n, 8), :] = x
 
 
-def halo_rows(even, m):
-    left, right = (H - 1 - m) * R, (H + C + m) * R
-    via_b = pl.ds(pl.multiple_of(jnp.where(even, left, right), R), R)
-    via_a = pl.ds(pl.multiple_of(jnp.where(even, right, left), R), R)
-    return via_b, via_a
-
-
 def first_interior(
-    f_ref, i_ref, v_ref, s_ref, m_ref, cor, st, sc, tmp1, tmp2, strip, f4, stage, mstage, sems
+    f_ref, i_ref, v_ref, s_ref, m_ref, f4, st, sc, tmp1, tmp2, strip, stage, mstage, sems
 ):
     stage_in((f_ref, i_ref, v_ref, s_ref, m_ref), stage, mstage, sems)
-    zero = jnp.zeros((R, 128), F32)
-    for k in (S1, S2, S12):
-        st[k, rows(-3), :] = zero
-        st[k, rows(18), :] = zero
-    f4[...] = 0.25 * cor[...]
     for c in range(C):
         put_column(
             st, sc, rows(c), {name: staged_column(stage, mstage, name, c) for name in FIELDS}
@@ -298,33 +363,22 @@
     rb, ra, rm, f4 = refs[:4]
     st, sc, tmp1, tmp2, strip, b_out, a_out = refs[9:]
     even = parity() == 0
-    for m in range(H):
-        via = halo_rows(even, m)
-        for at, src in zip(via, (rb, ra)):
-            raw = {
-                name: src[pl.ds(n * R, R), :] for n, (name, d) in enumerate(FIRST) if d == m
-            }
-            if m == 1:
-                raw["uo"] = raw["vo"] = raw["o"]
-                raw["tx"] = raw["ty"] = raw["t"]
-            if m < 2:
-                put_column(st, sc, at, raw)
-            else:
-                st[U, at, :] = raw["u"]
-                st[V, at, :] = raw["v"]
+    left, right = receive(rb, ra, (*FIELDS, *[n + "1" for n in NEXT]), even)
+    put_column(st, sc, rows(-1), left)
+    put_column(st, sc, rows(C), right)
     flip = 7 - iotas((8, 128))[0]
     packed = [rm[pl.ds(8 * n, 8), :] for n in range(3)]
     for k in range(TOP):
         for ih in range(2):
             x = spread(packed, 2 * k + ih)
             strip[TOP + k, pl.ds(16 - 8 * ih, 8), :] = jnp.take_along_axis(x, flip, axis=0)
-    edges(st, sc, tmp1, tmp2, f4[...])
-    for n, (name, m) in enumerate(SECOND):
-        left = st[STATE.index(name), rows(m), :]
-        right = st[STATE.index(name), rows(C - 1 - m), :]
-        b_out[pl.ds(n * R, R), :] = jnp.where(even, left, right)
-        a_out[pl.ds(n * R, R), :] = jnp.where(even, right, left)
-    base = len(SECOND) * R
+    near = [{n: x[n + "1"] for n in NEXT} for x in (left, right)]
+    edges(st, sc, tmp1, tmp2, f4[...], *near)
+    for k in range(5):
+        send(b_out, a_out, k, st[k, rows(0), :], st[k, rows(C - 1), :], even)
+    for n, pair in enumerate(zip(*outgoing(st, sc, f4[...]))):
+        send(b_out, a_out, 5 + n, *pair, even)
+    base = (5 + len(NEXT)) * R
     left = squeeze([strip[k, pl.ds(8, 8), :] for k in range(2 * TOP)])
     right = squeeze([strip[k, pl.ds(16, 8), :] for k in range(2 * TOP)])
     for n in range(3):
@@ -403,13 +457,11 @@
     rb, ra, f4 = refs[:3]
     vel_o, str_o, oce_o, st, sc, tmp1, tmp2, strip, work, stage, sems = refs[8:]
     even = parity() == 0
-    for m in range(H):
-        via = halo_rows(even, m)
-        for at, src in zip(via, (rb, ra)):
-            for n, (name, d) in enumerate(SECOND):
-                if d == m:
-                    st[STATE.index(name), at, :] = src[pl.ds(n * R, R), :]
-    base = len(SECOND) * R
+    left, right = receive(rb, ra, (*STATE, *[n + "1" for n in NEXT]), even)
+    for k, name in enumerate(STATE):
+        st[k, rows(-1), :], st[k, rows(C), :] = left[name], right[name]
+    near = [{n: x[n + "1"] for n in NEXT} for x in (left, right)]
+    base = (5 + len(NEXT)) * R
     pb = [rb[pl.ds(base + 8 * n, 8), :] for n in range(3)]
     pa = [ra[pl.ds(base + 8 * n, 8), :] for n in range(3)]
     low = [jnp.where(even, b, a) for b, a in zip(pb, pa)]
@@ -420,7 +472,7 @@
     step = run_strips(strip, work, f4)
     for _ in range(4):
         step()
-    edges(st, sc, tmp1, tmp2, f4[...])
+    edges(st, sc, tmp1, tmp2, f4[...], *near)
     row, lane = iotas((R, 128))
     top = (row == R - 1) & (lane >= 120)
 
@@ -463,14 +515,14 @@
 def coriolis():
     b = 4 * np.arange(8)[None, :] + np.arange(4)[:, None]
     j = b.reshape(32, 1) * 128 + np.arange(128)[None, :]
-    return (0.5 * np.sin(math.pi * ((j + 0.5) / 4096 - 0.5))).astype(np.float32)
+    return (0.125 * np.sin(math.pi * ((j + 0.5) / 4096 - 0.5))).astype(np.float32)
 
 
 def staging():
     return [
         pltpu.VMEM((11, *STAGE), F32),
         pltpu.VMEM((1, *STAGE), jnp.int32),
-        pltpu.SemaphoreType.DMA((5,)),
+        pltpu.SemaphoreType.DMA((6,)),
     ]
 
 
@@ -493,26 +545,26 @@
         pltpu.with_memory_space_constraint(view(x), pltpu.HBM)
         for x in (forcing, ice_state, velocity, stress, ice_mask[None])
     ]
-    n1, n2 = len(FIRST) * R, len(SECOND) * R + 24
-    b, a, m = call(
+    n1, n2 = (TOP + len(NEXT)) * R, (5 + len(NEXT)) * R + 24
+    cor = pltpu.with_memory_space_constraint(jnp.asarray(coriolis()), pltpu.HBM)
+    b, a, m, f4 = call(
         pack_kernel,
         "pack",
-        [shape(n1, 128), shape(n1, 128), shape(24, 128)],
-        raw,
-        [HBM] * 5,
-        staging(),
+        [shape(n1, 128), shape(n1, 128), shape(24, 128), shape(R, 128)],
+        [*raw, cor],
+        [HBM] * 6,
+        [pltpu.VMEM((5, NC * R, 128), F32), pltpu.VMEM((9, NC * R, 128), F32), *staging()],
     )
     rb, ra = swap(b, a)
     rm = lax.ppermute(m, AXES, [(d, 127 - d) for d in range(128)])
-    cor = jnp.asarray(coriolis())
     cost = pl.CostEstimate(flops=20_000_000, bytes_accessed=4_000_000, transcendentals=500_000)
     main = [shape(5, NC * R, 128), shape(9, NC * R, 128), *[shape(6, NC * R, 128)] * 2]
     strips = shape(2 * TOP, R, 128)
-    *state, strip, f4 = call(
+    *state, strip = call(
         first_interior,
         "interior1",
-        [*main, strips, shape(R, 128)],
-        [*raw, cor],
+        [*main, strips],
+        [*raw, f4],
         [HBM] * 5 + [VM],
         staging(),
         cost=cost,

time: 36.7 us -> 34.9 us (0.951)
  waiting for transfers between devices: 8.76 us -> 6.41 us
  starting transfers between devices: 12.9 us -> 13.5 us
    ppermute x1, waiting for transfers between devices: 3.39 us -> 2.05 us  [on_device(): rm = lax.ppermute(m, AXES, [(d, 127 - d) for d in range(128)])]
    ppermute x4, waiting for transfers between devices: 5.38 us -> 4.36 us  [swap(): return (lax.ppermute(b, AXES, cross), lax.ppermute(a, AXES, chip))]
    ppermute x4, starting transfers between devices: 11.4 us -> 12 us  [swap(): return (lax.ppermute(b, AXES, cross), lax.ppermute(a, AXES, chip))]
  transfers between devices with their start and end apart: 5 -> 5, of which waited for: 2 -> 2; matrix products, arithmetic and copies ran while one was open for 0% -> 0% of each run, Pallas kernels for 20% -> 21%
where the time goes in v2:
time: 34.9 us; the launch traced here: 34.8 us
  Pallas kernels  14.2 us (41%)
  starting transfers between devices  13.5 us (39%)
  waiting for transfers between devices  6.41 us (18%)
  between operations  0.67 us (2%)
    pallas_call x5, Pallas kernels, call(): pl.pallas_call(kernel, out_shape=out, in_specs=specs, out_specs=outs or [...  14.2 us
    ppermute x4, starting transfers between devices, swap(): return (lax.ppermute(b, AXES, cross), lax.ppermute(a, AXES, chip))  12 us
    ppermute x4, waiting for transfers between devices, swap(): return (lax.ppermute(b, AXES, cross), lax.ppermute(a, AXES, chip))  4.36 us
    ppermute x1, waiting for transfers between devices, on_device(): rm = lax.ppermute(m, AXES, [(d, 127 - d) for d in range(128)])  2.05 us
    ppermute x1, starting transfers between devices, on_device(): rm = lax.ppermute(m, AXES, [(d, 127 - d) for d in range(128)])  1.52 us
  transfers between devices with their start and end apart: 5, of which 2 were waited for; matrix products, arithmetic and copies ran while one was open for 0% of the time, Pallas kernels for 21%

profile of v2, /device:TPU:0, one launch (start us, length us, event | category | flops | bytes accessed | tf_op | source)
XLA Modules:
  0.0 34.8 jit_solution(306827180005302793)
XLA Ops:
  0.6 2.2 %pack.1 = (f32[544,128]{1,0:T(8,128)S(1)}, f32[544,128]{1,0:T(8,128)S(1)}, f32[24,128]{1,0:T(8,128)S(1)}, f32[32,128]{1,0:T(8,128)S(1)}) custom-call(f32[4,2,8,32,128]{4,3,2,1,0:T(8,128)} %bitcast.40, f32[2,2,8,32,128]{4,3,2,1,0:T(8,128)} %bitcast.44, f32[2,2,8,32,128]{4,3,2,1,0:T(8,128)} %bitcast.46, f32[3,2,8,32,128]{4,3,2,1,0:T(8,128)} %bitcast.42, ...), custom_call_target="tpu_custom_call" | custom-call | tf_op jit(solution)/shard_map/pack/pallas_call | solution.py:530
  2.8 8.3 %collective-permute-start = (f32[544,128]{1,0:T(8,128)S(1)}, f32[544,128]{1,0:T(8,128)S(1)}, u32[]{:S(2)}, u32[]{:S(2)}) collective-permute-start(f32[544,128]{1,0:T(8,128)S(1)} %get-tuple-element.26), channel_id=1, source_target_pairs={{0,127},{1,2},{2,1},{3,4},{4,3},{5,6},{6,5},{7,8},{8,7},{9,10},{10... | collective-permute-start | bytes 835592 | tf_op jit(solution)/shard_map/ppermute | solution.py:512
  11.2 0.0 collective-permute-start.1
  11.2 1.5 %collective-permute-start.2 = (f32[24,128]{1,0:T(8,128)S(1)}, f32[24,128]{1,0:T(8,128)S(1)}, u32[]{:S(2)}, u32[]{:S(2)}) collective-permute-start(f32[24,128]{1,0:T(8,128)S(1)} %get-tuple-element.28), channel_id=1, source_target_pairs={{0,127},{1,126},{2,125},{3,124},{4,123},{5,122},{6,121},{7,120},{8... | collective-permute-start | bytes 36872 | tf_op jit(solution)/shard_map/ppermute | solution.py:559
  12.7 5.0 %interior1.1 = (f32[5,704,128]{2,1,0:T(8,128)S(1)}, f32[9,704,128]{2,1,0:T(8,128)S(1)}, f32[6,704,128]{2,1,0:T(8,128)S(1)}, f32[6,704,128]{2,1,0:T(8,128)S(1)}, f32[24,32,128]{2,1,0:T(8,128)S(1)}) custom-call(f32[4,2,8,32,128]{4,3,2,1,0:T(8,128)} %bitcast.41, f32[2,2,8,32,128]{4,3,2,1,0:T(8,128)} %bitcast.45, f32[2,2,8,32,128]{4,3,2,1,0:T(8,128)} %bitcast.47, ...), custom_call_target="tpu_custom_call" | custom-call | flops 20000000 | bytes 4000000 | tf_op jit(solution)/shard_map/interior1/pallas_call | solution.py:530
  17.7 2.1 %collective-permute-done.2.refs_2_ = f32[24,128]{1,0:T(8,128)S(1)} collective-permute-done((f32[24,128]{1,0:T(8,128)S(1)}, f32[24,128]{1,0:T(8,128)S(1)}, u32[]{:S(2)}, u32[]{:S(2)}) %collective-permute-start.2) | collective-permute-done | bytes 12320 | tf_op jit(solution)/shard_map/ppermute | solution.py:559
  19.7 0.0 collective-permute-done.refs_0_
  19.7 0.0 collective-permute-done.1.refs_1_
  19.7 1.3 %edges1.1 = (f32[5,704,128]{2,1,0:T(8,128)S(1)}, f32[9,704,128]{2,1,0:T(8,128)S(1)}, f32[6,704,128]{2,1,0:T(8,128)S(1)}, f32[6,704,128]{2,1,0:T(8,128)S(1)}, f32...) custom-call(f32[544,128]{1,0:T(8,128)S(1)} %collective-permute-done., ...), custom_call_target="tpu_custom_call", output_to_operand_aliasing={{0}: (4, {}), {1}: (5, {}), {2}: (6, {}), {3}: (7, {}), {4}... | custom-call | tf_op jit(solution)/shard_map/edges1/pallas_call | solution.py:530
  21.0 3.7 %collective-permute-start.3 = (f32[344,128]{1,0:T(8,128)S(1)}, f32[344,128]{1,0:T(8,128)S(1)}, u32[]{:S(2)}, u32[]{:S(2)}) collective-permute-start(f32[344,128]{1,0:T(8,128)S(1)} %get-tuple-element.35), channel_id=1, source_target_pairs={{0,127},{1,2},{2,1},{3,4},{4,3},{5,6},{6,5},{7,8},{8,7},{9,10},{10... | collective-permute-start | bytes 528392 | tf_op jit(solution)/shard_map/ppermute | solution.py:512
  24.7 0.0 collective-permute-start.4
  24.7 2.3 %interior2.1 = (f32[5,704,128]{2,1,0:T(8,128)S(1)}, f32[9,704,128]{2,1,0:T(8,128)S(1)}, f32[6,704,128]{2,1,0:T(8,128)S(1)}, f32[6,704,128]{2,1,0:T(8,128)S(1)}) custom-call(f32[32,128]{1,0:T(8,128)S(1)} %get-tuple-element.29.f4.refs_3_.refs_0_.refs_2_, ...), custom_call_target="tpu_custom_call", output_to_operand_aliasing={{0}: (1, {}), {1}: (2, {}), {2}: (3, {}), {3}: (4, {})} | custom-call | flops 20000000 | bytes 4000000 | tf_op jit(solution)/shard_map/interior2/pallas_call | solution.py:530
  27.0 4.4 %collective-permute-done.3.refs_0_ = f32[344,128]{1,0:T(8,128)S(1)} collective-permute-done((f32[344,128]{1,0:T(8,128)S(1)}, f32[344,128]{1,0:T(8,128)S(1)}, u32[]{:S(2)}, u32[]{:S(2)}) %collective-permute-start.3) | collective-permute-done | bytes 176160 | tf_op jit(solution)/shard_map/ppermute | solution.py:512
  31.4 0.0 collective-permute-done.4.refs_1_
  31.4 3.4 %edges2.1 = (f32[2,2,8,32,128]{4,3,2,1,0:T(8,128)}, f32[3,2,8,32,128]{4,3,2,1,0:T(8,128)}, f32[2,2,8,32,128]{4,3,2,1,0:T(8,128)}, f32[5,704,128]{2,1,0:T(8,128)S...) custom-call(f32[344,128]{1,0:T(8,128)S(1)} %collective-permute-done., ...), custom_call_target="tpu_custom_call", output_to_operand_aliasing={{3}: (3, {}), {4}: (4, {}), {5}: (5, {}), {6}: (6, {}), {7}... | custom-call | tf_op jit(solution)/shard_map/edges2/pallas_call | solution.py:530
Async XLA Ops:
  2.8 16.9 %collective-permute-start = (f32[544,128]{1,0:T(8,128)S(1)}, f32[544,128]{1,0:T(8,128)S(1)}, u32[]{:S(2)}, u32[]{:S(2)}) collective-permute-start(f32[544,128]{1,0:T(8,128)S(1)} %get-tuple-element.26), channel_id=1, source_target_pairs={{0,127},{1,2},{2,1},{3,4},{4,3},{5,6},{6,5},{7,8},{8,7},{9,10},{10... | collective-permute-start | bytes 835592 | tf_op jit(solution)/shard_map/ppermute | solution.py:512
  11.2 8.6 %collective-permute-start.1 = (f32[544,128]{1,0:T(8,128)S(1)}, f32[544,128]{1,0:T(8,128)S(1)}, u32[]{:S(2)}, u32[]{:S(2)}) collective-permute-start(f32[544,128]{1,0:T(8,128)S(1)} %get-tuple-element.27), channel_id=1, source_target_pairs={{0,1},{1,0},{2,3},{3,2},{4,5},{5,4},{6,7},{7,6},{8,9},{9,8},{10,11... | collective-permute-start | bytes 835592 | tf_op jit(solution)/shard_map/ppermute | solution.py:512
  11.2 8.6 %collective-permute-start.2 = (f32[24,128]{1,0:T(8,128)S(1)}, f32[24,128]{1,0:T(8,128)S(1)}, u32[]{:S(2)}, u32[]{:S(2)}) collective-permute-start(f32[24,128]{1,0:T(8,128)S(1)} %get-tuple-element.28), channel_id=1, source_target_pairs={{0,127},{1,126},{2,125},{3,124},{4,123},{5,122},{6,121},{7,120},{8... | collective-permute-start | bytes 36872 | tf_op jit(solution)/shard_map/ppermute | solution.py:559
  21.0 10.4 %collective-permute-start.3 = (f32[344,128]{1,0:T(8,128)S(1)}, f32[344,128]{1,0:T(8,128)S(1)}, u32[]{:S(2)}, u32[]{:S(2)}) collective-permute-start(f32[344,128]{1,0:T(8,128)S(1)} %get-tuple-element.35), channel_id=1, source_target_pairs={{0,127},{1,2},{2,1},{3,4},{4,3},{5,6},{6,5},{7,8},{8,7},{9,10},{10... | collective-permute-start | bytes 528392 | tf_op jit(solution)/shard_map/ppermute | solution.py:512
  24.7 6.7 %collective-permute-start.4 = (f32[344,128]{1,0:T(8,128)S(1)}, f32[344,128]{1,0:T(8,128)S(1)}, u32[]{:S(2)}, u32[]{:S(2)}) collective-permute-start(f32[344,128]{1,0:T(8,128)S(1)} %get-tuple-element.36), channel_id=1, source_target_pairs={{0,1},{1,0},{2,3},{3,2},{4,5},{5,4},{6,7},{7,6},{8,9},{9,8},{10,11... | collective-permute-start | bytes 528392 | tf_op jit(solution)/shard_map/ppermute | solution.py:512

commit v3 on v2

--- a/solution.py
+++ b/solution.py
@@ -7,6 +7,7 @@
 from jax.experimental import pallas as pl
 from jax.experimental.pallas import tpu as pltpu
 from jax.sharding import PartitionSpec as P
+
 
 F32 = jnp.float32
 AXES = ("gx", "gy")
@@ -153,35 +154,39 @@
     each_column(mom, move)
 
 
-def both(a, b, c, d):
-    return [*range(a, b), *range(c, d)]
-
-
 def interior(st, sc, tmp1, tmp2, f4):
     masks = make_masks()
     subcycle(st, sc, tmp1, f4, masks, (0, 16, 8), (1, 15, 7), (2, 14, 6))
     subcycle(st, sc, tmp2, f4, masks, (2, 14, 6), (3, 13, 5), (4, 12, 4))
 
 
-def edges(st, sc, tmp1, tmp2, f4, left, right):
+def edges(st, sc, tmp1, tmp2, f4, left=None, right=None):
     masks = make_masks()
-    st[U, rows(-2), :], st[V, rows(-2), :] = left["u"], left["v"]
-    st[U, rows(17), :], st[V, rows(17), :] = right["u"], right["v"]
-    st[S12, rows(-2), :] = left["z"]
-    st[S1, rows(17), :] = right["z"]
-    st[S2, rows(17), :] = jnp.zeros((R, 128), F32)
+
+    def near(a, b, c, d):
+        return [*(range(a, b) if left else ()), *(range(c, d) if right else ())]
+
+    if left:
+        st[U, rows(-2), :], st[V, rows(-2), :] = left["u"], left["v"]
+        st[S12, rows(-2), :] = left["z"]
+    if right:
+        st[U, rows(17), :], st[V, rows(17), :] = right["u"], right["v"]
+        st[S1, rows(17), :] = right["z"]
+        st[S2, rows(17), :] = jnp.zeros((R, 128), F32)
     subcycle(
-        st, sc, tmp1, f4, masks, both(-2, 0, 16, 18), both(-1, 1, 15, 17), both(-1, 2, 14, 17)
-    )
-    n11 = 0.5 * (st[S1, rows(-1), :] + st[S2, rows(-1), :])
-    st[U, rows(-2), :] = left["alpha"] + left["beta"] * n11
-    st[V, rows(17), :] = right["alpha"] - right["beta"] * st[S12, rows(16), :]
+        st, sc, tmp1, f4, masks, near(-2, 0, 16, 18), near(-1, 1, 15, 17), near(-1, 2, 14, 17)
+    )
+    if left:
+        n11 = 0.5 * (st[S1, rows(-1), :] + st[S2, rows(-1), :])
+        st[U, rows(-2), :] = left["alpha"] + left["beta"] * n11
+    if right:
+        st[V, rows(17), :] = right["alpha"] - right["beta"] * st[S12, rows(16), :]
     subcycle(
-        st, sc, tmp2, f4, masks, both(-2, 2, 14, 18), both(-1, 3, 13, 17), both(0, 4, 12, 16)
-    )
-
-
-def outgoing(st, sc, f4):
+        st, sc, tmp2, f4, masks, near(-2, 2, 14, 18), near(-1, 3, 13, 17), near(0, 4, 12, 16)
+    )
+
+
+def outgoing(st, sc, f4, side):
     masks = make_masks()
 
     def around(c):
@@ -215,29 +220,42 @@
         a = (30.0 * x + c + force * mi + g * o + cor) * b
         return jnp.where(ice, a, open_o), jnp.where(ice, mi * b, 0.0)
 
-    s, f, t, w, q1, q2, s12 = around(1)
-    force = 0.5 * (above(q2, masks) - q2) + s12
-    ab = numbers(
-        s(V), f(VO), f(CV), f(MI), force, -f4 * (t[1] + t[0]), f(MK) == 2.0, f(OV)
-    )
-    left = (s(U), s(V), q1, *ab)
+    if side == 0:
+        s, f, t, w, q1, q2, s12 = around(1)
+        force = 0.5 * (above(q2, masks) - q2) + s12
+        cor = -f4 * (t[1] + t[0])
+        ice = f(MK) == 2.0
+        return s(U), s(V), q1, *numbers(s(V), f(VO), f(CV), f(MI), force, cor, ice, f(OV))
     s, f, t, w, q1, q2, s12 = around(C - 2)
     force = (s12 - below(s12, masks)) - 0.5 * q1
-    ab = numbers(s(U), f(UO), f(CU), f(MI), force, f4 * (w[1] + w[2]), f(MK) == 2.0, f(OU))
-    return left, (s(U), s(V), s12, *ab)
-
-
-def send(b_out, a_out, n, left, right, even):
-    b_out[pl.ds(n * R, R), :] = jnp.where(even, left, right)
-    a_out[pl.ds(n * R, R), :] = jnp.where(even, right, left)
+    cor = f4 * (w[1] + w[2])
+    ice = f(MK) == 2.0
+    return s(U), s(V), s12, *numbers(s(U), f(UO), f(CU), f(MI), force, cor, ice, f(OU))
+
+
+def put(out, xs, n=0):
+    for x in xs:
+        out[pl.ds(n * R, R), :] = x
+        n += 1
+
+
+def take(ref, names):
+    return {name: ref[pl.ds(n * R, R), :] for n, name in enumerate(names)}
 
 
 def receive(rb, ra, names, even):
-    left, right = {}, {}
-    for n, name in enumerate(names):
-        b, a = rb[pl.ds(n * R, R), :], ra[pl.ds(n * R, R), :]
-        left[name], right[name] = jnp.where(even, b, a), jnp.where(even, a, b)
+    b, a = take(rb, names), take(ra, names)
+    left = {n: jnp.where(even, b[n], a[n]) for n in names}
+    right = {n: jnp.where(even, a[n], b[n]) for n in names}
     return left, right
+
+
+def next_names(x):
+    return {n: x[n + "1"] for n in NEXT}
+
+
+FIRST = (*FIELDS, *[n + "1" for n in NEXT])
+SECOND = (*STATE, *[n + "1" for n in NEXT])
 
 
 def statics(raw):
@@ -319,36 +337,78 @@
     return ref[f, ih, pl.ds(7 * 40 + 24, 8), :].astype(F32)
 
 
-def pack_kernel(
-    f_ref, i_ref, v_ref, s_ref, m_ref, cor, b_out, a_out, m_out, f4, st, sc, stage, mstage, sems
+def by_side(cross, body):
+    even = parity() == 0
+    here = even if cross else jnp.logical_not(even)
+
+    @pl.when(here)
+    def _():
+        body(0)
+
+    @pl.when(jnp.logical_not(here))
+    def _():
+        body(1)
+
+
+def pack_side(out, f4, st, sc, stage, mstage, side, half):
+    def column(name, m):
+        ref, f = (mstage, 0) if name == "mask" else (stage, WHERE[name])
+        il = 7 - m if side else m
+        parts = [ref[f, half, pl.ds(8 * k + il, 8, stride=40), :] for k in range(4)]
+        return jnp.concatenate(parts, 0).astype(F32)
+
+    at = lambda m: rows(C - 1 - m if side else m)
+    put_column(st, sc, at(1), {name: column(name, 1) for name in FIELDS})
+    for m in (0, 2):
+        st[U, at(m), :], st[V, at(m), :] = column("u", m), column("v", m)
+    put(out, [column(name, 0) for name in FIELDS])
+    put(out, outgoing(st, sc, f4[...], side), TOP)
+
+
+def pack_cross(
+    f_ref, i_ref, v_ref, s_ref, m_ref, cor, b_out, m_out, f4, st, sc, stage, mstage, top, mtop, sems
 ):
-    cor_in = pltpu.make_async_copy(cor, f4, sems.at[5])
-    cor_in.start()
+    srcs = (f_ref, i_ref, v_ref, s_ref, m_ref)
+
+    def body(side):
+        main = [pltpu.make_async_copy(cor, f4, sems.at[5])]
+        tops = []
+        at = 0
+        for k, src in enumerate(srcs):
+            n = src.shape[0]
+            if k < 4:
+                dst = stage.reshape(11, 1, 8, 40, 128).at[pl.ds(at, n), 0, :, pl.ds(0, 32), :]
+            else:
+                dst = mstage.reshape(1, 1, 8, 40, 128).at[:, 0, :, pl.ds(0, 32), :]
+            main.append(pltpu.make_async_copy(src.at[:, side], dst, sems.at[k]))
+            dst = top.at[pl.ds(at, n)] if k < 4 else mtop
+            tile = src.at[:, :, 7, pl.ds(24, 8), :]
+            tops.append(pltpu.make_async_copy(tile, dst, sems.at[6 + k]))
+            at += n
+        for c in main + tops:
+            c.start()
+        for c in main:
+            c.wait()
+        pack_side(b_out, f4, st, sc, stage, mstage, side, 0)
+        for c in tops:
+            c.wait()
+        tiles = [
+            mtop[0, ih].astype(F32) if k == TOP - 1 else top[k, ih]
+            for k in range(TOP)
+            for ih in range(2)
+        ]
+        for n, x in enumerate(squeeze(tiles)):
+            m_out[pl.ds(8 * n, 8), :] = x
+
+    by_side(True, body)
+
+
+def pack_chip(f_ref, i_ref, v_ref, s_ref, m_ref, f4, a_out, stage, mstage, st, sc, sems):
     stage_in((f_ref, i_ref, v_ref, s_ref, m_ref), stage, mstage, sems)
-    cor_in.wait()
-    even = parity() == 0
-    for c in (1, C - 2):
-        put_column(
-            st, sc, rows(c), {name: staged_column(stage, mstage, name, c) for name in FIELDS}
-        )
-    for c in (0, 2, C - 3, C - 1):
-        for k, name in ((U, "u"), (V, "v")):
-            st[k, rows(c), :] = staged_column(stage, mstage, name, c)
-    for n, name in enumerate(FIELDS):
-        left = staged_column(stage, mstage, name, 0)
-        right = staged_column(stage, mstage, name, C - 1)
-        send(b_out, a_out, n, left, right, even)
-    for n, pair in enumerate(zip(*outgoing(st, sc, f4[...]))):
-        send(b_out, a_out, TOP + n, *pair, even)
-    tops = squeeze([top_tile(stage, mstage, k, ih) for k in range(TOP) for ih in range(2)])
-    for n, x in enumerate(tops):
-        m_out[pl.ds(8 * n, 8), :] = x
-
-
-def first_interior(
-    f_ref, i_ref, v_ref, s_ref, m_ref, f4, st, sc, tmp1, tmp2, strip, stage, mstage, sems
-):
-    stage_in((f_ref, i_ref, v_ref, s_ref, m_ref), stage, mstage, sems)
+    by_side(False, lambda side: pack_side(a_out, f4, st, sc, stage, mstage, side, side))
+
+
+def first_interior(stage, mstage, f4, st, sc, tmp1, tmp2, strip):
     for c in range(C):
         put_column(
             st, sc, rows(c), {name: staged_column(stage, mstage, name, c) for name in FIELDS}
@@ -359,31 +419,36 @@
     interior(st, sc, tmp1, tmp2, f4[...])
 
 
-def first_edges(*refs):
-    rb, ra, rm, f4 = refs[:4]
-    st, sc, tmp1, tmp2, strip, b_out, a_out = refs[9:]
-    even = parity() == 0
-    left, right = receive(rb, ra, (*FIELDS, *[n + "1" for n in NEXT]), even)
-    put_column(st, sc, rows(-1), left)
-    put_column(st, sc, rows(C), right)
+def edge_side(r, out, st, sc, tmp1, tmp2, strip, f4, cross):
+    def body(side):
+        got = take(r, FIRST)
+        put_column(st, sc, rows(C if side else -1), got)
+        edges(st, sc, tmp1, tmp2, f4[...], **{("left", "right")[side]: next_names(got)})
+        put(out, [st[k, rows(C - 1 if side else 0), :] for k in range(5)])
+        put(out, outgoing(st, sc, f4[...], side), 5)
+        tiles = squeeze([strip[k, pl.ds(16 if side else 8, 8), :] for k in range(2 * TOP)])
+        for n, x in enumerate(tiles):
+            out[pl.ds(len(SECOND) * R + 8 * n, 8), :] = x
+
+    by_side(cross, body)
+
+
+def cross_edges(*refs):
+    rb, rm, f4 = refs[:3]
+    st, sc, tmp1, tmp2, strip, out = refs[8:]
     flip = 7 - iotas((8, 128))[0]
     packed = [rm[pl.ds(8 * n, 8), :] for n in range(3)]
     for k in range(TOP):
         for ih in range(2):
             x = spread(packed, 2 * k + ih)
             strip[TOP + k, pl.ds(16 - 8 * ih, 8), :] = jnp.take_along_axis(x, flip, axis=0)
-    near = [{n: x[n + "1"] for n in NEXT} for x in (left, right)]
-    edges(st, sc, tmp1, tmp2, f4[...], *near)
-    for k in range(5):
-        send(b_out, a_out, k, st[k, rows(0), :], st[k, rows(C - 1), :], even)
-    for n, pair in enumerate(zip(*outgoing(st, sc, f4[...]))):
-        send(b_out, a_out, 5 + n, *pair, even)
-    base = (5 + len(NEXT)) * R
-    left = squeeze([strip[k, pl.ds(8, 8), :] for k in range(2 * TOP)])
-    right = squeeze([strip[k, pl.ds(16, 8), :] for k in range(2 * TOP)])
-    for n in range(3):
-        b_out[pl.ds(base + 8 * n, 8), :] = jnp.where(even, left[n], right[n])
-        a_out[pl.ds(base + 8 * n, 8), :] = jnp.where(even, right[n], left[n])
+    edge_side(rb, out, st, sc, tmp1, tmp2, strip, f4, True)
+
+
+def chip_edges(*refs):
+    ra, f4 = refs[:2]
+    st, sc, tmp1, tmp2, strip, out = refs[7:]
+    edge_side(ra, out, st, sc, tmp1, tmp2, strip, f4, False)
 
 
 def second_interior(*refs):
@@ -457,11 +522,10 @@
     rb, ra, f4 = refs[:3]
     vel_o, str_o, oce_o, st, sc, tmp1, tmp2, strip, work, stage, sems = refs[8:]
     even = parity() == 0
-    left, right = receive(rb, ra, (*STATE, *[n + "1" for n in NEXT]), even)
+    left, right = receive(rb, ra, SECOND, even)
     for k, name in enumerate(STATE):
         st[k, rows(-1), :], st[k, rows(C), :] = left[name], right[name]
-    near = [{n: x[n + "1"] for n in NEXT} for x in (left, right)]
-    base = (5 + len(NEXT)) * R
+    base = len(SECOND) * R
     pb = [rb[pl.ds(base + 8 * n, 8), :] for n in range(3)]
     pa = [ra[pl.ds(base + 8 * n, 8), :] for n in range(3)]
     low = [jnp.where(even, b, a) for b, a in zip(pb, pa)]
@@ -472,27 +536,27 @@
     step = run_strips(strip, work, f4)
     for _ in range(4):
         step()
-    edges(st, sc, tmp1, tmp2, f4[...], *near)
+    edges(st, sc, tmp1, tmp2, f4[...], next_names(left), next_names(right))
     row, lane = iotas((R, 128))
     top = (row == R - 1) & (lane >= 120)
 
-    for c in range(C):
-        x = [
-            jnp.where(top, work[k, pl.ds(8 + c, 1), :], st[k, rows(c), :]) for k in range(5)
-        ]
-        for w, o in ((U, UO), (V, VO)):
-            d = x[w] - sc[o, rows(c), :]
-            x.append(0.5 * root(d * d + 0.0025) * d)
-        for f, y in enumerate(x):
-            for k in range(4):
-                stage[f, c // 8, pl.ds(8 * k + c % 8, 8, stride=40), :] = y[8 * k : 8 * k + 8]
     whole = stage.reshape(7, 2, 8, 40, 128)
     copies = []
-    for n, (dst, at) in enumerate(((vel_o, 0), (str_o, 2), (oce_o, 5))):
-        src = whole.at[pl.ds(at, dst.shape[0]), :, :, pl.ds(0, 32), :]
-        copies.append(pltpu.make_async_copy(src, dst, sems.at[n]))
-    for c in copies:
-        c.start()
+    for ih in range(2):
+        for c in range(8 * ih, 8 * ih + 8):
+            x = [
+                jnp.where(top, work[k, pl.ds(8 + c, 1), :], st[k, rows(c), :]) for k in range(5)
+            ]
+            for w, o in ((U, UO), (V, VO)):
+                d = x[w] - sc[o, rows(c), :]
+                x.append(0.5 * root(d * d + 0.0025) * d)
+            for f, y in enumerate(x):
+                for k in range(4):
+                    stage[f, ih, pl.ds(8 * k + c % 8, 8, stride=40), :] = y[8 * k : 8 * k + 8]
+        for n, (dst, at) in enumerate(((vel_o, 0), (str_o, 2), (oce_o, 5))):
+            src = whole.at[pl.ds(at, dst.shape[0]), ih, :, pl.ds(0, 32), :]
+            copies.append(pltpu.make_async_copy(src, dst.at[:, ih], sems.at[3 * ih + n]))
+            copies[-1].start()
     for c in copies:
         c.wait()
 
@@ -505,11 +569,14 @@
     return jax.ShapeDtypeStruct(dims, F32)
 
 
-def swap(b, a):
-    n = 128
-    cross = [(d, (d + 1) % n if d % 2 else (d - 1) % n) for d in range(n)]
-    chip = [(d, d ^ 1) for d in range(n)]
-    return lax.ppermute(b, AXES, cross), lax.ppermute(a, AXES, chip)
+def permuted(x, pairs):
+    return lax.ppermute(x, AXES, pairs)
+
+
+N = 128
+CROSS = [(d, (d + 1) % N if d % 2 else (d - 1) % N) for d in range(N)]
+CHIP = [(d, d ^ 1) for d in range(N)]
+MIRROR = [(d, N - 1 - d) for d in range(N)]
 
 
 def coriolis():
@@ -518,15 +585,11 @@
     return (0.125 * np.sin(math.pi * ((j + 0.5) / 4096 - 0.5))).astype(np.float32)
 
 
-def staging():
-    return [
-        pltpu.VMEM((11, *STAGE), F32),
-        pltpu.VMEM((1, *STAGE), jnp.int32),
-        pltpu.SemaphoreType.DMA((6,)),
-    ]
-
-
-def call(kernel, name, out, ins, specs, scratch, alias=None, outs=None, cost=None):
+def edge_scratch():
+    return [pltpu.VMEM((5, NC * R, 128), F32), pltpu.VMEM((9, NC * R, 128), F32)]
+
+
+def call(kernel, out, ins, specs, scratch, alias=None, outs=None, cost=None):
     return pl.pallas_call(
         kernel,
         out_shape=out,
@@ -536,7 +599,6 @@
         input_output_aliases=alias or {},
         compiler_params=pltpu.CompilerParams(vmem_limit_bytes=20 << 20),
         cost_estimate=cost,
-        name=name,
     )(*ins)
 
 
@@ -545,43 +607,69 @@
         pltpu.with_memory_space_constraint(view(x), pltpu.HBM)
         for x in (forcing, ice_state, velocity, stress, ice_mask[None])
     ]
-    n1, n2 = (TOP + len(NEXT)) * R, (5 + len(NEXT)) * R + 24
+    vel, strs, ocean = window(raw)
+    return unview(vel), unview(strs), unview(ocean)
+
+
+def window(raw):
+    n1, n2 = len(FIRST) * R, len(SECOND) * R + 24
     cor = pltpu.with_memory_space_constraint(jnp.asarray(coriolis()), pltpu.HBM)
-    b, a, m, f4 = call(
-        pack_kernel,
-        "pack",
-        [shape(n1, 128), shape(n1, 128), shape(24, 128), shape(R, 128)],
+    cost = pl.CostEstimate(flops=20_000_000, bytes_accessed=4_000_000, transcendentals=500_000)
+    b, m, f4 = call(
+        pack_cross,
+        [shape(n1, 128), shape(24, 128), shape(R, 128)],
         [*raw, cor],
         [HBM] * 6,
-        [pltpu.VMEM((5, NC * R, 128), F32), pltpu.VMEM((9, NC * R, 128), F32), *staging()],
-    )
-    rb, ra = swap(b, a)
-    rm = lax.ppermute(m, AXES, [(d, 127 - d) for d in range(128)])
-    cost = pl.CostEstimate(flops=20_000_000, bytes_accessed=4_000_000, transcendentals=500_000)
+        [
+            *edge_scratch(),
+            pltpu.VMEM((11, 1, *STAGE[1:]), F32),
+            pltpu.VMEM((1, 1, *STAGE[1:]), jnp.int32),
+            pltpu.VMEM((11, 2, 8, 128), F32),
+            pltpu.VMEM((1, 2, 8, 128), jnp.int32),
+            pltpu.SemaphoreType.DMA((11,)),
+        ],
+    )
+    rb = permuted(b, CROSS)
+    rm = permuted(m, MIRROR)
+    a, stage, mstage = call(
+        pack_chip,
+        [
+            shape(n1, 128),
+            shape(11, *STAGE),
+            jax.ShapeDtypeStruct((1, *STAGE), jnp.int32),
+        ],
+        [*raw, f4],
+        [HBM] * 5 + [VM],
+        [*edge_scratch(), pltpu.SemaphoreType.DMA((5,))],
+        cost=cost,
+    )
+    ra = permuted(a, CHIP)
     main = [shape(5, NC * R, 128), shape(9, NC * R, 128), *[shape(6, NC * R, 128)] * 2]
     strips = shape(2 * TOP, R, 128)
     *state, strip = call(
-        first_interior,
-        "interior1",
-        [*main, strips],
-        [*raw, f4],
-        [HBM] * 5 + [VM],
-        staging(),
+        first_interior, [*main, strips], [stage, mstage, f4], [VM] * 3, [], cost=cost
+    )
+    *state, strip, b = call(
+        cross_edges,
+        [*main, strips, shape(n2, 128)],
+        [rb, rm, f4, *state, strip],
+        [VM] * 8,
+        [],
+        alias={3 + k: k for k in range(5)},
+    )
+    rb = permuted(b, CROSS)
+    *state, strip, a = call(
+        chip_edges,
+        [*main, strips, shape(n2, 128)],
+        [ra, f4, *state, strip],
+        [VM] * 7,
+        [],
+        alias={2 + k: k for k in range(5)},
         cost=cost,
     )
-    *state, strip, b, a = call(
-        first_edges,
-        "edges1",
-        [*main, strips, shape(n2, 128), shape(n2, 128)],
-        [rb, ra, rm, f4, *state, strip],
-        [VM] * 9,
-        [],
-        alias={4 + k: k for k in range(5)},
-    )
-    rb, ra = swap(b, a)
+    ra = permuted(a, CHIP)
     state = call(
         second_interior,
-        "interior2",
         main,
         [f4, *state],
         [VM] * 5,
@@ -591,19 +679,18 @@
     )
     vel, strs, ocean, *_ = call(
         second_edges,
-        "edges2",
         [*[shape(n, 2, 8, 32, 128) for n in (2, 3, 2)], *main, strips],
         [rb, ra, f4, *state, strip],
         [VM] * 8,
         [
             pltpu.VMEM((28, R, 128), F32),
             pltpu.VMEM((7, *STAGE), F32),
-            pltpu.SemaphoreType.DMA((3,)),
+            pltpu.SemaphoreType.DMA((6,)),
         ],
         alias={3 + k: 3 + k for k in range(5)},
         outs=[HBM] * 3 + [VM] * 5,
     )
-    return unview(vel), unview(strs), unview(ocean)
+    return vel, strs, ocean
 
 
 def solution(mesh):

time: 34.9 us -> 36.2 us (1.037)
  waiting for transfers between devices: 6.41 us -> 9.66 us
  starting transfers between devices: 13.5 us -> 11.7 us
    ppermute x5, waiting for transfers between devices: 6.41 us -> 9.66 us  [permuted(): return lax.ppermute(x, AXES, pairs)]
    ppermute x5, starting transfers between devices: 13.5 us -> 11.7 us  [permuted(): return lax.ppermute(x, AXES, pairs)]
    pallas_call x5 -> x7, Pallas kernels: 14.2 us -> 13.9 us  [call(): pl.pallas_call(kernel, out_shape=out, in_specs=specs, out_specs=outs or [...]
  transfers between devices with their start and end apart: 5 -> 5, of which waited for: 2 -> 2; matrix products, arithmetic and copies ran while one was open for 0% -> 0% of each run, Pallas kernels for 21% -> 25%
where the time goes in v3:
time: 36.2 us; the launch traced here: 36 us
  Pallas kernels  13.9 us (38%)
  starting transfers between devices  11.7 us (32%)
  waiting for transfers between devices  9.66 us (27%)
  between operations  0.7 us (2%)
    pallas_call x7, Pallas kernels, call(): pl.pallas_call(kernel, out_shape=out, in_specs=specs, out_specs=outs or [...  13.9 us
    ppermute x5, starting transfers between devices, permuted(): return lax.ppermute(x, AXES, pairs)  11.7 us
    ppermute x5, waiting for transfers between devices, permuted(): return lax.ppermute(x, AXES, pairs)  9.66 us
  transfers between devices with their start and end apart: 5, of which 2 were waited for; matrix products, arithmetic and copies ran while one was open for 0% of the time, Pallas kernels for 25%

profile of v3, /device:TPU:0, one launch (start us, length us, event | category | flops | bytes accessed | tf_op | source)
XLA Modules:
  0.0 36.0 jit_solution(17843953715122602573)
XLA Ops:
  0.6 1.8 %shard_map.85 = (f32[544,128]{1,0:T(8,128)S(1)}, f32[24,128]{1,0:T(8,128)S(1)}, f32[32,128]{1,0:T(8,128)S(1)}) custom-call(f32[4,2,8,32,128]{4,3,2,1,0:T(8,128)} %bitcast.40, f32[2,2,8,32,128]{4,3,2,1,0:T(8,128)} %bitcast.44, f32[2,2,8,32,128]{4,3,2,1,0:T(8,128)} %bitcast.46, f32[3,2,8,32,128]{4,3,2,1,0:T(8,128)} %bitcast.42, ...), custom_call_target="tpu_custom_call" | custom-call | tf_op jit(solution)/shard_map/pallas_call | solution.py:593
  2.4 8.3 %collective-permute-start = (f32[544,128]{1,0:T(8,128)S(1)}, f32[544,128]{1,0:T(8,128)S(1)}, u32[]{:S(2)}, u32[]{:S(2)}) collective-permute-start(f32[544,128]{1,0:T(8,128)S(1)} %get-tuple-element.33), channel_id=1, source_target_pairs={{0,127},{1,2},{2,1},{3,4},{4,3},{5,6},{6,5},{7,8},{8,7},{9,10},{10... | collective-permute-start | bytes 835592 | tf_op jit(solution)/shard_map/ppermute | solution.py:573
  10.8 2.1 %shard_map.86 = (f32[544,128]{1,0:T(8,128)S(1)}, f32[11,2,320,128]{3,2,1,0:T(8,128)S(1)}, s32[1,2,320,128]{3,2,1,0:T(8,128)S(1)}) custom-call(f32[4,2,8,32,128]{4,3,2,1,0:T(8,128)} %bitcast.41, f32[2,2,8,32,128]{4,3,2,1,0:T(8,128)} %bitcast.45, f32[2,2,8,32,128]{4,3,2,1,0:T(8,128)} %bitcast.47, f32[3,2,8,32,128]{4,3,2,1,0:T(8,128)} %bitcast.43, ...), custom_call_target="tpu_custom_call" | custom-call | flops 20000000 | bytes 4000000 | tf_op jit(solution)/shard_map/pallas_call | solution.py:593
  12.8 0.1 collective-permute-start.3
  12.9 1.5 %collective-permute-start.1 = (f32[24,128]{1,0:T(8,128)S(1)}, f32[24,128]{1,0:T(8,128)S(1)}, u32[]{:S(2)}, u32[]{:S(2)}) collective-permute-start(f32[24,128]{1,0:T(8,128)S(1)} %get-tuple-element.34), channel_id=1, source_target_pairs={{0,127},{1,126},{2,125},{3,124},{4,123},{5,122},{6,121},{7,120},{8... | collective-permute-start | bytes 36872 | tf_op jit(solution)/shard_map/ppermute | solution.py:573
  14.4 3.0 %shard_map.87 = (f32[5,704,128]{2,1,0:T(8,128)S(1)}, f32[9,704,128]{2,1,0:T(8,128)S(1)}, f32[6,704,128]{2,1,0:T(8,128)S(1)}, f32[6,704,128]{2,1,0:T(8,128)S(1)}, f32[24,32,128]{2,1,0:T(8,128)S(1)}) custom-call(f32[11,2,320,128]{3,2,1,0:T(8,128)S(1)} %get-tuple-element.36.stage, s32[1,2,320,128]{3,2,1,0:T(8,128)S(1)} %get-tuple-element.37.mstage, ...), custom_call_target="tpu_custom_call" | custom-call | flops 20000000 | bytes 4000000 | tf_op jit(solution)/shard_map/pallas_call | solution.py:593
  17.5 4.1 %collective-permute-done.1.refs_1_ = f32[24,128]{1,0:T(8,128)S(1)} collective-permute-done((f32[24,128]{1,0:T(8,128)S(1)}, f32[24,128]{1,0:T(8,128)S(1)}, u32[]{:S(2)}, u32[]{:S(2)}) %collective-permute-start.1) | collective-permute-done | bytes 12320 | tf_op jit(solution)/shard_map/ppermute | solution.py:573
  21.6 0.0 collective-permute-done.refs_0_
  21.6 0.9 %shard_map.88 = (f32[5,704,128]{2,1,0:T(8,128)S(1)}, f32[9,704,128]{2,1,0:T(8,128)S(1)}, f32[6,704,128]{2,1,0:T(8,128)S(1)}, f32[6,704,128]{2,1,0:T(8,128)S(1)},...) custom-call(f32[544,128]{1,0:T(8,128)S(1)} %collective-permute-done., ...), custom_call_target="tpu_custom_call", output_to_operand_aliasing={{0}: (3, {}), {1}: (4, {}), {2}: (5, {}), {3}: (6, {}), {4}... | custom-call | tf_op jit(solution)/shard_map/pallas_call | solution.py:593
  22.4 1.7 %collective-permute-start.2 = (f32[344,128]{1,0:T(8,128)S(1)}, f32[344,128]{1,0:T(8,128)S(1)}, u32[]{:S(2)}, u32[]{:S(2)}) collective-permute-start(f32[344,128]{1,0:T(8,128)S(1)} %get-tuple-element.43), channel_id=1, source_target_pairs={{0,127},{1,2},{2,1},{3,4},{4,3},{5,6},{6,5},{7,8},{8,7},{9,10},{10... | collective-permute-start | bytes 528392 | tf_op jit(solution)/shard_map/ppermute | solution.py:573
  24.2 0.0 collective-permute-done.3.refs_0_
  24.2 0.7 %shard_map.89 = (f32[5,704,128]{2,1,0:T(8,128)S(1)}, f32[9,704,128]{2,1,0:T(8,128)S(1)}, f32[6,704,128]{2,1,0:T(8,128)S(1)}, f32[6,704,128]{2,1,0:T(8,128)S(1)},...) custom-call(f32[544,128]{1,0:T(8,128)S(1)} %collective-permute-done., ...), custom_call_target="tpu_custom_call", output_to_operand_aliasing={{0}: (2, {}), {1}: (3, {}), {2}: (4, {}), {3}: (5, {}), {4}... | custom-call | flops 20000000 | bytes 4000000 | tf_op jit(solution)/shard_map/pallas_call | solution.py:593
  24.9 0.1 collective-permute-start.4
  25.0 2.2 %shard_map.90 = (f32[5,704,128]{2,1,0:T(8,128)S(1)}, f32[9,704,128]{2,1,0:T(8,128)S(1)}, f32[6,704,128]{2,1,0:T(8,128)S(1)}, f32[6,704,128]{2,1,0:T(8,128)S(1)}) custom-call(f32[32,128]{1,0:T(8,128)S(1)} %get-tuple-element.35.f4.refs_2_.refs_1_.refs_0_, ...), custom_call_target="tpu_custom_call", output_to_operand_aliasing={{0}: (1, {}), {1}: (2, {}), {2}: (3, {}), {3}: (4, {})} | custom-call | flops 20000000 | bytes 4000000 | tf_op jit(solution)/shard_map/pallas_call | solution.py:593
  27.3 5.6 %collective-permute-done.2.refs_0_ = f32[344,128]{1,0:T(8,128)S(1)} collective-permute-done((f32[344,128]{1,0:T(8,128)S(1)}, f32[344,128]{1,0:T(8,128)S(1)}, u32[]{:S(2)}, u32[]{:S(2)}) %collective-permute-start.2) | collective-permute-done | bytes 176160 | tf_op jit(solution)/shard_map/ppermute | solution.py:573
  32.8 0.0 collective-permute-done.4.refs_1_
  32.8 3.2 %shard_map.91 = (f32[2,2,8,32,128]{4,3,2,1,0:T(8,128)}, f32[3,2,8,32,128]{4,3,2,1,0:T(8,128)}, f32[2,2,8,32,128]{4,3,2,1,0:T(8,128)}, f32[5,704,128]{2,1,0:T(8,1...) custom-call(f32[344,128]{1,0:T(8,128)S(1)} %collective-permute-done., ...), custom_call_target="tpu_custom_call", output_to_operand_aliasing={{3}: (3, {}), {4}: (4, {}), {5}: (5, {}), {6}: (6, {}), {7}... | custom-call | tf_op jit(solution)/shard_map/pallas_call | solution.py:593
Async XLA Ops:
  2.4 19.1 %collective-permute-start = (f32[544,128]{1,0:T(8,128)S(1)}, f32[544,128]{1,0:T(8,128)S(1)}, u32[]{:S(2)}, u32[]{:S(2)}) collective-permute-start(f32[544,128]{1,0:T(8,128)S(1)} %get-tuple-element.33), channel_id=1, source_target_pairs={{0,127},{1,2},{2,1},{3,4},{4,3},{5,6},{6,5},{7,8},{8,7},{9,10},{10... | collective-permute-start | bytes 835592 | tf_op jit(solution)/shard_map/ppermute | solution.py:573
  12.8 11.3 %collective-permute-start.3 = (f32[544,128]{1,0:T(8,128)S(1)}, f32[544,128]{1,0:T(8,128)S(1)}, u32[]{:S(2)}, u32[]{:S(2)}) collective-permute-start(f32[544,128]{1,0:T(8,128)S(1)} %get-tuple-element.44), channel_id=1, source_target_pairs={{0,1},{1,0},{2,3},{3,2},{4,5},{5,4},{6,7},{7,6},{8,9},{9,8},{10,11... | collective-permute-start | bytes 835592 | tf_op jit(solution)/shard_map/ppermute | solution.py:573
  12.9 8.6 %collective-permute-start.1 = (f32[24,128]{1,0:T(8,128)S(1)}, f32[24,128]{1,0:T(8,128)S(1)}, u32[]{:S(2)}, u32[]{:S(2)}) collective-permute-start(f32[24,128]{1,0:T(8,128)S(1)} %get-tuple-element.34), channel_id=1, source_target_pairs={{0,127},{1,126},{2,125},{3,124},{4,123},{5,122},{6,121},{7,120},{8... | collective-permute-start | bytes 36872 | tf_op jit(solution)/shard_map/ppermute | solution.py:573
  22.4 10.4 %collective-permute-start.2 = (f32[344,128]{1,0:T(8,128)S(1)}, f32[344,128]{1,0:T(8,128)S(1)}, u32[]{:S(2)}, u32[]{:S(2)}) collective-permute-start(f32[344,128]{1,0:T(8,128)S(1)} %get-tuple-element.43), channel_id=1, source_target_pairs={{0,127},{1,2},{2,1},{3,4},{4,3},{5,6},{6,5},{7,8},{8,7},{9,10},{10... | collective-permute-start | bytes 528392 | tf_op jit(solution)/shard_map/ppermute | solution.py:573
  24.9 7.9 %collective-permute-start.4 = (f32[344,128]{1,0:T(8,128)S(1)}, f32[344,128]{1,0:T(8,128)S(1)}, u32[]{:S(2)}, u32[]{:S(2)}) collective-permute-start(f32[344,128]{1,0:T(8,128)S(1)} %get-tuple-element.50), channel_id=1, source_target_pairs={{0,1},{1,0},{2,3},{3,2},{4,5},{5,4},{6,7},{7,6},{8,9},{9,8},{10,11... | collective-permute-start | bytes 528392 | tf_op jit(solution)/shard_map/ppermute | solution.py:573

commit v4 on v3

--- a/solution.py
+++ b/solution.py
@@ -451,9 +451,21 @@
     edge_side(ra, out, st, sc, tmp1, tmp2, strip, f4, False)
 
 
+def stage_out(st, sc, out, cols):
+    for c in cols:
+        x = [st[k, rows(c), :] for k in range(5)]
+        for w, o in ((U, UO), (V, VO)):
+            d = x[w] - sc[o, rows(c), :]
+            x.append(0.5 * root(d * d + 0.0025) * d)
+        for f, y in enumerate(x):
+            for k in range(4):
+                out[f, c // 8, pl.ds(8 * k + c % 8, 8, stride=40), :] = y[8 * k : 8 * k + 8]
+
+
 def second_interior(*refs):
-    f4, (st, sc, tmp1, tmp2) = refs[0], refs[5:]
+    f4, (st, sc, tmp1, tmp2, out) = refs[0], refs[5:]
     interior(st, sc, tmp1, tmp2, f4[...])
+    stage_out(st, sc, out, range(4, 12))
 
 
 def run_strips(strip, work, cor4):
@@ -520,11 +532,25 @@
 
 def second_edges(*refs):
     rb, ra, f4 = refs[:3]
-    vel_o, str_o, oce_o, st, sc, tmp1, tmp2, strip, work, stage, sems = refs[8:]
+    vel_o, str_o, oce_o, st, sc, tmp1, tmp2, strip, out, work, sems = refs[9:]
     even = parity() == 0
     left, right = receive(rb, ra, SECOND, even)
     for k, name in enumerate(STATE):
         st[k, rows(-1), :], st[k, rows(C), :] = left[name], right[name]
+    edges(st, sc, tmp1, tmp2, f4[...], next_names(left), next_names(right))
+    whole = out.reshape(7, 2, 8, 40, 128)
+    copies = []
+
+    def start(ih, at):
+        for dst, f in ((vel_o, 0), (str_o, 2), (oce_o, 5)):
+            src = whole.at[pl.ds(f, dst.shape[0]), ih, at, pl.ds(0, 32), :]
+            sem = sems.at[len(copies)]
+            copies.append(pltpu.make_async_copy(src, dst.at[:, ih, at], sem))
+            copies[-1].start()
+
+    for ih, cols in enumerate((range(4), range(12, 16))):
+        stage_out(st, sc, out, cols)
+        start(ih, pl.ds(0, 7))
     base = len(SECOND) * R
     pb = [rb[pl.ds(base + 8 * n, 8), :] for n in range(3)]
     pa = [ra[pl.ds(base + 8 * n, 8), :] for n in range(3)]
@@ -536,27 +562,17 @@
     step = run_strips(strip, work, f4)
     for _ in range(4):
         step()
-    edges(st, sc, tmp1, tmp2, f4[...], next_names(left), next_names(right))
-    row, lane = iotas((R, 128))
-    top = (row == R - 1) & (lane >= 120)
-
-    whole = stage.reshape(7, 2, 8, 40, 128)
-    copies = []
+    top = iotas((8, 128))[1] >= 120
     for ih in range(2):
-        for c in range(8 * ih, 8 * ih + 8):
-            x = [
-                jnp.where(top, work[k, pl.ds(8 + c, 1), :], st[k, rows(c), :]) for k in range(5)
-            ]
-            for w, o in ((U, UO), (V, VO)):
-                d = x[w] - sc[o, rows(c), :]
-                x.append(0.5 * root(d * d + 0.0025) * d)
-            for f, y in enumerate(x):
-                for k in range(4):
-                    stage[f, ih, pl.ds(8 * k + c % 8, 8, stride=40), :] = y[8 * k : 8 * k + 8]
-        for n, (dst, at) in enumerate(((vel_o, 0), (str_o, 2), (oce_o, 5))):
-            src = whole.at[pl.ds(at, dst.shape[0]), ih, :, pl.ds(0, 32), :]
-            copies.append(pltpu.make_async_copy(src, dst.at[:, ih], sems.at[3 * ih + n]))
-            copies[-1].start()
+        mine = pl.ds(8 + 8 * ih, 8)
+        x = [work[k, mine, :] for k in range(5)]
+        for w, o in ((U, UO), (V, VO)):
+            d = x[w] - work[10 + o, mine, :]
+            x.append(0.5 * root(d * d + 0.0025) * d)
+        tile = pl.ds(7 * 40 + 24, 8)
+        for f, y in enumerate(x):
+            out[f, ih, tile, :] = jnp.where(top, y, out[f, ih, tile, :])
+        start(ih, pl.ds(7, 1))
     for c in copies:
         c.wait()
 
@@ -668,9 +684,9 @@
         cost=cost,
     )
     ra = permuted(a, CHIP)
-    state = call(
+    *state, out = call(
         second_interior,
-        main,
+        [*main, shape(7, *STAGE)],
         [f4, *state],
         [VM] * 5,
         [],
@@ -679,16 +695,12 @@
     )
     vel, strs, ocean, *_ = call(
         second_edges,
-        [*[shape(n, 2, 8, 32, 128) for n in (2, 3, 2)], *main, strips],
-        [rb, ra, f4, *state, strip],
-        [VM] * 8,
-        [
-            pltpu.VMEM((28, R, 128), F32),
-            pltpu.VMEM((7, *STAGE), F32),
-            pltpu.SemaphoreType.DMA((6,)),
-        ],
-        alias={3 + k: 3 + k for k in range(5)},
-        outs=[HBM] * 3 + [VM] * 5,
+        [*[shape(n, 2, 8, 32, 128) for n in (2, 3, 2)], *main, strips, shape(7, *STAGE)],
+        [rb, ra, f4, *state, strip, out],
+        [VM] * 9,
+        [pltpu.VMEM((28, R, 128), F32), pltpu.SemaphoreType.DMA((12,))],
+        alias={3 + k: 3 + k for k in range(6)},
+        outs=[HBM] * 3 + [VM] * 6,
     )
     return vel, strs, ocean
 

time: 36.2 us -> 35.8 us (0.989)
  transfers between devices with their start and end apart: 5 -> 5, of which waited for: 2 -> 2; matrix products, arithmetic and copies ran while one was open for 0% -> 0% of each run, Pallas kernels for 25% -> 26%
where the time goes in v4:
time: 35.8 us; the launch traced here: 35.6 us
  Pallas kernels  13.7 us (38%)
  starting transfers between devices  11.7 us (33%)
  waiting for transfers between devices  9.53 us (27%)
  between operations  0.7 us (2%)
    pallas_call x7, Pallas kernels, call(): pl.pallas_call(kernel, out_shape=out, in_specs=specs, out_specs=outs or [...  13.7 us
    ppermute x5, starting transfers between devices, permuted(): return lax.ppermute(x, AXES, pairs)  11.7 us
    ppermute x5, waiting for transfers between devices, permuted(): return lax.ppermute(x, AXES, pairs)  9.53 us
  transfers between devices with their start and end apart: 5, of which 2 were waited for; matrix products, arithmetic and copies ran while one was open for 0% of the time, Pallas kernels for 26%

profile of v4, /device:TPU:0, one launch (start us, length us, event | category | flops | bytes accessed | tf_op | source)
XLA Modules:
  0.0 35.6 jit_solution(12564831787030860261)
XLA Ops:
  0.6 1.8 %shard_map.85 = (f32[544,128]{1,0:T(8,128)S(1)}, f32[24,128]{1,0:T(8,128)S(1)}, f32[32,128]{1,0:T(8,128)S(1)}) custom-call(f32[4,2,8,32,128]{4,3,2,1,0:T(8,128)} %bitcast.40, f32[2,2,8,32,128]{4,3,2,1,0:T(8,128)} %bitcast.44, f32[2,2,8,32,128]{4,3,2,1,0:T(8,128)} %bitcast.46, f32[3,2,8,32,128]{4,3,2,1,0:T(8,128)} %bitcast.42, ...), custom_call_target="tpu_custom_call" | custom-call | tf_op jit(solution)/shard_map/pallas_call | solution.py:609
  2.4 8.3 %collective-permute-start = (f32[544,128]{1,0:T(8,128)S(1)}, f32[544,128]{1,0:T(8,128)S(1)}, u32[]{:S(2)}, u32[]{:S(2)}) collective-permute-start(f32[544,128]{1,0:T(8,128)S(1)} %get-tuple-element.34), channel_id=1, source_target_pairs={{0,127},{1,2},{2,1},{3,4},{4,3},{5,6},{6,5},{7,8},{8,7},{9,10},{10... | collective-permute-start | bytes 835592 | tf_op jit(solution)/shard_map/ppermute | solution.py:589
  10.8 2.1 %shard_map.86 = (f32[544,128]{1,0:T(8,128)S(1)}, f32[11,2,320,128]{3,2,1,0:T(8,128)S(1)}, s32[1,2,320,128]{3,2,1,0:T(8,128)S(1)}) custom-call(f32[4,2,8,32,128]{4,3,2,1,0:T(8,128)} %bitcast.41, f32[2,2,8,32,128]{4,3,2,1,0:T(8,128)} %bitcast.45, f32[2,2,8,32,128]{4,3,2,1,0:T(8,128)} %bitcast.47, f32[3,2,8,32,128]{4,3,2,1,0:T(8,128)} %bitcast.43, ...), custom_call_target="tpu_custom_call" | custom-call | flops 20000000 | bytes 4000000 | tf_op jit(solution)/shard_map/pallas_call | solution.py:609
  12.8 0.1 collective-permute-start.3
  12.9 1.5 %collective-permute-start.1 = (f32[24,128]{1,0:T(8,128)S(1)}, f32[24,128]{1,0:T(8,128)S(1)}, u32[]{:S(2)}, u32[]{:S(2)}) collective-permute-start(f32[24,128]{1,0:T(8,128)S(1)} %get-tuple-element.35), channel_id=1, source_target_pairs={{0,127},{1,126},{2,125},{3,124},{4,123},{5,122},{6,121},{7,120},{8... | collective-permute-start | bytes 36872 | tf_op jit(solution)/shard_map/ppermute | solution.py:589
  14.4 3.0 %shard_map.87 = (f32[5,704,128]{2,1,0:T(8,128)S(1)}, f32[9,704,128]{2,1,0:T(8,128)S(1)}, f32[6,704,128]{2,1,0:T(8,128)S(1)}, f32[6,704,128]{2,1,0:T(8,128)S(1)}, f32[24,32,128]{2,1,0:T(8,128)S(1)}) custom-call(f32[11,2,320,128]{3,2,1,0:T(8,128)S(1)} %get-tuple-element.37.stage, s32[1,2,320,128]{3,2,1,0:T(8,128)S(1)} %get-tuple-element.38.mstage, ...), custom_call_target="tpu_custom_call" | custom-call | flops 20000000 | bytes 4000000 | tf_op jit(solution)/shard_map/pallas_call | solution.py:609
  17.4 4.1 %collective-permute-done.1.refs_1_ = f32[24,128]{1,0:T(8,128)S(1)} collective-permute-done((f32[24,128]{1,0:T(8,128)S(1)}, f32[24,128]{1,0:T(8,128)S(1)}, u32[]{:S(2)}, u32[]{:S(2)}) %collective-permute-start.1) | collective-permute-done | bytes 12320 | tf_op jit(solution)/shard_map/ppermute | solution.py:589
  21.6 0.0 collective-permute-done.refs_0_
  21.6 0.8 %shard_map.88 = (f32[5,704,128]{2,1,0:T(8,128)S(1)}, f32[9,704,128]{2,1,0:T(8,128)S(1)}, f32[6,704,128]{2,1,0:T(8,128)S(1)}, f32[6,704,128]{2,1,0:T(8,128)S(1)},...) custom-call(f32[544,128]{1,0:T(8,128)S(1)} %collective-permute-done., ...), custom_call_target="tpu_custom_call", output_to_operand_aliasing={{0}: (3, {}), {1}: (4, {}), {2}: (5, {}), {3}: (6, {}), {4}... | custom-call | tf_op jit(solution)/shard_map/pallas_call | solution.py:609
  22.4 1.7 %collective-permute-start.2 = (f32[344,128]{1,0:T(8,128)S(1)}, f32[344,128]{1,0:T(8,128)S(1)}, u32[]{:S(2)}, u32[]{:S(2)}) collective-permute-start(f32[344,128]{1,0:T(8,128)S(1)} %get-tuple-element.44), channel_id=1, source_target_pairs={{0,127},{1,2},{2,1},{3,4},{4,3},{5,6},{6,5},{7,8},{8,7},{9,10},{10... | collective-permute-start | bytes 528392 | tf_op jit(solution)/shard_map/ppermute | solution.py:589
  24.1 0.0 collective-permute-done.3.refs_0_
  24.1 0.7 %shard_map.89 = (f32[5,704,128]{2,1,0:T(8,128)S(1)}, f32[9,704,128]{2,1,0:T(8,128)S(1)}, f32[6,704,128]{2,1,0:T(8,128)S(1)}, f32[6,704,128]{2,1,0:T(8,128)S(1)},...) custom-call(f32[544,128]{1,0:T(8,128)S(1)} %collective-permute-done., ...), custom_call_target="tpu_custom_call", output_to_operand_aliasing={{0}: (2, {}), {1}: (3, {}), {2}: (4, {}), {3}: (5, {}), {4}... | custom-call | flops 20000000 | bytes 4000000 | tf_op jit(solution)/shard_map/pallas_call | solution.py:609
  24.9 0.1 collective-permute-start.4
  24.9 2.5 %shard_map.90 = (f32[5,704,128]{2,1,0:T(8,128)S(1)}, f32[9,704,128]{2,1,0:T(8,128)S(1)}, f32[6,704,128]{2,1,0:T(8,128)S(1)}, f32[6,704,128]{2,1,0:T(8,128)S(1)}, f32[7,2,320,128]{3,2,1,0:T(8,128)S(1)}) custom-call(f32[32,128]{1,0:T(8,128)S(1)} %get-tuple-element.36.f4.refs_2_.refs_1_.refs_0_,, ...), custom_call_target="tpu_custom_call", output_to_operand_aliasing={{0}: (1, {}), {1}: (2, {}), {2}: (3, {}), {3}: (4, {})} | custom-call | flops 20000000 | bytes 4000000 | tf_op jit(solution)/shard_map/pallas_call | solution.py:609
  27.4 5.4 %collective-permute-done.2.refs_0_ = f32[344,128]{1,0:T(8,128)S(1)} collective-permute-done((f32[344,128]{1,0:T(8,128)S(1)}, f32[344,128]{1,0:T(8,128)S(1)}, u32[]{:S(2)}, u32[]{:S(2)}) %collective-permute-start.2) | collective-permute-done | bytes 176160 | tf_op jit(solution)/shard_map/ppermute | solution.py:589
  32.8 0.0 collective-permute-done.4.refs_1_
  32.8 2.8 %shard_map.91 = (f32[2,2,8,32,128]{4,3,2,1,0:T(8,128)}, f32[3,2,8,32,128]{4,3,2,1,0:T(8,128)}, f32[2,2,8,32,128]{4,3,2,1,0:T(8,128)}, f32[5,704,128]{2,1,0:T(8,1...) custom-call(f32[344,128]{1,0:T(8,128)S(1)} %collective-permute-done., ...), custom_call_target="tpu_custom_call", output_to_operand_aliasing={{3}: (3, {}), {4}: (4, {}), {5}: (5, {}), {6}: (6, {}), {7}... | custom-call | tf_op jit(solution)/shard_map/pallas_call | solution.py:609
Async XLA Ops:
  2.4 19.1 %collective-permute-start = (f32[544,128]{1,0:T(8,128)S(1)}, f32[544,128]{1,0:T(8,128)S(1)}, u32[]{:S(2)}, u32[]{:S(2)}) collective-permute-start(f32[544,128]{1,0:T(8,128)S(1)} %get-tuple-element.34), channel_id=1, source_target_pairs={{0,127},{1,2},{2,1},{3,4},{4,3},{5,6},{6,5},{7,8},{8,7},{9,10},{10... | collective-permute-start | bytes 835592 | tf_op jit(solution)/shard_map/ppermute | solution.py:589
  12.8 11.3 %collective-permute-start.3 = (f32[544,128]{1,0:T(8,128)S(1)}, f32[544,128]{1,0:T(8,128)S(1)}, u32[]{:S(2)}, u32[]{:S(2)}) collective-permute-start(f32[544,128]{1,0:T(8,128)S(1)} %get-tuple-element.45), channel_id=1, source_target_pairs={{0,1},{1,0},{2,3},{3,2},{4,5},{5,4},{6,7},{7,6},{8,9},{9,8},{10,11... | collective-permute-start | bytes 835592 | tf_op jit(solution)/shard_map/ppermute | solution.py:589
  12.9 8.6 %collective-permute-start.1 = (f32[24,128]{1,0:T(8,128)S(1)}, f32[24,128]{1,0:T(8,128)S(1)}, u32[]{:S(2)}, u32[]{:S(2)}) collective-permute-start(f32[24,128]{1,0:T(8,128)S(1)} %get-tuple-element.35), channel_id=1, source_target_pairs={{0,127},{1,126},{2,125},{3,124},{4,123},{5,122},{6,121},{7,120},{8... | collective-permute-start | bytes 36872 | tf_op jit(solution)/shard_map/ppermute | solution.py:589
  22.4 10.4 %collective-permute-start.2 = (f32[344,128]{1,0:T(8,128)S(1)}, f32[344,128]{1,0:T(8,128)S(1)}, u32[]{:S(2)}, u32[]{:S(2)}) collective-permute-start(f32[344,128]{1,0:T(8,128)S(1)} %get-tuple-element.44), channel_id=1, source_target_pairs={{0,127},{1,2},{2,1},{3,4},{4,3},{5,6},{6,5},{7,8},{8,7},{9,10},{10... | collective-permute-start | bytes 528392 | tf_op jit(solution)/shard_map/ppermute | solution.py:589
  24.9 8.0 %collective-permute-start.4 = (f32[344,128]{1,0:T(8,128)S(1)}, f32[344,128]{1,0:T(8,128)S(1)}, u32[]{:S(2)}, u32[]{:S(2)}) collective-permute-start(f32[344,128]{1,0:T(8,128)S(1)} %get-tuple-element.51), channel_id=1, source_target_pairs={{0,1},{1,0},{2,3},{3,2},{4,5},{5,4},{6,7},{7,6},{8,9},{9,8},{10,11... | collective-permute-start | bytes 528392 | tf_op jit(solution)/shard_map/ppermute | solution.py:589

commit v5 on v4

--- a/solution.py
+++ b/solution.py
@@ -373,14 +373,16 @@
     def body(side):
         main = [pltpu.make_async_copy(cor, f4, sems.at[5])]
         tops = []
+        il = pl.ds(5 if side else 0, 3)
         at = 0
         for k, src in enumerate(srcs):
             n = src.shape[0]
             if k < 4:
-                dst = stage.reshape(11, 1, 8, 40, 128).at[pl.ds(at, n), 0, :, pl.ds(0, 32), :]
+                dst = stage.reshape(11, 8, 5, 8, 128).at[pl.ds(at, n), :, pl.ds(0, 4), il, :]
             else:
-                dst = mstage.reshape(1, 1, 8, 40, 128).at[:, 0, :, pl.ds(0, 32), :]
-            main.append(pltpu.make_async_copy(src.at[:, side], dst, sems.at[k]))
+                dst = mstage.reshape(1, 8, 5, 8, 128).at[:, :, pl.ds(0, 4), il, :]
+            part = src.reshape(n, 2, 8, 4, 8, 128).at[:, side, :, :, il, :]
+            main.append(pltpu.make_async_copy(part, dst, sems.at[k]))
             dst = top.at[pl.ds(at, n)] if k < 4 else mtop
             tile = src.at[:, :, 7, pl.ds(24, 8), :]
             tops.append(pltpu.make_async_copy(tile, dst, sems.at[6 + k]))
@@ -399,6 +401,7 @@
         ]
         for n, x in enumerate(squeeze(tiles)):
             m_out[pl.ds(8 * n, 8), :] = x
+            b_out[pl.ds(len(FIRST) * R + 8 * n, 8), :] = x
 
     by_side(True, body)
 
@@ -437,7 +440,12 @@
     rb, rm, f4 = refs[:3]
     st, sc, tmp1, tmp2, strip, out = refs[8:]
     flip = 7 - iotas((8, 128))[0]
-    packed = [rm[pl.ds(8 * n, 8), :] for n in range(3)]
+    slab = lax.axis_index("gx") * lax.axis_size("gy") + lax.axis_index("gy")
+    paired = (slab == 0) | (slab == N - 1) | (slab == N // 2 - 1) | (slab == N // 2)
+    packed = [
+        jnp.where(paired, rb[pl.ds(len(FIRST) * R + 8 * n, 8), :], rm[pl.ds(8 * n, 8), :])
+        for n in range(3)
+    ]
     for k in range(TOP):
         for ih in range(2):
             x = spread(packed, 2 * k + ih)
@@ -592,7 +600,7 @@
 N = 128
 CROSS = [(d, (d + 1) % N if d % 2 else (d - 1) % N) for d in range(N)]
 CHIP = [(d, d ^ 1) for d in range(N)]
-MIRROR = [(d, N - 1 - d) for d in range(N)]
+MIRROR = [(d, (d + N // 2) % N if (d, N - 1 - d) in CROSS else N - 1 - d) for d in range(N)]
 
 
 def coriolis():
@@ -633,7 +641,7 @@
     cost = pl.CostEstimate(flops=20_000_000, bytes_accessed=4_000_000, transcendentals=500_000)
     b, m, f4 = call(
         pack_cross,
-        [shape(n1, 128), shape(24, 128), shape(R, 128)],
+        [shape(n1 + 24, 128), shape(24, 128), shape(R, 128)],
         [*raw, cor],
         [HBM] * 6,
         [

time: 35.8 us -> 34.6 us (0.966)
  waiting for transfers between devices: 9.53 us -> 8.07 us
  starting transfers between devices: 11.7 us -> 12.2 us
    ppermute x5, waiting for transfers between devices: 9.53 us -> 8.07 us  [permuted(): return lax.ppermute(x, AXES, pairs)]
    ppermute x5, starting transfers between devices: 11.7 us -> 12.2 us  [permuted(): return lax.ppermute(x, AXES, pairs)]
where the time goes in v5:
time: 34.6 us; the launch traced here: 34.5 us
  Pallas kernels  13.5 us (39%)
  starting transfers between devices  12.2 us (35%)
  waiting for transfers between devices  8.07 us (23%)
  between operations  0.7 us (2%)
    pallas_call x7, Pallas kernels, call(): pl.pallas_call(kernel, out_shape=out, in_specs=specs, out_specs=outs or [...  13.5 us
    ppermute x5, starting transfers between devices, permuted(): return lax.ppermute(x, AXES, pairs)  12.2 us
    ppermute x5, waiting for transfers between devices, permuted(): return lax.ppermute(x, AXES, pairs)  8.07 us
  transfers between devices with their start and end apart: 5, of which 2 were waited for; matrix products, arithmetic and copies ran while one was open for 0% of the time, Pallas kernels for 26%

profile of v5, /device:TPU:0, one launch (start us, length us, event | category | flops | bytes accessed | tf_op | source)
XLA Modules:
  0.0 34.5 jit_solution(10921280343875149937)
XLA Ops:
  0.6 1.6 %shard_map.85 = (f32[568,128]{1,0:T(8,128)S(1)}, f32[24,128]{1,0:T(8,128)S(1)}, f32[32,128]{1,0:T(8,128)S(1)}) custom-call(f32[4,2,8,32,128]{4,3,2,1,0:T(8,128)} %bitcast.40, f32[2,2,8,32,128]{4,3,2,1,0:T(8,128)} %bitcast.44, f32[2,2,8,32,128]{4,3,2,1,0:T(8,128)} %bitcast.46, f32[3,2,8,32,128]{4,3,2,1,0:T(8,128)} %bitcast.42, ...), custom_call_target="tpu_custom_call" | custom-call | tf_op jit(solution)/shard_map/pallas_call | solution.py:617
  2.2 8.3 %collective-permute-start = (f32[568,128]{1,0:T(8,128)S(1)}, f32[568,128]{1,0:T(8,128)S(1)}, u32[]{:S(2)}, u32[]{:S(2)}) collective-permute-start(f32[568,128]{1,0:T(8,128)S(1)} %get-tuple-element.34), channel_id=1, source_target_pairs={{0,127},{1,2},{2,1},{3,4},{4,3},{5,6},{6,5},{7,8},{8,7},{9,10},{10... | collective-permute-start | bytes 872456 | tf_op jit(solution)/shard_map/ppermute | solution.py:597
  10.5 2.1 %shard_map.86 = (f32[544,128]{1,0:T(8,128)S(1)}, f32[11,2,320,128]{3,2,1,0:T(8,128)S(1)}, s32[1,2,320,128]{3,2,1,0:T(8,128)S(1)}) custom-call(f32[4,2,8,32,128]{4,3,2,1,0:T(8,128)} %bitcast.41, f32[2,2,8,32,128]{4,3,2,1,0:T(8,128)} %bitcast.45, f32[2,2,8,32,128]{4,3,2,1,0:T(8,128)} %bitcast.47, f32[3,2,8,32,128]{4,3,2,1,0:T(8,128)} %bitcast.43, ...), custom_call_target="tpu_custom_call" | custom-call | flops 20000000 | bytes 4000000 | tf_op jit(solution)/shard_map/pallas_call | solution.py:617
  12.6 0.1 collective-permute-start.3
  12.7 0.1 collective-permute-start.1
  12.8 3.0 %shard_map.87 = (f32[5,704,128]{2,1,0:T(8,128)S(1)}, f32[9,704,128]{2,1,0:T(8,128)S(1)}, f32[6,704,128]{2,1,0:T(8,128)S(1)}, f32[6,704,128]{2,1,0:T(8,128)S(1)}, f32[24,32,128]{2,1,0:T(8,128)S(1)}) custom-call(f32[11,2,320,128]{3,2,1,0:T(8,128)S(1)} %get-tuple-element.37.stage, s32[1,2,320,128]{3,2,1,0:T(8,128)S(1)} %get-tuple-element.38.mstage, ...), custom_call_target="tpu_custom_call" | custom-call | flops 20000000 | bytes 4000000 | tf_op jit(solution)/shard_map/pallas_call | solution.py:617
  15.8 3.1 %collective-permute-done.1.refs_1_ = f32[24,128]{1,0:T(8,128)S(1)} collective-permute-done((f32[24,128]{1,0:T(8,128)S(1)}, f32[24,128]{1,0:T(8,128)S(1)}, u32[]{:S(2)}, u32[]{:S(2)}) %collective-permute-start.1) | collective-permute-done | bytes 12320 | tf_op jit(solution)/shard_map/ppermute | solution.py:597
  18.9 0.0 collective-permute-done.refs_0_
  18.9 0.8 %shard_map.88 = (f32[5,704,128]{2,1,0:T(8,128)S(1)}, f32[9,704,128]{2,1,0:T(8,128)S(1)}, f32[6,704,128]{2,1,0:T(8,128)S(1)}, f32[6,704,128]{2,1,0:T(8,128)S(1)},...) custom-call(f32[568,128]{1,0:T(8,128)S(1)} %collective-permute-done., ...), custom_call_target="tpu_custom_call", output_to_operand_aliasing={{0}: (3, {}), {1}: (4, {}), {2}: (5, {}), {3}: (6, {}), {4}... | custom-call | tf_op jit(solution)/shard_map/pallas_call | solution.py:617
  19.7 3.6 %collective-permute-start.2 = (f32[344,128]{1,0:T(8,128)S(1)}, f32[344,128]{1,0:T(8,128)S(1)}, u32[]{:S(2)}, u32[]{:S(2)}) collective-permute-start(f32[344,128]{1,0:T(8,128)S(1)} %get-tuple-element.44), channel_id=1, source_target_pairs={{0,127},{1,2},{2,1},{3,4},{4,3},{5,6},{6,5},{7,8},{8,7},{9,10},{10... | collective-permute-start | bytes 528392 | tf_op jit(solution)/shard_map/ppermute | solution.py:597
  23.3 0.0 collective-permute-done.3.refs_0_
  23.3 0.7 %shard_map.89 = (f32[5,704,128]{2,1,0:T(8,128)S(1)}, f32[9,704,128]{2,1,0:T(8,128)S(1)}, f32[6,704,128]{2,1,0:T(8,128)S(1)}, f32[6,704,128]{2,1,0:T(8,128)S(1)},...) custom-call(f32[544,128]{1,0:T(8,128)S(1)} %collective-permute-done., ...), custom_call_target="tpu_custom_call", output_to_operand_aliasing={{0}: (2, {}), {1}: (3, {}), {2}: (4, {}), {3}: (5, {}), {4}... | custom-call | flops 20000000 | bytes 4000000 | tf_op jit(solution)/shard_map/pallas_call | solution.py:617
  24.0 0.1 collective-permute-start.4
  24.2 2.4 %shard_map.90 = (f32[5,704,128]{2,1,0:T(8,128)S(1)}, f32[9,704,128]{2,1,0:T(8,128)S(1)}, f32[6,704,128]{2,1,0:T(8,128)S(1)}, f32[6,704,128]{2,1,0:T(8,128)S(1)}, f32[7,2,320,128]{3,2,1,0:T(8,128)S(1)}) custom-call(f32[32,128]{1,0:T(8,128)S(1)} %get-tuple-element.36.f4.refs_2_.refs_1_.refs_0_,, ...), custom_call_target="tpu_custom_call", output_to_operand_aliasing={{0}: (1, {}), {1}: (2, {}), {2}: (3, {}), {3}: (4, {})} | custom-call | flops 20000000 | bytes 4000000 | tf_op jit(solution)/shard_map/pallas_call | solution.py:617
  26.6 5.0 %collective-permute-done.2.refs_0_ = f32[344,128]{1,0:T(8,128)S(1)} collective-permute-done((f32[344,128]{1,0:T(8,128)S(1)}, f32[344,128]{1,0:T(8,128)S(1)}, u32[]{:S(2)}, u32[]{:S(2)}) %collective-permute-start.2) | collective-permute-done | bytes 176160 | tf_op jit(solution)/shard_map/ppermute | solution.py:597
  31.6 0.0 collective-permute-done.4.refs_1_
  31.6 2.8 %shard_map.91 = (f32[2,2,8,32,128]{4,3,2,1,0:T(8,128)}, f32[3,2,8,32,128]{4,3,2,1,0:T(8,128)}, f32[2,2,8,32,128]{4,3,2,1,0:T(8,128)}, f32[5,704,128]{2,1,0:T(8,1...) custom-call(f32[344,128]{1,0:T(8,128)S(1)} %collective-permute-done., ...), custom_call_target="tpu_custom_call", output_to_operand_aliasing={{3}: (3, {}), {4}: (4, {}), {5}: (5, {}), {6}: (6, {}), {7}... | custom-call | tf_op jit(solution)/shard_map/pallas_call | solution.py:617
Async XLA Ops:
  2.2 16.7 %collective-permute-start = (f32[568,128]{1,0:T(8,128)S(1)}, f32[568,128]{1,0:T(8,128)S(1)}, u32[]{:S(2)}, u32[]{:S(2)}) collective-permute-start(f32[568,128]{1,0:T(8,128)S(1)} %get-tuple-element.34), channel_id=1, source_target_pairs={{0,127},{1,2},{2,1},{3,4},{4,3},{5,6},{6,5},{7,8},{8,7},{9,10},{10... | collective-permute-start | bytes 872456 | tf_op jit(solution)/shard_map/ppermute | solution.py:597
  12.6 10.7 %collective-permute-start.3 = (f32[544,128]{1,0:T(8,128)S(1)}, f32[544,128]{1,0:T(8,128)S(1)}, u32[]{:S(2)}, u32[]{:S(2)}) collective-permute-start(f32[544,128]{1,0:T(8,128)S(1)} %get-tuple-element.45), channel_id=1, source_target_pairs={{0,1},{1,0},{2,3},{3,2},{4,5},{5,4},{6,7},{7,6},{8,9},{9,8},{10,11... | collective-permute-start | bytes 835592 | tf_op jit(solution)/shard_map/ppermute | solution.py:597
  12.7 6.2 %collective-permute-start.1 = (f32[24,128]{1,0:T(8,128)S(1)}, f32[24,128]{1,0:T(8,128)S(1)}, u32[]{:S(2)}, u32[]{:S(2)}) collective-permute-start(f32[24,128]{1,0:T(8,128)S(1)} %get-tuple-element.35), channel_id=1, source_target_pairs={{0,64},{1,126},{2,125},{3,124},{4,123},{5,122},{6,121},{7,120},{8,... | collective-permute-start | bytes 36872 | tf_op jit(solution)/shard_map/ppermute | solution.py:597
  19.7 11.9 %collective-permute-start.2 = (f32[344,128]{1,0:T(8,128)S(1)}, f32[344,128]{1,0:T(8,128)S(1)}, u32[]{:S(2)}, u32[]{:S(2)}) collective-permute-start(f32[344,128]{1,0:T(8,128)S(1)} %get-tuple-element.44), channel_id=1, source_target_pairs={{0,127},{1,2},{2,1},{3,4},{4,3},{5,6},{6,5},{7,8},{8,7},{9,10},{10... | collective-permute-start | bytes 528392 | tf_op jit(solution)/shard_map/ppermute | solution.py:597
  24.0 7.6 %collective-permute-start.4 = (f32[344,128]{1,0:T(8,128)S(1)}, f32[344,128]{1,0:T(8,128)S(1)}, u32[]{:S(2)}, u32[]{:S(2)}) collective-permute-start(f32[344,128]{1,0:T(8,128)S(1)} %get-tuple-element.51), channel_id=1, source_target_pairs={{0,1},{1,0},{2,3},{3,2},{4,5},{5,4},{6,7},{7,6},{8,9},{9,8},{10,11... | collective-permute-start | bytes 528392 | tf_op jit(solution)/shard_map/ppermute | solution.py:597

commit v6 on v5

--- a/solution.py
+++ b/solution.py
@@ -102,7 +102,7 @@
     return jnp.where(ice, new, open_o)
 
 
-def subcycle(st, sc, tmp, f4, masks, vel, stress, mom):
+def subcycle(st, sc, tmp, f4, masks, vel, stress, mom, also=None):
     def shift(c):
         u, v = st[U, rows(c), :], st[V, rows(c), :]
         up, um = above(u, masks), below(u, masks)
@@ -133,7 +133,11 @@
         st[S2, rows(c), :] = K29 * st[S2, rows(c), :] + a2
         st[S12, rows(c), :] = K29 * st[S12, rows(c), :] + a12
 
+    if also:
+        also()
     each_column(stress, strain)
+    if also:
+        also()
 
     def move(c):
         ss = lambda k, d=0: st[k, rows(c + d), :]
@@ -160,7 +164,7 @@
     subcycle(st, sc, tmp2, f4, masks, (2, 14, 6), (3, 13, 5), (4, 12, 4))
 
 
-def edges(st, sc, tmp1, tmp2, f4, left=None, right=None):
+def edges(st, sc, tmp1, tmp2, f4, left=None, right=None, also=None):
     masks = make_masks()
 
     def near(a, b, c, d):
@@ -174,7 +178,7 @@
         st[S1, rows(17), :] = right["z"]
         st[S2, rows(17), :] = jnp.zeros((R, 128), F32)
     subcycle(
-        st, sc, tmp1, f4, masks, near(-2, 0, 16, 18), near(-1, 1, 15, 17), near(-1, 2, 14, 17)
+        st, sc, tmp1, f4, masks, near(-2, 0, 16, 18), near(-1, 1, 15, 17), near(-1, 2, 14, 17), also
     )
     if left:
         n11 = 0.5 * (st[S1, rows(-1), :] + st[S2, rows(-1), :])
@@ -182,7 +186,7 @@
     if right:
         st[V, rows(17), :] = right["alpha"] - right["beta"] * st[S12, rows(16), :]
     subcycle(
-        st, sc, tmp2, f4, masks, near(-2, 2, 14, 18), near(-1, 3, 13, 17), near(0, 4, 12, 16)
+        st, sc, tmp2, f4, masks, near(-2, 2, 14, 18), near(-1, 3, 13, 17), near(0, 4, 12, 16), also
     )
 
 
@@ -315,21 +319,27 @@
     return lax.rem(lax.axis_index("gy"), 2)
 
 
+def turned(x, by):
+    return pltpu.roll(x, by % 128, 1) if by % 128 else x
+
+
 def squeeze(tiles):
     _, lane = iotas((8, 128))
     out = []
     for t in range(0, len(tiles), 8):
-        x = tiles[t + 7]
-        for g in range(7):
-            x = jnp.where(lane // 16 == g, pltpu.roll(tiles[t + g], 16 * (g + 1), 1), x)
+        for g in range(8):
+            tile, first = tiles[t + g]
+            y = turned(tile, 16 * g - first)
+            x = y if g == 0 else jnp.where(lane // 16 >= g, y, x)
         out.append(x)
     return out
 
 
-def spread(packed, n):
-    x = packed[n // 8]
-    g = n % 8
-    return x if g == 7 else pltpu.roll(x, 128 - 16 * (g + 1), 1)
+def spread(packed, n, first):
+    return turned(packed[n // 8], first - 16 * (n % 8))
+
+
+OWN, OTHER = 112, 48
 
 
 def top_tile(stage, mstage, k, ih):
@@ -399,7 +409,7 @@
             for k in range(TOP)
             for ih in range(2)
         ]
-        for n, x in enumerate(squeeze(tiles)):
+        for n, x in enumerate(squeeze([(x, OWN) for x in tiles])):
             m_out[pl.ds(8 * n, 8), :] = x
             b_out[pl.ds(len(FIRST) * R + 8 * n, 8), :] = x
 
@@ -429,7 +439,8 @@
         edges(st, sc, tmp1, tmp2, f4[...], **{("left", "right")[side]: next_names(got)})
         put(out, [st[k, rows(C - 1 if side else 0), :] for k in range(5)])
         put(out, outgoing(st, sc, f4[...], side), 5)
-        tiles = squeeze([strip[k, pl.ds(16 if side else 8, 8), :] for k in range(2 * TOP)])
+        at = pl.ds(16 if side else 8, 8)
+        tiles = squeeze([(strip[k, at, :], first) for first in (OWN, OTHER) for k in range(TOP)])
         for n, x in enumerate(tiles):
             out[pl.ds(len(SECOND) * R + 8 * n, 8), :] = x
 
@@ -439,7 +450,9 @@
 def cross_edges(*refs):
     rb, rm, f4 = refs[:3]
     st, sc, tmp1, tmp2, strip, out = refs[8:]
-    flip = 7 - iotas((8, 128))[0]
+    row, lane = iotas((8, 128))
+    flip = 7 - row
+    own = lane >= 64
     slab = lax.axis_index("gx") * lax.axis_size("gy") + lax.axis_index("gy")
     paired = (slab == 0) | (slab == N - 1) | (slab == N // 2 - 1) | (slab == N // 2)
     packed = [
@@ -448,8 +461,9 @@
     ]
     for k in range(TOP):
         for ih in range(2):
-            x = spread(packed, 2 * k + ih)
-            strip[TOP + k, pl.ds(16 - 8 * ih, 8), :] = jnp.take_along_axis(x, flip, axis=0)
+            x = jnp.take_along_axis(spread(packed, 2 * k + ih, OTHER), flip, axis=0)
+            at = pl.ds(16 - 8 * ih, 8)
+            strip[k, at, :] = jnp.where(own, strip[k, at, :], x)
     edge_side(rb, out, st, sc, tmp1, tmp2, strip, f4, True)
 
 
@@ -470,117 +484,120 @@
                 out[f, c // 8, pl.ds(8 * k + c % 8, 8, stride=40), :] = y[8 * k : 8 * k + 8]
 
 
+def rows_out(out, dsts, sems, copies, ih, s, il):
+    f = 0
+    for dst in dsts:
+        n = dst.shape[0]
+        src = out.reshape(7, 2, 8, 5, 8, 128).at[pl.ds(f, n), ih, s, pl.ds(0, 4), il, :]
+        to = dst.reshape(n, 2, 8, 4, 8, 128).at[:, ih, s, :, il, :]
+        copies.append(pltpu.make_async_copy(src, to, sems.at[len(copies)]))
+        copies[-1].start()
+        f += n
+
+
+FREE, TIED = pl.ds(0, 7), pl.ds(7, 1)
+
+
 def second_interior(*refs):
-    f4, (st, sc, tmp1, tmp2, out) = refs[0], refs[5:]
+    f4, (st, sc, tmp1, tmp2, out, vel_o, str_o, oce_o, sems) = refs[0], refs[5:]
     interior(st, sc, tmp1, tmp2, f4[...])
-    stage_out(st, sc, out, range(4, 12))
+    copies = []
+    for ih in range(2):
+        stage_out(st, sc, out, range(8, 12) if ih else range(4, 8))
+        il = pl.ds(0 if ih else 4, 4)
+        rows_out(out, (vel_o, str_o, oce_o), sems, copies, ih, FREE, il)
+    for c in copies:
+        c.wait()
 
 
 def run_strips(strip, work, cor4):
     _, lane = iotas((R, 128))
-    last = lane == 127
+    last = lane % 64 == 63
+    own = lane >= 64
     f4 = jnp.broadcast_to(cor4[pl.ds(31, 1), :], (R, 128))
-    for side in range(2):
-        raw = {name: strip[side * TOP + k] for k, name in enumerate(FIELDS)}
-        out, ice = statics(raw)
-        work[5 * side + U] = raw["u"]
-        work[5 * side + V] = raw["v"]
-        for k, name in ((S1, "s1"), (S2, "s2"), (S12, "s12")):
-            work[5 * side + k] = jnp.where(ice, raw[name], 0.0)
-        for k in range(9):
-            work[10 + 9 * side + k] = out[k]
+    f4 = jnp.where(own, f4, pltpu.roll(f4, 64, 1))
+    raw = {name: strip[k] for k, name in enumerate(FIELDS)}
+    out, ice = statics(raw)
+    work[U] = raw["u"]
+    work[V] = raw["v"]
+    for k, name in ((S1, "s1"), (S2, "s2"), (S12, "s12")):
+        work[k] = jnp.where(ice, raw[name], 0.0)
+    for k in range(9):
+        work[5 + k] = out[k]
+    ice = out[MK] == 2.0
+
+    def west_east(y):
+        plus, minus = pltpu.roll(y, R - 1, 0), pltpu.roll(y, 1, 0)
+        return jnp.where(own, minus, plus), jnp.where(own, plus, minus)
+
+    def down(y):
+        return pltpu.roll(y, 1, 1)
+
+    def up(y, sign):
+        return jnp.where(last, sign * pltpu.roll(y, 64, 1), pltpu.roll(y, 127, 1))
 
     def step():
-        x = [[work[5 * side + k] for k in range(5)] for side in range(2)]
-        east = [lambda y: pltpu.roll(y, R - 1, 0), lambda y: pltpu.roll(y, 1, 0)]
-        west = [east[1], east[0]]
-        down = lambda y: pltpu.roll(y, 1, 1)
-        up = lambda y, other, sign: jnp.where(last, sign * other, pltpu.roll(y, 127, 1))
-        terms = []
-        for side in range(2):
-            e, w = east[side], west[side]
-            u, v = x[side][U], x[side][V]
-            ou, ov = x[1 - side][U], x[1 - side][V]
-            upu, um, vp, vm = up(u, ou, -1.0), down(u), up(v, ov, -1.0), down(v)
-            tt, d2, ww, dv2 = u + upu, upu - um, v + vm, vp - vm
-            terms.append((tt, ww))
-            k = lambda n: work[10 + 9 * side + n]
-            a1, a2, a12 = stress_terms(
-                u - w(u),
-                v - vm,
-                (d2 + w(d2)) + (e(ww) - w(ww)),
-                e(tt) - w(tt),
-                dv2 + e(dv2),
-                (upu - u) + (e(v) - v),
-                k(PR),
-            )
-            x[side][S1] = K29 * x[side][S1] + a1
-            x[side][S2] = K29 * x[side][S2] + a2
-            x[side][S12] = K29 * x[side][S12] + a12
-        new = []
-        for side in range(2):
-            e, w = east[side], west[side]
-            u, v, s1, s2, s12 = x[side]
-            q1, q2 = s1 + s2, s1 - s2
-            other = x[1 - side][S1] - x[1 - side][S2]
-            fu = 0.5 * (e(q1) - q1) + (s12 - down(s12))
-            fv = 0.5 * (up(q2, other, 1.0) - q2) + (s12 - w(s12))
-            tt, ww = terms[side]
-            k = lambda n: work[10 + 9 * side + n]
-            ice = k(MK) == 2.0
-            nu = momentum(u, k(UO), k(CU), k(MI), fu, f4 * (ww + e(ww)), ice, k(OU))
-            nv = momentum(v, k(VO), k(CV), k(MI), fv, -f4 * (tt + w(tt)), ice, k(OV))
-            new.append((nu, nv, s1, s2, s12))
-        for side in range(2):
-            for k in range(5):
-                work[5 * side + k] = new[side][k]
+        u, v, s1, s2, s12 = [work[k] for k in range(5)]
+        k = lambda n: work[5 + n]
+        upu, um, vp, vm = up(u, -1.0), down(u), up(v, -1.0), down(v)
+        tt, d2, ww, dv2 = u + upu, upu - um, v + vm, vp - vm
+        w_ww, e_ww = west_east(ww)
+        w_tt, e_tt = west_east(tt)
+        a1, a2, a12 = stress_terms(
+            u - west_east(u)[0],
+            v - vm,
+            (d2 + west_east(d2)[0]) + (e_ww - w_ww),
+            e_tt - w_tt,
+            dv2 + west_east(dv2)[1],
+            (upu - u) + (west_east(v)[1] - v),
+            k(PR),
+        )
+        s1, s2, s12 = K29 * s1 + a1, K29 * s2 + a2, K29 * s12 + a12
+        q1, q2 = s1 + s2, s1 - s2
+        fu = 0.5 * (west_east(q1)[1] - q1) + (s12 - down(s12))
+        fv = 0.5 * (up(q2, 1.0) - q2) + (s12 - west_east(s12)[0])
+        work[U] = momentum(u, k(UO), k(CU), k(MI), fu, f4 * (ww + e_ww), ice, k(OU))
+        work[V] = momentum(v, k(VO), k(CV), k(MI), fv, -f4 * (tt + w_tt), ice, k(OV))
+        work[S1], work[S2], work[S12] = s1, s2, s12
 
     return step
 
 
 def second_edges(*refs):
     rb, ra, f4 = refs[:3]
-    vel_o, str_o, oce_o, st, sc, tmp1, tmp2, strip, out, work, sems = refs[9:]
+    vel_o, str_o, oce_o, st, sc, tmp1, tmp2, strip, out, work, sems = refs[12:]
     even = parity() == 0
     left, right = receive(rb, ra, SECOND, even)
     for k, name in enumerate(STATE):
         st[k, rows(-1), :], st[k, rows(C), :] = left[name], right[name]
-    edges(st, sc, tmp1, tmp2, f4[...], next_names(left), next_names(right))
-    whole = out.reshape(7, 2, 8, 40, 128)
-    copies = []
-
-    def start(ih, at):
-        for dst, f in ((vel_o, 0), (str_o, 2), (oce_o, 5)):
-            src = whole.at[pl.ds(f, dst.shape[0]), ih, at, pl.ds(0, 32), :]
-            sem = sems.at[len(copies)]
-            copies.append(pltpu.make_async_copy(src, dst.at[:, ih, at], sem))
-            copies[-1].start()
-
-    for ih, cols in enumerate((range(4), range(12, 16))):
-        stage_out(st, sc, out, cols)
-        start(ih, pl.ds(0, 7))
     base = len(SECOND) * R
     pb = [rb[pl.ds(base + 8 * n, 8), :] for n in range(3)]
     pa = [ra[pl.ds(base + 8 * n, 8), :] for n in range(3)]
     low = [jnp.where(even, b, a) for b, a in zip(pb, pa)]
     high = [jnp.where(even, a, b) for b, a in zip(pb, pa)]
-    for k in range(2 * TOP):
-        strip[k, pl.ds(0, 8), :] = spread(low, k)
-        strip[k, pl.ds(24, 8), :] = spread(high, k)
+    own = iotas((8, 128))[1] >= 64
+    for k in range(TOP):
+        for at, x in ((0, low), (24, high)):
+            strip[k, pl.ds(at, 8), :] = jnp.where(
+                own, spread(x, k, OWN), spread(x, TOP + k, OTHER)
+            )
     step = run_strips(strip, work, f4)
-    for _ in range(4):
-        step()
+    edges(st, sc, tmp1, tmp2, f4[...], next_names(left), next_names(right), step)
+    copies = []
+    outs = (vel_o, str_o, oce_o)
     top = iotas((8, 128))[1] >= 120
+    tile = pl.ds(7 * 40 + 24, 8)
     for ih in range(2):
+        stage_out(st, sc, out, range(12, 16) if ih else range(4))
+        rows_out(out, outs, sems, copies, ih, FREE, pl.ds(4 if ih else 0, 4))
         mine = pl.ds(8 + 8 * ih, 8)
         x = [work[k, mine, :] for k in range(5)]
         for w, o in ((U, UO), (V, VO)):
-            d = x[w] - work[10 + o, mine, :]
+            d = x[w] - work[5 + o, mine, :]
             x.append(0.5 * root(d * d + 0.0025) * d)
-        tile = pl.ds(7 * 40 + 24, 8)
         for f, y in enumerate(x):
             out[f, ih, tile, :] = jnp.where(top, y, out[f, ih, tile, :])
-        start(ih, pl.ds(7, 1))
+        rows_out(out, outs, sems, copies, ih, TIED, pl.ds(0, 8))
     for c in copies:
         c.wait()
 
@@ -669,7 +686,7 @@
     )
     ra = permuted(a, CHIP)
     main = [shape(5, NC * R, 128), shape(9, NC * R, 128), *[shape(6, NC * R, 128)] * 2]
-    strips = shape(2 * TOP, R, 128)
+    strips = shape(TOP, R, 128)
     *state, strip = call(
         first_interior, [*main, strips], [stage, mstage, f4], [VM] * 3, [], cost=cost
     )
@@ -692,22 +709,24 @@
         cost=cost,
     )
     ra = permuted(a, CHIP)
-    *state, out = call(
+    results = [shape(n, 2, 8, 32, 128) for n in (2, 3, 2)]
+    *state, out, vel, strs, ocean = call(
         second_interior,
-        [*main, shape(7, *STAGE)],
+        [*main, shape(7, *STAGE), *results],
         [f4, *state],
         [VM] * 5,
-        [],
+        [pltpu.SemaphoreType.DMA((6,))],
         alias={1 + k: k for k in range(4)},
+        outs=[VM] * 5 + [HBM] * 3,
         cost=cost,
     )
     vel, strs, ocean, *_ = call(
         second_edges,
-        [*[shape(n, 2, 8, 32, 128) for n in (2, 3, 2)], *main, strips, shape(7, *STAGE)],
-        [rb, ra, f4, *state, strip, out],
-        [VM] * 9,
-        [pltpu.VMEM((28, R, 128), F32), pltpu.SemaphoreType.DMA((12,))],
-        alias={3 + k: 3 + k for k in range(6)},
+        [*results, *main, strips, shape(7, *STAGE)],
+        [rb, ra, f4, vel, strs, ocean, *state, strip, out],
+        [VM] * 3 + [HBM] * 3 + [VM] * 6,
+        [pltpu.VMEM((14, R, 128), F32), pltpu.SemaphoreType.DMA((12,))],
+        alias={3 + k: k for k in range(9)},
         outs=[HBM] * 3 + [VM] * 6,
     )
     return vel, strs, ocean

time: 34.6 us -> 34.3 us (level)
  waiting for transfers between devices: 8.07 us -> 7.28 us
  Pallas kernels: 13.5 us -> 14 us
    ppermute x5, waiting for transfers between devices: 8.07 us -> 7.28 us  [permuted(): return lax.ppermute(x, AXES, pairs)]
    pallas_call x7, Pallas kernels: 13.5 us -> 14 us  [call(): pl.pallas_call(kernel, out_shape=out, in_specs=specs, out_specs=outs or [...]
  transfers between devices with their start and end apart: 5 -> 5, of which waited for: 2 -> 2; matrix products, arithmetic and copies ran while one was open for 0% -> 0% of each run, Pallas kernels for 26% -> 29%
where the time goes in v6:
time: 34.3 us; the launch traced here: 34.2 us
  Pallas kernels  14 us (41%)
  starting transfers between devices  12.2 us (36%)
  waiting for transfers between devices  7.28 us (21%)
  between operations  0.7 us (2%)
    pallas_call x7, Pallas kernels, call(): pl.pallas_call(kernel, out_shape=out, in_specs=specs, out_specs=outs or [...  14 us
    ppermute x5, starting transfers between devices, permuted(): return lax.ppermute(x, AXES, pairs)  12.2 us
    ppermute x5, waiting for transfers between devices, permuted(): return lax.ppermute(x, AXES, pairs)  7.28 us
  transfers between devices with their start and end apart: 5, of which 2 were waited for; matrix products, arithmetic and copies ran while one was open for 0% of the time, Pallas kernels for 29%

profile of v6, /device:TPU:0, one launch (start us, length us, event | category | flops | bytes accessed | tf_op | source)
XLA Modules:
  0.0 34.2 jit_solution(15521169545380212129)
XLA Ops:
  0.6 1.6 %shard_map.85 = (f32[568,128]{1,0:T(8,128)S(1)}, f32[24,128]{1,0:T(8,128)S(1)}, f32[32,128]{1,0:T(8,128)S(1)}) custom-call(f32[4,2,8,32,128]{4,3,2,1,0:T(8,128)} %bitcast.40, f32[2,2,8,32,128]{4,3,2,1,0:T(8,128)} %bitcast.44, f32[2,2,8,32,128]{4,3,2,1,0:T(8,128)} %bitcast.46, f32[3,2,8,32,128]{4,3,2,1,0:T(8,128)} %bitcast.42, ...), custom_call_target="tpu_custom_call" | custom-call | tf_op jit(solution)/shard_map/pallas_call | solution.py:634
  2.2 8.3 %collective-permute-start = (f32[568,128]{1,0:T(8,128)S(1)}, f32[568,128]{1,0:T(8,128)S(1)}, u32[]{:S(2)}, u32[]{:S(2)}) collective-permute-start(f32[568,128]{1,0:T(8,128)S(1)} %get-tuple-element.37), channel_id=1, source_target_pairs={{0,127},{1,2},{2,1},{3,4},{4,3},{5,6},{6,5},{7,8},{8,7},{9,10},{10... | collective-permute-start | bytes 872456 | tf_op jit(solution)/shard_map/ppermute | solution.py:614
  10.5 2.1 %shard_map.86 = (f32[544,128]{1,0:T(8,128)S(1)}, f32[11,2,320,128]{3,2,1,0:T(8,128)S(1)}, s32[1,2,320,128]{3,2,1,0:T(8,128)S(1)}) custom-call(f32[4,2,8,32,128]{4,3,2,1,0:T(8,128)} %bitcast.41, f32[2,2,8,32,128]{4,3,2,1,0:T(8,128)} %bitcast.45, f32[2,2,8,32,128]{4,3,2,1,0:T(8,128)} %bitcast.47, f32[3,2,8,32,128]{4,3,2,1,0:T(8,128)} %bitcast.43, ...), custom_call_target="tpu_custom_call" | custom-call | flops 20000000 | bytes 4000000 | tf_op jit(solution)/shard_map/pallas_call | solution.py:634
  12.6 0.1 collective-permute-start.3
  12.7 0.1 collective-permute-start.1
  12.8 3.0 %shard_map.87 = (f32[5,704,128]{2,1,0:T(8,128)S(1)}, f32[9,704,128]{2,1,0:T(8,128)S(1)}, f32[6,704,128]{2,1,0:T(8,128)S(1)}, f32[6,704,128]{2,1,0:T(8,128)S(1)}, f32[12,32,128]{2,1,0:T(8,128)S(1)}) custom-call(f32[11,2,320,128]{3,2,1,0:T(8,128)S(1)} %get-tuple-element.40.stage, s32[1,2,320,128]{3,2,1,0:T(8,128)S(1)} %get-tuple-element.41.mstage, ...), custom_call_target="tpu_custom_call" | custom-call | flops 20000000 | bytes 4000000 | tf_op jit(solution)/shard_map/pallas_call | solution.py:634
  15.8 3.1 %collective-permute-done.1.refs_1_ = f32[24,128]{1,0:T(8,128)S(1)} collective-permute-done((f32[24,128]{1,0:T(8,128)S(1)}, f32[24,128]{1,0:T(8,128)S(1)}, u32[]{:S(2)}, u32[]{:S(2)}) %collective-permute-start.1) | collective-permute-done | bytes 12320 | tf_op jit(solution)/shard_map/ppermute | solution.py:614
  18.9 0.0 collective-permute-done.refs_0_
  18.9 0.8 %shard_map.88 = (f32[5,704,128]{2,1,0:T(8,128)S(1)}, f32[9,704,128]{2,1,0:T(8,128)S(1)}, f32[6,704,128]{2,1,0:T(8,128)S(1)}, f32[6,704,128]{2,1,0:T(8,128)S(1)},...) custom-call(f32[568,128]{1,0:T(8,128)S(1)} %collective-permute-done., ...), custom_call_target="tpu_custom_call", output_to_operand_aliasing={{0}: (3, {}), {1}: (4, {}), {2}: (5, {}), {3}: (6, {}), {4}... | custom-call | tf_op jit(solution)/shard_map/pallas_call | solution.py:634
  19.7 3.6 %collective-permute-start.2 = (f32[344,128]{1,0:T(8,128)S(1)}, f32[344,128]{1,0:T(8,128)S(1)}, u32[]{:S(2)}, u32[]{:S(2)}) collective-permute-start(f32[344,128]{1,0:T(8,128)S(1)} %get-tuple-element.47), channel_id=1, source_target_pairs={{0,127},{1,2},{2,1},{3,4},{4,3},{5,6},{6,5},{7,8},{8,7},{9,10},{10... | collective-permute-start | bytes 528392 | tf_op jit(solution)/shard_map/ppermute | solution.py:614
  23.3 0.0 collective-permute-done.3.refs_0_
  23.3 0.7 %shard_map.89 = (f32[5,704,128]{2,1,0:T(8,128)S(1)}, f32[9,704,128]{2,1,0:T(8,128)S(1)}, f32[6,704,128]{2,1,0:T(8,128)S(1)}, f32[6,704,128]{2,1,0:T(8,128)S(1)},...) custom-call(f32[544,128]{1,0:T(8,128)S(1)} %collective-permute-done., ...), custom_call_target="tpu_custom_call", output_to_operand_aliasing={{0}: (2, {}), {1}: (3, {}), {2}: (4, {}), {3}: (5, {}), {4}... | custom-call | flops 20000000 | bytes 4000000 | tf_op jit(solution)/shard_map/pallas_call | solution.py:634
  24.0 0.1 collective-permute-start.4
  24.2 3.3 %shard_map.90 = (f32[5,704,128]{2,1,0:T(8,128)S(1)}, f32[9,704,128]{2,1,0:T(8,128)S(1)}, f32[6,704,128]{2,1,0:T(8,128)S(1)}, f32[6,704,128]{2,1,0:T(8,128)S(1)},...) custom-call(f32[32,128]{1,0:T(8,128)S(1)} %get-tuple-element.39.f4.r, ...), custom_call_target="tpu_custom_call", output_to_operand_aliasing={{0}: (1, {}), {1}: (2, {}), {2}: (3, {}), {3}: (4, {})} | custom-call | flops 20000000 | bytes 4000000 | tf_op jit(solution)/shard_map/pallas_call | solution.py:634
  27.5 4.2 %collective-permute-done.2.refs_0_ = f32[344,128]{1,0:T(8,128)S(1)} collective-permute-done((f32[344,128]{1,0:T(8,128)S(1)}, f32[344,128]{1,0:T(8,128)S(1)}, u32[]{:S(2)}, u32[]{:S(2)}) %collective-permute-start.2) | collective-permute-done | bytes 176160 | tf_op jit(solution)/shard_map/ppermute | solution.py:614
  31.7 0.0 collective-permute-done.4.refs_1_
  31.7 2.5 %shard_map.91 = (f32[2,2,8,32,128]{4,3,2,1,0:T(8,128)}, f32[3,2,8,32,128]{4,3,2,1,0:T(8,128)}, f32[2,2,8,32,128]{4,3,2,1,0:T(8,128)}, f32[5,704,128]{2,1,0:T(8,1...) custom-call(f32[344,128]{1,0:T(8,128)S(1)} %collective-permute-done., ...), custom_call_target="tpu_custom_call", output_to_operand_aliasing={{0}: (3, {}), {1}: (4, {}), {2}: (5, {}), {3}: (6, {}), {4}... | custom-call | tf_op jit(solution)/shard_map/pallas_call | solution.py:634
Async XLA Ops:
  2.2 16.7 %collective-permute-start = (f32[568,128]{1,0:T(8,128)S(1)}, f32[568,128]{1,0:T(8,128)S(1)}, u32[]{:S(2)}, u32[]{:S(2)}) collective-permute-start(f32[568,128]{1,0:T(8,128)S(1)} %get-tuple-element.37), channel_id=1, source_target_pairs={{0,127},{1,2},{2,1},{3,4},{4,3},{5,6},{6,5},{7,8},{8,7},{9,10},{10... | collective-permute-start | bytes 872456 | tf_op jit(solution)/shard_map/ppermute | solution.py:614
  12.6 10.7 %collective-permute-start.3 = (f32[544,128]{1,0:T(8,128)S(1)}, f32[544,128]{1,0:T(8,128)S(1)}, u32[]{:S(2)}, u32[]{:S(2)}) collective-permute-start(f32[544,128]{1,0:T(8,128)S(1)} %get-tuple-element.48), channel_id=1, source_target_pairs={{0,1},{1,0},{2,3},{3,2},{4,5},{5,4},{6,7},{7,6},{8,9},{9,8},{10,11... | collective-permute-start | bytes 835592 | tf_op jit(solution)/shard_map/ppermute | solution.py:614
  12.7 6.2 %collective-permute-start.1 = (f32[24,128]{1,0:T(8,128)S(1)}, f32[24,128]{1,0:T(8,128)S(1)}, u32[]{:S(2)}, u32[]{:S(2)}) collective-permute-start(f32[24,128]{1,0:T(8,128)S(1)} %get-tuple-element.38), channel_id=1, source_target_pairs={{0,64},{1,126},{2,125},{3,124},{4,123},{5,122},{6,121},{7,120},{8,... | collective-permute-start | bytes 36872 | tf_op jit(solution)/shard_map/ppermute | solution.py:614
  19.7 11.9 %collective-permute-start.2 = (f32[344,128]{1,0:T(8,128)S(1)}, f32[344,128]{1,0:T(8,128)S(1)}, u32[]{:S(2)}, u32[]{:S(2)}) collective-permute-start(f32[344,128]{1,0:T(8,128)S(1)} %get-tuple-element.47), channel_id=1, source_target_pairs={{0,127},{1,2},{2,1},{3,4},{4,3},{5,6},{6,5},{7,8},{8,7},{9,10},{10... | collective-permute-start | bytes 528392 | tf_op jit(solution)/shard_map/ppermute | solution.py:614
  24.0 7.6 %collective-permute-start.4 = (f32[344,128]{1,0:T(8,128)S(1)}, f32[344,128]{1,0:T(8,128)S(1)}, u32[]{:S(2)}, u32[]{:S(2)}) collective-permute-start(f32[344,128]{1,0:T(8,128)S(1)} %get-tuple-element.54), channel_id=1, source_target_pairs={{0,1},{1,0},{2,3},{3,2},{4,5},{5,4},{6,7},{7,6},{8,9},{9,8},{10,11... | collective-permute-start | bytes 528392 | tf_op jit(solution)/shard_map/ppermute | solution.py:614

commit v7 on v6

--- a/solution.py
+++ b/solution.py
@@ -432,8 +432,10 @@
     interior(st, sc, tmp1, tmp2, f4[...])
 
 
-def edge_side(r, out, st, sc, tmp1, tmp2, strip, f4, cross):
+def edge_side(r, out, st, sc, tmp1, tmp2, strip, f4, cross, first=None):
     def body(side):
+        if first:
+            first()
         got = take(r, FIRST)
         put_column(st, sc, rows(C if side else -1), got)
         edges(st, sc, tmp1, tmp2, f4[...], **{("left", "right")[side]: next_names(got)})
@@ -459,12 +461,15 @@
         jnp.where(paired, rb[pl.ds(len(FIRST) * R + 8 * n, 8), :], rm[pl.ds(8 * n, 8), :])
         for n in range(3)
     ]
-    for k in range(TOP):
-        for ih in range(2):
-            x = jnp.take_along_axis(spread(packed, 2 * k + ih, OTHER), flip, axis=0)
-            at = pl.ds(16 - 8 * ih, 8)
-            strip[k, at, :] = jnp.where(own, strip[k, at, :], x)
-    edge_side(rb, out, st, sc, tmp1, tmp2, strip, f4, True)
+
+    def mirrored():
+        for k in range(TOP):
+            for ih in range(2):
+                x = jnp.take_along_axis(spread(packed, 2 * k + ih, OTHER), flip, axis=0)
+                at = pl.ds(16 - 8 * ih, 8)
+                strip[k, at, :] = jnp.where(own, strip[k, at, :], x)
+
+    edge_side(rb, out, st, sc, tmp1, tmp2, strip, f4, True, mirrored)
 
 
 def chip_edges(*refs):

time: 34.3 us -> 34.2 us (level)
  no operation moved by 1% of the time
where the time goes in v7:
time: 34.2 us; the launch traced here: 34.1 us
  Pallas kernels  13.9 us (41%)
  starting transfers between devices  12.2 us (36%)
  waiting for transfers between devices  7.3 us (21%)
  between operations  0.7 us (2%)
    pallas_call x7, Pallas kernels, call(): pl.pallas_call(kernel, out_shape=out, in_specs=specs, out_specs=outs or [...  13.9 us
    ppermute x5, starting transfers between devices, permuted(): return lax.ppermute(x, AXES, pairs)  12.2 us
    ppermute x5, waiting for transfers between devices, permuted(): return lax.ppermute(x, AXES, pairs)  7.3 us
  transfers between devices with their start and end apart: 5, of which 2 were waited for; matrix products, arithmetic and copies ran while one was open for 0% of the time, Pallas kernels for 29%

profile of v7, /device:TPU:0, one launch (start us, length us, event | category | flops | bytes accessed | tf_op | source)
XLA Modules:
  0.0 34.1 jit_solution(12195274811975361022)
XLA Ops:
  0.6 1.6 %shard_map.85 = (f32[568,128]{1,0:T(8,128)S(1)}, f32[24,128]{1,0:T(8,128)S(1)}, f32[32,128]{1,0:T(8,128)S(1)}) custom-call(f32[4,2,8,32,128]{4,3,2,1,0:T(8,128)} %bitcast.40, f32[2,2,8,32,128]{4,3,2,1,0:T(8,128)} %bitcast.44, f32[2,2,8,32,128]{4,3,2,1,0:T(8,128)} %bitcast.46, f32[3,2,8,32,128]{4,3,2,1,0:T(8,128)} %bitcast.42, ...), custom_call_target="tpu_custom_call" | custom-call | tf_op jit(solution)/shard_map/pallas_call | solution.py:639
  2.2 8.3 %collective-permute-start = (f32[568,128]{1,0:T(8,128)S(1)}, f32[568,128]{1,0:T(8,128)S(1)}, u32[]{:S(2)}, u32[]{:S(2)}) collective-permute-start(f32[568,128]{1,0:T(8,128)S(1)} %get-tuple-element.37), channel_id=1, source_target_pairs={{0,127},{1,2},{2,1},{3,4},{4,3},{5,6},{6,5},{7,8},{8,7},{9,10},{10... | collective-permute-start | bytes 872456 | tf_op jit(solution)/shard_map/ppermute | solution.py:619
  10.5 2.1 %shard_map.86 = (f32[544,128]{1,0:T(8,128)S(1)}, f32[11,2,320,128]{3,2,1,0:T(8,128)S(1)}, s32[1,2,320,128]{3,2,1,0:T(8,128)S(1)}) custom-call(f32[4,2,8,32,128]{4,3,2,1,0:T(8,128)} %bitcast.41, f32[2,2,8,32,128]{4,3,2,1,0:T(8,128)} %bitcast.45, f32[2,2,8,32,128]{4,3,2,1,0:T(8,128)} %bitcast.47, f32[3,2,8,32,128]{4,3,2,1,0:T(8,128)} %bitcast.43, ...), custom_call_target="tpu_custom_call" | custom-call | flops 20000000 | bytes 4000000 | tf_op jit(solution)/shard_map/pallas_call | solution.py:639
  12.6 0.1 collective-permute-start.3
  12.7 0.1 collective-permute-start.1
  12.8 3.0 %shard_map.87 = (f32[5,704,128]{2,1,0:T(8,128)S(1)}, f32[9,704,128]{2,1,0:T(8,128)S(1)}, f32[6,704,128]{2,1,0:T(8,128)S(1)}, f32[6,704,128]{2,1,0:T(8,128)S(1)}, f32[12,32,128]{2,1,0:T(8,128)S(1)}) custom-call(f32[11,2,320,128]{3,2,1,0:T(8,128)S(1)} %get-tuple-element.40.stage, s32[1,2,320,128]{3,2,1,0:T(8,128)S(1)} %get-tuple-element.41.mstage, ...), custom_call_target="tpu_custom_call" | custom-call | flops 20000000 | bytes 4000000 | tf_op jit(solution)/shard_map/pallas_call | solution.py:639
  15.8 3.1 %collective-permute-done.1.refs_1_ = f32[24,128]{1,0:T(8,128)S(1)} collective-permute-done((f32[24,128]{1,0:T(8,128)S(1)}, f32[24,128]{1,0:T(8,128)S(1)}, u32[]{:S(2)}, u32[]{:S(2)}) %collective-permute-start.1) | collective-permute-done | bytes 12320 | tf_op jit(solution)/shard_map/ppermute | solution.py:619
  18.9 0.0 collective-permute-done.refs_0_
  18.9 0.7 %shard_map.88 = (f32[5,704,128]{2,1,0:T(8,128)S(1)}, f32[9,704,128]{2,1,0:T(8,128)S(1)}, f32[6,704,128]{2,1,0:T(8,128)S(1)}, f32[6,704,128]{2,1,0:T(8,128)S(1)},...) custom-call(f32[568,128]{1,0:T(8,128)S(1)} %collective-permute-done., ...), custom_call_target="tpu_custom_call", output_to_operand_aliasing={{0}: (3, {}), {1}: (4, {}), {2}: (5, {}), {3}: (6, {}), {4}... | custom-call | tf_op jit(solution)/shard_map/pallas_call | solution.py:639
  19.6 3.6 %collective-permute-start.2 = (f32[344,128]{1,0:T(8,128)S(1)}, f32[344,128]{1,0:T(8,128)S(1)}, u32[]{:S(2)}, u32[]{:S(2)}) collective-permute-start(f32[344,128]{1,0:T(8,128)S(1)} %get-tuple-element.47), channel_id=1, source_target_pairs={{0,127},{1,2},{2,1},{3,4},{4,3},{5,6},{6,5},{7,8},{8,7},{9,10},{10... | collective-permute-start | bytes 528392 | tf_op jit(solution)/shard_map/ppermute | solution.py:619
  23.2 0.0 collective-permute-done.3.refs_0_
  23.2 0.7 %shard_map.89 = (f32[5,704,128]{2,1,0:T(8,128)S(1)}, f32[9,704,128]{2,1,0:T(8,128)S(1)}, f32[6,704,128]{2,1,0:T(8,128)S(1)}, f32[6,704,128]{2,1,0:T(8,128)S(1)},...) custom-call(f32[544,128]{1,0:T(8,128)S(1)} %collective-permute-done., ...), custom_call_target="tpu_custom_call", output_to_operand_aliasing={{0}: (2, {}), {1}: (3, {}), {2}: (4, {}), {3}: (5, {}), {4}... | custom-call | flops 20000000 | bytes 4000000 | tf_op jit(solution)/shard_map/pallas_call | solution.py:639
  24.0 0.1 collective-permute-start.4
  24.1 3.3 %shard_map.90 = (f32[5,704,128]{2,1,0:T(8,128)S(1)}, f32[9,704,128]{2,1,0:T(8,128)S(1)}, f32[6,704,128]{2,1,0:T(8,128)S(1)}, f32[6,704,128]{2,1,0:T(8,128)S(1)},...) custom-call(f32[32,128]{1,0:T(8,128)S(1)} %get-tuple-element.39.f4.r, ...), custom_call_target="tpu_custom_call", output_to_operand_aliasing={{0}: (1, {}), {1}: (2, {}), {2}: (3, {}), {3}: (4, {})} | custom-call | flops 20000000 | bytes 4000000 | tf_op jit(solution)/shard_map/pallas_call | solution.py:639
  27.3 4.2 %collective-permute-done.2.refs_0_ = f32[344,128]{1,0:T(8,128)S(1)} collective-permute-done((f32[344,128]{1,0:T(8,128)S(1)}, f32[344,128]{1,0:T(8,128)S(1)}, u32[]{:S(2)}, u32[]{:S(2)}) %collective-permute-start.2) | collective-permute-done | bytes 176160 | tf_op jit(solution)/shard_map/ppermute | solution.py:619
  31.6 0.0 collective-permute-done.4.refs_1_
  31.6 2.5 %shard_map.91 = (f32[2,2,8,32,128]{4,3,2,1,0:T(8,128)}, f32[3,2,8,32,128]{4,3,2,1,0:T(8,128)}, f32[2,2,8,32,128]{4,3,2,1,0:T(8,128)}, f32[5,704,128]{2,1,0:T(8,1...) custom-call(f32[344,128]{1,0:T(8,128)S(1)} %collective-permute-done., ...), custom_call_target="tpu_custom_call", output_to_operand_aliasing={{0}: (3, {}), {1}: (4, {}), {2}: (5, {}), {3}: (6, {}), {4}... | custom-call | tf_op jit(solution)/shard_map/pallas_call | solution.py:639
Async XLA Ops:
  2.2 16.7 %collective-permute-start = (f32[568,128]{1,0:T(8,128)S(1)}, f32[568,128]{1,0:T(8,128)S(1)}, u32[]{:S(2)}, u32[]{:S(2)}) collective-permute-start(f32[568,128]{1,0:T(8,128)S(1)} %get-tuple-element.37), channel_id=1, source_target_pairs={{0,127},{1,2},{2,1},{3,4},{4,3},{5,6},{6,5},{7,8},{8,7},{9,10},{10... | collective-permute-start | bytes 872456 | tf_op jit(solution)/shard_map/ppermute | solution.py:619
  12.6 10.6 %collective-permute-start.3 = (f32[544,128]{1,0:T(8,128)S(1)}, f32[544,128]{1,0:T(8,128)S(1)}, u32[]{:S(2)}, u32[]{:S(2)}) collective-permute-start(f32[544,128]{1,0:T(8,128)S(1)} %get-tuple-element.48), channel_id=1, source_target_pairs={{0,1},{1,0},{2,3},{3,2},{4,5},{5,4},{6,7},{7,6},{8,9},{9,8},{10,11... | collective-permute-start | bytes 835592 | tf_op jit(solution)/shard_map/ppermute | solution.py:619
  12.7 6.2 %collective-permute-start.1 = (f32[24,128]{1,0:T(8,128)S(1)}, f32[24,128]{1,0:T(8,128)S(1)}, u32[]{:S(2)}, u32[]{:S(2)}) collective-permute-start(f32[24,128]{1,0:T(8,128)S(1)} %get-tuple-element.38), channel_id=1, source_target_pairs={{0,64},{1,126},{2,125},{3,124},{4,123},{5,122},{6,121},{7,120},{8,... | collective-permute-start | bytes 36872 | tf_op jit(solution)/shard_map/ppermute | solution.py:619
  19.6 11.9 %collective-permute-start.2 = (f32[344,128]{1,0:T(8,128)S(1)}, f32[344,128]{1,0:T(8,128)S(1)}, u32[]{:S(2)}, u32[]{:S(2)}) collective-permute-start(f32[344,128]{1,0:T(8,128)S(1)} %get-tuple-element.47), channel_id=1, source_target_pairs={{0,127},{1,2},{2,1},{3,4},{4,3},{5,6},{6,5},{7,8},{8,7},{9,10},{10... | collective-permute-start | bytes 528392 | tf_op jit(solution)/shard_map/ppermute | solution.py:619
  24.0 7.6 %collective-permute-start.4 = (f32[344,128]{1,0:T(8,128)S(1)}, f32[344,128]{1,0:T(8,128)S(1)}, u32[]{:S(2)}, u32[]{:S(2)}) collective-permute-start(f32[344,128]{1,0:T(8,128)S(1)} %get-tuple-element.54), channel_id=1, source_target_pairs={{0,1},{1,0},{2,3},{3,2},{4,5},{5,4},{6,7},{7,6},{8,9},{9,8},{10,11... | collective-permute-start | bytes 528392 | tf_op jit(solution)/shard_map/ppermute | solution.py:619
